TPU v7x, 8 devices: a whole 2x2x1 slice. The times are simulated.
8 devices in a mesh: tp: 4 (over z, y, x), ep: 2 (over core).
Axes of the slice: x: 2, y: 2, z: 1, core: 2. Of those that a mesh axis runs over, the one named last changes fastest.
Arguments:
- x: bfloat16 [8192, 2048], P(('ep', 'tp'))
- y_grad: bfloat16 [8192, 2048], P(('ep', 'tp'))
- expert_ids: int32 [8192, 2], P(('ep', 'tp'))
- norm_gain: bfloat16 [2048], replicated
- w_router: bfloat16 [2048, 8], replicated
- w_gate: bfloat16 [8, 2048, 5632], P('ep', None, 'tp')
- w_up: bfloat16 [8, 2048, 5632], P('ep', None, 'tp')
- w_down: bfloat16 [8, 5632, 2048], P('ep', 'tp')
Outputs:
- output 1: bfloat16 [8192, 2048], P(('ep', 'tp'))
- output 2: bfloat16 [8192, 2048], P(('ep', 'tp'))
- output 3: bfloat16 [2048], replicated
- output 4: bfloat16 [2048, 8], replicated
- output 5: bfloat16 [8, 2048, 5632], P('ep', None, 'tp')
- output 6: bfloat16 [8, 2048, 5632], P('ep', None, 'tp')
- output 7: bfloat16 [8, 5632, 2048], P('ep', 'tp')
- output 8: float32 [], replicated
- output 9: float32 [], replicated
All inputs are finite; a program needn't handle non-finite values.
Results may differ from a plain program's by a relative error of at most 0.0154491.
Values are sent between devices in bfloat16 or wider.
A program may use at most 1 GiB of HBM per device.

v0:
```python
import functools

import jax
import jax.numpy as jnp
from jax import lax
from jax.experimental import pallas as pl
from jax.experimental.pallas import tpu as pltpu
from jax.sharding import PartitionSpec as P

NORM_EPS = 1e-6
ACT_COEF = 1e-5
BALANCE_COEF = 1e-3
TILE = 256
LANES = 128
GROUP = 4
PARTS = (384, 256, 384)
CHUNKS = len(PARTS)
WINDOWS = (1, 2, 3, 4)
VMEM_LIMIT = 62 * 1024 * 1024


def call(kernel, name, table, operands, in_specs, out_shape, out_specs, scratch, cost, grid=()):
    return pl.pallas_call(
        kernel,
        grid_spec=pltpu.PrefetchScalarGridSpec(
            num_scalar_prefetch=1, grid=grid, in_specs=in_specs, out_specs=out_specs, scratch_shapes=scratch
        ),
        out_shape=out_shape,
        compiler_params=pltpu.CompilerParams(vmem_limit_bytes=VMEM_LIMIT),
        cost_estimate=pl.CostEstimate(flops=cost[0], bytes_accessed=cost[1], transcendentals=0),
        name=name,
    )(table, *operands)


ANY = pl.BlockSpec(memory_space=pl.ANY)
WHOLE = pl.BlockSpec(memory_space=pltpu.VMEM)


def row_block(width):
    return pl.BlockSpec((TILE, width), lambda t: (t, 0))


def dispatch_phase(at, spans, table_ref, pos_ref, prob_ref, tok_hbm, outs):
    tokens, dim = tok_hbm.shape
    blocks = tokens // TILE

    def run(tok, waited, sems):
        def block_copy(index):
            rows = pl.ds(index * TILE if isinstance(index, int) else pl.multiple_of(index * TILE, TILE), TILE)
            return pltpu.make_async_copy(tok_hbm.at[rows, :], tok.at[rows, :], sems.at[index])

        waited[0] = 0
        for index in range(blocks):
            block_copy(index).start()

        def await_tokens(stop_span):
            need = (stop_span * LANES + TILE - 1) // TILE

            @pl.loop(waited[0], need)
            def _(index):
                block_copy(index).wait()

            waited[0] = jnp.maximum(waited[0], need)

        def tile_body(x_ref, gate_ref=None):
            tile = pl.program_id(0)
            group = table_ref[at["group"] + tile]
            width = table_ref[at["width"] + tile]

            def window(half, count, start):
                row_id = lax.broadcasted_iota(jnp.int32, (LANES, LANES), 0) + (tile * TILE + half * LANES)
                into = pl.ds(half * LANES if isinstance(half, int) else pl.multiple_of(half * LANES, LANES), LANES)
                hot, gate = [], jnp.zeros((LANES, LANES), jnp.float32)
                for q in range(count):
                    span = pl.ds(spans[0] + start + q, 1)
                    match = pos_ref[group, span, :] == row_id
                    hot.append(jnp.where(match, 1.0, 0.0).astype(jnp.bfloat16))
                    if gate_ref is not None:
                        gate = gate + jnp.where(match, prob_ref[group, span, :], 0.0)
                rows = tok[pl.ds(pl.multiple_of(start * LANES, LANES), count * LANES), :]
                out = jnp.dot(jnp.concatenate(hot, axis=1), rows, preferred_element_type=jnp.float32)
                x_ref[into, :] = out.astype(x_ref.dtype)
                if gate_ref is not None:
                    gate_ref[into, :] = jnp.broadcast_to(jnp.sum(gate, axis=1, keepdims=True), (LANES, LANES))

            @pl.when(width > WINDOWS[-1])
            def _():
                await_tokens(spans[1])

                @pl.loop(0, 2)
                def _(half):
                    window(half, spans[1], 0)

            for k in WINDOWS:
                @pl.when(width == k)
                def _(k=k):
                    starts = [jnp.minimum(table_ref[at["lo"] + 2 * tile + half], spans[1] - 2 * k) for half in range(2)]
                    await_tokens(jnp.maximum(starts[0], starts[1]) + 2 * k)
                    for half in range(2):
                        window(half, 2 * k, starts[half])

        pltpu.emit_pipeline(
            tile_body, grid=(table_ref[at["count"]],), out_specs=[row_block(out.shape[1]) for out in outs]
        )(*outs)
        await_tokens(spans[1])

    pl.run_scoped(
        run,
        pltpu.VMEM((tokens, dim), jnp.bfloat16),
        pltpu.SMEM((1,), jnp.int32),
        pltpu.SemaphoreType.DMA((blocks,)),
    )


def combine_kernel(at, spans, groups, with_gate, table_ref, pos_ref, rows_hbm, *rest):
    if with_gate:
        gate_hbm, out_ref, gout_ref, rows, gates, waited, sems = rest
    else:
        out_ref, rows, waited, sems = rest
    step = pl.program_id(0)
    steps = pl.num_programs(0)
    row_iota = lax.broadcasted_iota(jnp.int32, (LANES, LANES), 0)
    over = table_ref[at["over"] + step]

    def region(g):
        return table_ref[at["first"] + g], table_ref[at["first"] + g + 1]

    def start_of(g, span):
        return pl.multiple_of(table_ref[at["start"][g] + span], 16)

    def block_copies(index):
        into = pl.ds(pl.multiple_of(index * TILE, TILE), TILE)
        copies = [pltpu.make_async_copy(rows_hbm.at[into, :], rows.at[into, :], sems.at[0, index])]
        if with_gate:
            copies.append(pltpu.make_async_copy(gate_hbm.at[into, :], gates.at[into, :], sems.at[1, index]))
        return copies

    @pl.when(step == 0)
    def _():
        for g in range(groups):
            waited[g] = region(g)[0]
        longest = region(0)[1] - region(0)[0]
        for g in range(1, groups):
            longest = jnp.maximum(longest, region(g)[1] - region(g)[0])

        @pl.loop(0, longest)
        def _(index):
            for g in range(groups):
                begin, stop = region(g)

                @pl.when(begin + index < stop)
                def _(begin=begin):
                    for copy in block_copies(begin + index):
                        copy.start()

    for g in range(groups):
        stop = region(g)[1]
        need = jnp.minimum((start_of(g, (step + 1) * GROUP - 1) + LANES + over * LANES + TILE - 1) // TILE, stop)
        need = jnp.where(step == steps - 1, stop, need)

        @pl.loop(waited[g], need)
        def _(index):
            for copy in block_copies(index):
                copy.wait()

        waited[g] = jnp.maximum(waited[g], need)

    def window(q, second):
        span = step * GROUP + q
        hot, data, gdata = [], [], []
        for g in range(groups):
            begin = place = start_of(g, span)
            if second:
                first, stop = region(g)
                place = pl.multiple_of(jnp.where(first == stop, begin, jnp.minimum(begin + LANES, stop * TILE - LANES)), 16)
                begin = begin + LANES
            row = row_iota + place
            match = pos_ref[g, pl.ds(spans[0] + span, 1), :] == row
            if second:
                match = jnp.logical_and(match, row >= begin)
            hot.append(jnp.where(match, 1.0, 0.0).astype(jnp.bfloat16))
            data.append(rows[pl.ds(place, LANES), :])
            if with_gate:
                gdata.append(gates[pl.ds(place, LANES), :])
        hot = jnp.concatenate(hot, axis=0)
        dims = (((0,), (0,)), ((), ()))
        out = lax.dot_general(hot, jnp.concatenate(data, axis=0), dims, preferred_element_type=jnp.float32)
        if not with_gate:
            return out, None
        exact = jnp.concatenate(gdata, axis=0)
        high = exact.astype(jnp.bfloat16)
        low = (exact - high.astype(jnp.float32)).astype(jnp.bfloat16)
        pair = lax.dot_general(hot, jnp.concatenate([high, low], axis=1), dims, preferred_element_type=jnp.float32)
        return out, pair[:, :LANES] + pair[:, LANES:]

    def put(q, wide):
        out, gate = window(q, False)
        if wide:
            out2, gate2 = window(q, True)
            out = out + out2
            gate = gate + gate2 if with_gate else None
        into = pl.ds(q * LANES if isinstance(q, int) else pl.multiple_of(q * LANES, LANES), LANES)
        out_ref[into, :] = out.astype(out_ref.dtype)
        if with_gate:
            gout_ref[into, :] = gate

    @pl.when(over == 0)
    def _():
        for q in range(GROUP):
            put(q, False)

    @pl.when(over != 0)
    def _():
        @pl.loop(0, GROUP)
        def _(q):
            put(q, True)


def combine(layout, chunk, table, pos, rows, gate_rows=None):
    rows_max, dim = rows.shape
    groups = pos.shape[0]
    spans = layout[chunk]["spans"]
    tokens = spans[1] * LANES
    with_gate = gate_rows is not None
    block = GROUP * LANES
    operands, in_specs = [pos, rows], [WHOLE, ANY]
    out_shape = [jax.ShapeDtypeStruct((tokens, dim), jnp.bfloat16)]
    out_specs = [pl.BlockSpec((block, dim), lambda t, *_: (t, 0))]
    scratch = [pltpu.VMEM((rows_max, dim), jnp.bfloat16)]
    if with_gate:
        operands.append(gate_rows)
        in_specs.append(ANY)
        out_shape.append(jax.ShapeDtypeStruct((tokens, LANES), jnp.float32))
        out_specs.append(pl.BlockSpec((block, LANES), lambda t, *_: (t, 0)))
        scratch.append(pltpu.VMEM((rows_max, LANES), jnp.float32))
    scratch += [pltpu.SMEM((groups,), jnp.int32), pltpu.SemaphoreType.DMA((2, rows_max // TILE))]
    kernel = functools.partial(combine_kernel, layout[chunk], spans, groups, with_gate)
    return call(kernel, "combine", table, operands, in_specs, out_shape, out_specs, scratch, (9 * 10**9, 35 * 10**6), (tokens // block,))


class WeightStream:
    def __init__(self, at, table_ref, weights, scratch):
        self.at, self.table_ref, self.own, self.helped = at, table_ref, weights[:3], weights[3:]
        self.wide, self.down, self.sems = scratch
        self.experts, _, self.ffn = weights[0].shape

    def copies(self, sources, s):
        wg, wu, wd = sources
        return (
            pltpu.make_async_copy(wg, self.wide.at[s, :, pl.ds(0, self.ffn)], self.sems.at[s, 0]),
            pltpu.make_async_copy(wu, self.wide.at[s, :, pl.ds(self.ffn, self.ffn)], self.sems.at[s, 1]),
            pltpu.make_async_copy(wd, self.down.at[s], self.sems.at[s, 2]),
        )

    def start(self, group, s):
        @pl.when(jnp.logical_and(group >= 0, group < self.experts))
        def _():
            for copy in self.copies([w.at[group] for w in self.own], s):
                copy.start()

        @pl.when(group == self.experts)
        def _():
            for copy in self.copies([w.at[0] for w in self.helped], s):
                copy.start()

    def begin(self):
        self.start(self.table_ref[self.at["group"]], 0)

    def slot(self):
        tile = pl.program_id(0)
        s = table_slot = self.table_ref[self.at["slot"] + tile]

        @pl.when(self.table_ref[self.at["fresh"] + tile] != 0)
        def _():
            self.start(self.table_ref[self.at["next"] + tile], 1 - table_slot)
            for copy in self.copies([w.at[0] for w in self.own], table_slot):
                copy.wait()

        return s


def forward_kernel(at, spans, table_ref, pos_ref, prob_ref, tok_hbm, *rest):
    x_hbm, gate_hbm, ab_hbm, h_hbm, out_hbm = rest[6:11]
    stream = WeightStream(at, table_ref, rest[:6], rest[11:])
    wide, down, ffn = stream.wide, stream.down, stream.ffn
    stream.begin()
    dispatch_phase(at, spans, table_ref, pos_ref, prob_ref, tok_hbm, (x_hbm, gate_hbm))

    def tile_body(x_ref, gate_ref, ab_ref, h_ref, out_ref):
        slot = stream.slot()
        x = x_ref[...]
        for j in range(ffn // LANES):
            cols = slice(j * LANES, (j + 1) * LANES)
            ucols = slice(ffn + j * LANES, ffn + (j + 1) * LANES)
            both = jnp.dot(x, jnp.concatenate([wide[slot, :, cols], wide[slot, :, ucols]], axis=1), preferred_element_type=jnp.float32)
            a, b = both[:, :LANES], both[:, LANES:]
            ab_ref[:, cols] = a
            ab_ref[:, ucols] = b
            h_ref[:, cols] = (a * jax.nn.sigmoid(a) * b).astype(h_ref.dtype)
        out = jnp.dot(h_ref[...], down[slot], preferred_element_type=jnp.float32)
        gate = gate_ref[...]
        for j in range(out.shape[1] // LANES):
            cols = slice(j * LANES, (j + 1) * LANES)
            out_ref[:, cols] = (out[:, cols] * gate).astype(out_ref.dtype)

    piped_in, piped_out = (x_hbm, gate_hbm), (ab_hbm, h_hbm, out_hbm)
    pltpu.emit_pipeline(
        tile_body, grid=(table_ref[at["count"]],),
        in_specs=[row_block(ref.shape[1]) for ref in piped_in],
        out_specs=[row_block(ref.shape[1]) for ref in piped_out],
    )(*piped_in, *piped_out)


def backward_kernel(at, spans, table_ref, pos_ref, tok_hbm, ab_hbm, h_hbm, gate_hbm, *rest):
    m_hbm, d_hbm, in_hbm, mg_hbm, dgate_hbm = rest[6:11]
    stream = WeightStream(at, table_ref, rest[:6], rest[11:])
    wide, down, ffn = stream.wide, stream.down, stream.ffn
    trans = (((1,), (1,)), ((), ()))
    stream.begin()
    dispatch_phase(at, spans, table_ref, pos_ref, None, tok_hbm, (m_hbm,))

    def tile_body(m_ref, ab_ref, h_ref, gate_ref, d_ref, in_ref, mg_ref, dgate_ref):
        slot = stream.slot()
        m = m_ref[...]
        gate = gate_ref[...]
        dgate = jnp.zeros(gate.shape, jnp.float32)
        for c in range(0, ffn, 2 * LANES):
            width = min(2 * LANES, ffn - c)
            raw = lax.dot_general(m, down[slot, c:c + width, :], trans, preferred_element_type=jnp.float32)
            for k in range(width // LANES):
                lo = c + k * LANES
                cols = slice(lo, lo + LANES)
                ucols = slice(ffn + lo, ffn + lo + LANES)
                g = raw[:, k * LANES:(k + 1) * LANES]
                a, b = ab_ref[:, cols], ab_ref[:, ucols]
                sig = jax.nn.sigmoid(a)
                hidden_grad = g * gate
                d_ref[:, cols] = (hidden_grad * b * sig * (1.0 + a * (1.0 - sig))).astype(d_ref.dtype)
                d_ref[:, ucols] = (hidden_grad * (a * sig)).astype(d_ref.dtype)
                dgate = dgate + g * h_ref[:, cols].astype(jnp.float32)
        in_ref[...] = lax.dot_general(d_ref[...], wide[slot], trans, preferred_element_type=jnp.float32).astype(in_ref.dtype)
        for j in range(m.shape[1] // LANES):
            cols = slice(j * LANES, (j + 1) * LANES)
            mg_ref[:, cols] = (m[:, cols].astype(jnp.float32) * gate).astype(mg_ref.dtype)
        lane = lax.broadcasted_iota(jnp.int32, gate.shape, 1)
        expert = table_ref[at["expert"] + table_ref[at["group"] + pl.program_id(0)]]
        dgate_ref[...] = jnp.where(lane == expert, jnp.sum(dgate, axis=1, keepdims=True), 0.0)

    piped_in, piped_out = (m_hbm, ab_hbm, h_hbm, gate_hbm), (d_hbm, in_hbm, mg_hbm, dgate_hbm)
    pltpu.emit_pipeline(
        tile_body, grid=(table_ref[at["count"]],),
        in_specs=[row_block(ref.shape[1]) for ref in piped_in],
        out_specs=[row_block(ref.shape[1]) for ref in piped_out],
    )(*piped_in, *piped_out)


def weight_scratch(wg):
    _, dim, ffn = wg.shape
    return [
        pltpu.VMEM((2, dim, 2 * ffn), wg.dtype),
        pltpu.VMEM((2, ffn, dim), wg.dtype),
        pltpu.SemaphoreType.DMA((2, 3)),
    ]


def shapes(rows_max, *kinds):
    return [jax.ShapeDtypeStruct((rows_max, width), dtype) for width, dtype in kinds]


def forward(layout, chunk, table, pos, prob, tok, weights):
    _, dim, ffn = weights[0].shape
    kinds = ((dim, jnp.bfloat16), (LANES, jnp.float32), (2 * ffn, jnp.float32), (ffn, jnp.bfloat16), (dim, jnp.bfloat16))
    at = layout[chunk]
    kernel = functools.partial(forward_kernel, at, at["spans"])
    return call(
        kernel, "forward", table, (pos, prob, tok, *weights), [WHOLE, WHOLE] + [ANY] * 7,
        shapes(at["rows_max"], *kinds), [ANY] * 5, weight_scratch(weights[0]), (75 * 10**9, 150 * 10**6),
    )


def backward(layout, chunk, table, pos, tok, ab, hidden, gates, weights):
    _, dim, ffn = weights[0].shape
    kinds = ((dim, jnp.bfloat16), (2 * ffn, jnp.bfloat16), (dim, jnp.bfloat16), (dim, jnp.bfloat16), (LANES, jnp.float32))
    at = layout[chunk]
    kernel = functools.partial(backward_kernel, at, at["spans"])
    return call(
        kernel, "backward", table, (pos, tok, ab, hidden, gates, *weights), [WHOLE] + [ANY] * 10,
        shapes(at["rows_max"], *kinds), [ANY] * 5, weight_scratch(weights[0]), (75 * 10**9, 150 * 10**6),
    )


def weight_grad_kernel(at, tiles_max, outs, table_ref, *rest):
    lhs_hbm, rhs_hbm = rest[:CHUNKS], rest[CHUNKS:2 * CHUNKS]
    own_out, helped_out = rest[2 * CHUNKS:2 * CHUNKS + outs], rest[2 * CHUNKS + outs:2 * CHUNKS + 2 * outs]
    lhs, rhs, lhs_t, acc, staged, pending, sems, out_sems = rest[2 * CHUNKS + 2 * outs:]
    experts = own_out[0].shape[0]
    steps = table_ref[at["steps"]]

    def copies(chunk, row, s, half):
        source = pl.ds(pl.multiple_of(row, TILE), TILE)
        into = pl.ds(half * TILE, TILE)
        return (
            pltpu.make_async_copy(lhs_hbm[chunk].at[source, :], lhs.at[s, into, :], sems.at[s, half, 0]),
            pltpu.make_async_copy(rhs_hbm[chunk].at[source, :], rhs.at[s, into, :], sems.at[s, half, 1]),
        )

    def start(index, s):
        for half in range(2):
            src = table_ref[at["src"] + 2 * index + half]
            for chunk in range(CHUNKS):
                @pl.when(jnp.logical_and(src >= chunk * tiles_max, src < (chunk + 1) * tiles_max))
                def _(chunk=chunk, src=src, half=half):
                    for copy in copies(chunk, (src - chunk * tiles_max) * TILE, s, half):
                        copy.start()

    def out_copies(targets):
        return [pltpu.make_async_copy(staged.at[i], target, out_sems.at[i]) for i, target in enumerate(targets)]

    def drain():
        @pl.when(pending[0] != 0)
        def _():
            for copy in out_copies([out.at[0] for out in own_out]):
                copy.wait()

        pending[0] = 0

    pending[0] = 0
    start(0, 0)

    def accumulate(slot, fresh, depth):
        lhs_t[:, :depth] = jnp.transpose(lhs[slot, :depth, :], (1, 0))
        block = 2 * LANES
        for c in range(0, acc.shape[1], block):
            part = jnp.dot(lhs_t[:, :depth], rhs[slot, :depth, c:c + block], preferred_element_type=jnp.float32)
            acc[:, c:c + block] = jnp.where(fresh, 0.0, acc[:, c:c + block]) + part

    @pl.loop(0, steps)
    def _(step):
        slot = lax.rem(step, 2)
        group = table_ref[at["owner"] + step]

        @pl.when(step + 1 < steps)
        def _():
            start(step + 1, 1 - slot)

        fresh = jnp.logical_or(step == 0, group != table_ref[at["owner"] + jnp.maximum(step - 1, 0)])
        last = jnp.logical_or(step == steps - 1, group != table_ref[at["owner"] + step + 1])
        pair = table_ref[at["src"] + 2 * step + 1] >= 0
        for copy in copies(0, 0, slot, 0):
            copy.wait()

        @pl.when(pair)
        def _():
            for copy in copies(0, 0, slot, 1):
                copy.wait()
            accumulate(slot, fresh, 2 * TILE)

        @pl.when(jnp.logical_not(pair))
        def _():
            accumulate(slot, fresh, TILE)

        @pl.when(last)
        def _():
            drain()
            width = acc.shape[1] // outs
            for i in range(outs):
                staged[i, :, :] = acc[:, i * width:(i + 1) * width].astype(staged.dtype)

            @pl.when(group < experts)
            def _():
                for copy in out_copies([out.at[group] for out in own_out]):
                    copy.start()

            @pl.when(group == experts)
            def _():
                for copy in out_copies([out.at[0] for out in helped_out]):
                    copy.start()

            pending[0] = 1

    drain()


def weight_grad(layout, table, lhs, rhs, experts, outs):
    left, right = lhs[0].shape[1], rhs[0].shape[1]
    width = right // outs
    kernel = functools.partial(weight_grad_kernel, layout["grad"], layout["tiles_max"], outs)
    scratch = [
        pltpu.VMEM((2, 2 * TILE, left), jnp.bfloat16),
        pltpu.VMEM((2, 2 * TILE, right), jnp.bfloat16),
        pltpu.VMEM((left, 2 * TILE), jnp.bfloat16),
        pltpu.VMEM((left, right), jnp.float32),
        pltpu.VMEM((outs, left, width), jnp.bfloat16),
        pltpu.SMEM((1,), jnp.int32),
        pltpu.SemaphoreType.DMA((2, 2, 2)),
        pltpu.SemaphoreType.DMA((outs,)),
    ]
    out_shape = [jax.ShapeDtypeStruct((n, left, width), jnp.bfloat16) for n in [experts] * outs + [1] * outs]
    return call(
        kernel, "weight_grad", table, (*lhs, *rhs), [ANY] * (2 * CHUNKS), out_shape, [ANY] * len(out_shape),
        scratch, (2 * 9000 * left * right, 100 * 10**6),
    )


def insert_kernel(at, table_ref, *rest):
    back, outs, staged, sems = rest[:3], rest[6:9], rest[9:12], rest[12]
    place = table_ref[at]

    @pl.when(place >= 0)
    def _():
        fetch = [pltpu.make_async_copy(b.at[0], s, sems.at[0, i]) for i, (b, s) in enumerate(zip(back, staged))]
        store = [pltpu.make_async_copy(s, out.at[place], sems.at[1, i]) for i, (s, out) in enumerate(zip(staged, outs))]
        for copy in fetch:
            copy.start()
        for i in range(3):
            fetch[i].wait()
            store[i].start()
        for copy in store:
            copy.wait()


def insert(layout, table, back, grads):
    kernel = functools.partial(insert_kernel, layout["insert"])
    return pl.pallas_call(
        kernel,
        grid_spec=pltpu.PrefetchScalarGridSpec(
            num_scalar_prefetch=1,
            in_specs=[ANY] * 6,
            out_specs=[ANY] * 3,
            scratch_shapes=[pltpu.VMEM(g.shape[1:], g.dtype) for g in grads] + [pltpu.SemaphoreType.DMA((2, 3))],
        ),
        out_shape=[jax.ShapeDtypeStruct(g.shape, g.dtype) for g in grads],
        input_output_aliases={4 + i: i for i in range(3)},
        compiler_params=pltpu.CompilerParams(vmem_limit_bytes=VMEM_LIMIT),
        cost_estimate=pl.CostEstimate(flops=10**9, bytes_accessed=35 * 10**6, transcendentals=0),
        name="insert",
    )(table, *back, *grads)


def below(size, strict):
    i = lax.broadcasted_iota(jnp.int32, (size, size), 0)
    j = lax.broadcasted_iota(jnp.int32, (size, size), 1)
    return (i < j if strict else i <= j).astype(jnp.float32)


def running(values):
    size = values.shape[-1]
    i = lax.broadcasted_iota(jnp.int32, (size, size), 0)
    j = lax.broadcasted_iota(jnp.int32, (size, size), 1)
    return jnp.sum(jnp.where(i <= j, values[..., :, None], 0), axis=-2)


def count(condition, axis):
    return jnp.sum(condition.astype(jnp.int32), axis=axis)


def choose_help(tiles, experts):
    half = [jnp.sum(tiles[:experts]), jnp.sum(tiles[experts:])]
    gap = jnp.abs(half[0] - half[1])
    index = jnp.arange(2 * experts, dtype=jnp.int32)
    on_busier = (index >= experts) == (half[1] > half[0])
    left = jnp.where(on_busier, jnp.abs(gap - 2 * tiles), gap)
    best = jnp.min(left)
    moved = jnp.min(jnp.where(left == best, index, 2 * experts))
    return jnp.where(best < gap, moved, -1)


def routing(hot, experts_of, place):
    groups, span_total, _ = hot.shape
    spans_of = [part * (span_total * LANES // sum(PARTS)) // LANES for part in PARTS]
    firsts = [sum(spans_of[:c]) for c in range(CHUNKS)]
    chunk_of = jnp.concatenate([jnp.full((n,), c, jnp.int32) for c, n in enumerate(spans_of)])
    member = chunk_of[:, None] == jnp.arange(CHUNKS, dtype=jnp.int32)[None, :]
    same = chunk_of[:, None] == chunk_of[None, :]
    tiles_of = [2 * n * LANES // TILE + groups for n in spans_of]
    tiles_max = max(tiles_of)

    within = jnp.einsum("gsi,ij->gsj", hot, below(LANES, False), preferred_element_type=jnp.float32)
    span_count = jnp.sum(hot, axis=-1)
    before = jnp.einsum("gi,ij->gj", span_count, jnp.where(same, below(span_total, True), 0.0), preferred_element_type=jnp.float32)
    total = jnp.sum(jnp.where(member[:, None, :], span_count.T[:, :, None], 0.0), axis=0).T.astype(jnp.int32)
    tiles = (total + TILE - 1) // TILE
    none = jnp.logical_and(jnp.sum(tiles, axis=1, keepdims=True) == 0, jnp.arange(groups, dtype=jnp.int32) == 0)
    tiles = jnp.where(none, 1, tiles)
    stop = running(tiles)
    begin = stop - tiles

    def to_spans(values):
        return jnp.sum(jnp.where(member[None], values.T[:, None, :], 0), axis=2)

    span_first = to_spans(begin) * TILE + before.astype(jnp.int32)
    span_stop = span_first + span_count.astype(jnp.int32)
    pos = jnp.where(hot > 0, span_first[:, :, None] + within.astype(jnp.int32) - 1, -1)

    index = jnp.arange(groups, dtype=jnp.int32)
    tile = jnp.arange(tiles_max, dtype=jnp.int32)
    group = jnp.minimum(count(tile[None, :, None] >= stop[:, None, :], 2), groups - 1)
    mine = group[:, :, None] == index
    ordinal = running((tiles > 0).astype(jnp.int32)) - 1
    later = jnp.logical_and(index[None, None, :] > group[:, :, None], tiles[:, None, :] > 0)
    follow = jnp.min(jnp.where(later, index, groups), axis=2)
    follow = jnp.where(follow == groups, -1, follow)
    fresh = jnp.sum(jnp.where(mine, begin[:, None, :], 0), axis=2) == tile
    slot = jnp.sum(jnp.where(mine, ordinal[:, None, :], 0), axis=2) % 2

    half_mine = jnp.repeat(mine, 2, axis=1)
    stops = jnp.sum(jnp.where(half_mine[..., None], span_stop[None, None], 0), axis=2)
    row0 = jnp.arange(2 * tiles_max, dtype=jnp.int32)[None, :, None] * LANES
    inside = member.T[:, None, :]
    lo = count(jnp.logical_and(inside, stops <= row0), 2)
    hi = jnp.minimum(count(jnp.logical_and(inside, stops < row0 + LANES), 2), jnp.array(spans_of, jnp.int32)[:, None] - 1)
    width = jnp.maximum(jnp.max(((hi - lo + 2) // 2).reshape(CHUNKS, tiles_max, 2), axis=2), 1)
    start = jnp.minimum(span_first // 16 * 16, to_spans(stop) * TILE - LANES)
    empty = to_spans(tiles) == 0
    leading = jnp.logical_and(jnp.logical_not(empty), to_spans(ordinal) == 0)
    start = jnp.where(empty, jnp.sum(jnp.where(leading, start, 0), axis=0), start)
    over = jnp.any(jnp.logical_and(jnp.logical_not(empty), span_stop - start > LANES), axis=0)
    over = jnp.any(over.reshape(-1, GROUP), axis=1)

    in_chunks = running(tiles.T)
    both = in_chunks[:, -1]
    step_stop = running((both + 1) // 2)
    step_first = step_stop - (both + 1) // 2
    steps = CHUNKS * tiles_max // 2 + groups
    step = jnp.arange(steps, dtype=jnp.int32)
    owner = jnp.minimum(count(step[:, None] >= step_stop[None, :], 1), groups - 1)
    step_mine = owner[:, None] == index

    def of_step(values):
        return jnp.sum(jnp.where(step_mine[:, :, None], values[None], 0), axis=1)[:, None, :]

    local = 2 * (step - of_step(step_first[:, None])[:, 0, 0])[:, None, None] + jnp.arange(2, dtype=jnp.int32)[None, :, None]
    ends, sizes = of_step(in_chunks), of_step(tiles.T)
    offset = local - (ends - sizes)
    found = jnp.logical_and(offset >= 0, local < ends)
    chunk_at = jnp.arange(CHUNKS, dtype=jnp.int32) * tiles_max
    src = jnp.sum(jnp.where(found, of_step(begin.T) + offset + chunk_at + 1, 0), axis=2) - 1

    sections = (
        ("expert", experts_of), ("insert", place.reshape(1)), ("steps", step_stop[-1:]), ("owner", owner), ("src", src),
        ("count", stop[:, -1:]), ("group", group), ("slot", slot), ("fresh", fresh), ("next", follow), ("lo", lo), ("width", width),
        ("first", jnp.concatenate([jnp.zeros((CHUNKS, 1), jnp.int32), stop], axis=1)), ("start", start), ("over", over),
    )
    table = jnp.concatenate([values.reshape(-1).astype(jnp.int32) for _, values in sections])
    places, sizes_of, at = {}, {}, 0
    for name, values in sections:
        places[name], sizes_of[name] = at, values.size
        at += values.size
    layout = {}
    for c in range(CHUNKS):
        layout[c] = {name: places[name] + c * (sizes_of[name] // CHUNKS) for name in ("count", "group", "slot", "fresh", "next", "lo", "width", "first")}
        layout[c] |= {
            "expert": places["expert"], "spans": (firsts[c], spans_of[c]), "rows_max": tiles_of[c] * TILE,
            "start": [places["start"] + g * span_total + firsts[c] for g in range(groups)],
            "over": places["over"] + firsts[c] // GROUP,
        }
    layout |= {"grad": {name: places[name] for name in ("steps", "owner", "src")}, "insert": places["insert"], "tiles_max": tiles_max}
    return pos, table, layout


def solution(mesh):
    tp_size = mesh.shape["tp"]
    ep_size = mesh.shape["ep"]
    dev_count = tp_size * ep_size
    rows_axes = ("ep", "tp")
    row_spec = P(rows_axes, None)
    wide_spec = P("ep", None, "tp")
    down_spec = P("ep", "tp", None)
    swap = [(0, 1), (1, 0)]

    def body(x, y_grad, expert_ids, norm_gain, w_router, w_gate, w_up, w_down):
        tokens, model_dim = x.shape
        top_k = expert_ids.shape[1]
        num_experts = w_router.shape[1]
        local_experts = w_gate.shape[0]
        total_tokens = tokens * dev_count
        my_ep = lax.axis_index("ep").astype(jnp.int32)
        firsts = [sum(PARTS[:c]) for c in range(CHUNKS)]

        def of_chunk(rows, c, axis=0):
            return lax.slice_in_dim(rows, firsts[c], firsts[c] + PARTS[c], axis=axis)

        def gather(rows):
            return lax.all_gather(rows, rows_axes, axis=0, tiled=True)

        def scatter(rows):
            return lax.psum_scatter(rows, rows_axes, scatter_dimension=0, tiled=True)

        def after(values, first):
            return lax.optimization_barrier((values, first))

        x_float = x.astype(jnp.float32)
        inv_rms = lax.rsqrt(jnp.mean(x_float * x_float, axis=-1, keepdims=True) + NORM_EPS)
        unit = x_float * inv_rms
        gain = norm_gain.astype(jnp.float32)
        x_norm = (unit * gain).astype(jnp.bfloat16)
        tok = [gather(of_chunk(x_norm, c)) for c in range(CHUNKS)]

        route_prob = jax.nn.softmax(jnp.dot(x_norm, w_router, preferred_element_type=jnp.float32), axis=-1)
        expert_range = jnp.arange(num_experts, dtype=jnp.int32)
        choice = jnp.sum((expert_ids[:, :, None] == expert_range[None, None, :]).astype(jnp.float32), axis=1)
        small = lax.all_gather(jnp.concatenate([choice, route_prob], axis=1).T, rows_axes, axis=0, tiled=False)
        counts = jnp.sum(small[:, :num_experts], axis=(0, 2))
        balance_scale = BALANCE_COEF * num_experts / (total_tokens * total_tokens * top_k)
        balance_loss = balance_scale * jnp.sum(counts * jnp.sum(small[:, num_experts:], axis=(0, 2)))

        rows_in = jnp.stack([jnp.sum(of_chunk(small[:, :num_experts], c, 2), axis=(0, 2)) for c in range(CHUNKS)])
        tiles_in = jnp.sum((rows_in.astype(jnp.int32) + TILE - 1) // TILE, axis=0)
        moved = choose_help(tiles_in, local_experts)
        my_base = my_ep * local_experts
        local = jnp.arange(local_experts, dtype=jnp.int32)
        giving = jnp.logical_and(moved >= my_base, moved < my_base + local_experts)
        helping = jnp.logical_and(moved >= 0, jnp.logical_not(giving))
        given = jnp.where(giving, moved - my_base, 0)
        group_experts = jnp.concatenate([my_base + local, jnp.maximum(moved, 0).reshape(1)])
        active = jnp.concatenate([my_base + local != moved, helping.reshape(1)])
        take = jnp.logical_and(group_experts[:, None] == expert_range, active[:, None])
        spread = jnp.concatenate([of_chunk(small, c, 2).transpose(1, 0, 2).reshape(2 * num_experts, -1) for c in range(CHUNKS)], axis=1)
        spread = spread.reshape(2, 1, num_experts, -1, LANES)
        own = jnp.sum(jnp.where(take[None, :, :, None, None], spread, 0.0), axis=2)
        prob = own[1]
        pos, table, layout = routing(own[0], group_experts, jnp.where(giving, given, -1))
        helped = [lax.ppermute(lax.dynamic_slice_in_dim(w, given, 1, axis=0), "ep", swap) for w in (w_gate, w_up, w_down)]
        weights = (w_gate, w_up, w_down, *helped)

        grad_scale = 2.0 * ACT_COEF / (total_tokens * model_dim)
        x_rows, gate_rows, pre, hidden, d_rows, mg_rows = [], [], [], [], [], []
        out_raw, moe_out, m_own, m_tok, in_raw, gate_part = [], [], [], [], [], []

        def send_cotangent(c, gate):
            raw, (gate, _) = after(out_raw[c], (gate, m_own[-1:]))
            moe_out.append(raw.astype(jnp.float32))
            moe_grad = of_chunk(y_grad, c).astype(jnp.float32) + grad_scale * moe_out[c]
            m_own.append(moe_grad.astype(jnp.bfloat16))
            m_tok.append(gather(m_own[c]))
            return gate

        for c in range(CHUNKS):
            rows, gates, ab, h, out_rows = forward(layout, c, table, pos, prob, tok[c], weights)
            (partial,) = combine(layout, c, table, pos, out_rows)
            if c == 0:
                partial, tok[1:] = after(partial, tok[1:])
            else:
                partial = send_cotangent(c - 1, partial)
            out_raw.append(scatter(partial))
            x_rows.append(rows)
            gate_rows.append(gates)
            pre.append(ab)
            hidden.append(h)
        for c in range(CHUNKS):
            _, d, in_rows, mg, dgate = backward(layout, c, table, pos, m_tok[c], pre[c], hidden[c], gate_rows[c], weights)
            if c == 0:
                in_rows = send_cotangent(CHUNKS - 1, in_rows)
            partial, gate_tok = combine(layout, c, table, pos, in_rows, dgate)
            if c == 0:
                partial, m_tok[-1] = after(partial, m_tok[-1])
            in_raw.append(scatter(partial))
            gate_part.append(gate_tok[:, :num_experts])
            d_rows.append(d)
            mg_rows.append(mg)
        *wide_grads, helped_gate, helped_up = weight_grad(layout, table, x_rows, d_rows, local_experts, 2)
        back = [lax.ppermute(g, "ep", swap) for g in (helped_gate, helped_up)]
        mg_rows[0], _ = after(mg_rows[0], wide_grads[0])
        down_grad, helped_down = weight_grad(layout, table, hidden, mg_rows, local_experts, 1)
        back.append(lax.ppermute(helped_down, "ep", swap))

        moe_all = jnp.concatenate(moe_out, axis=0)
        y = (x_float + moe_all).astype(jnp.bfloat16)
        gate_part[0], _ = after(gate_part[0], (wide_grads[0], in_raw))
        sums = jnp.concatenate([g.reshape(dev_count, -1) for g in gate_part], axis=1)
        gate_weight_grad = lax.psum_scatter(sums, rows_axes, scatter_dimension=0, tiled=False)
        prob_grad = gate_weight_grad.reshape(tokens, num_experts) + balance_scale * counts[None, :]
        logit_grad = (route_prob * (prob_grad - jnp.sum(route_prob * prob_grad, axis=-1, keepdims=True))).astype(jnp.bfloat16)
        x_norm_grad = jnp.concatenate(in_raw, axis=0).astype(jnp.float32)
        x_norm_grad = x_norm_grad + jnp.einsum("se,de->sd", logit_grad, w_router, preferred_element_type=jnp.float32)
        unit_grad = x_norm_grad * gain
        x_grad = y_grad.astype(jnp.float32) + inv_rms * (unit_grad - unit * jnp.mean(unit_grad * unit, axis=-1, keepdims=True))
        gain_sum, router_sum, act_sum = lax.psum(
            (
                jnp.sum(x_norm_grad * unit, axis=0),
                jnp.einsum("sd,se->de", x_norm, logit_grad, preferred_element_type=jnp.float32),
                jnp.sum(moe_all * moe_all),
            ),
            ("tp", "ep"),
        )
        table, _ = after(table, (x_grad, gain_sum))
        act_loss = ACT_COEF * act_sum / (total_tokens * model_dim)
        gate_grad, up_grad, down_grad = insert(layout, table, back, (*wide_grads, down_grad))
        return (y, x_grad.astype(jnp.bfloat16), gain_sum.astype(jnp.bfloat16), router_sum.astype(jnp.bfloat16), gate_grad, up_grad, down_grad, balance_loss, act_loss)

    return jax.shard_map(body, mesh=mesh, in_specs=(row_spec, row_spec, row_spec, P(), P(), wide_spec, wide_spec, down_spec), out_specs=(row_spec, row_spec, P(), P(), wide_spec, wide_spec, down_spec, P(), P()), check_vma=False)
```

profile of v0, /device:TPU:0, one launch (start us, length us, event | category | flops | bytes accessed | tf_op | source)
XLA Modules:
  0.0 1170.7 jit_solution(9626044417615245653)
XLA Ops:
  7.2 3.2 fusion.10
  19.5 3.4 fusion.66
  23.6 18.7 %all-gather = f32[128,1024]{1,0:T(8,128)S(1)} all-gather(f32[16,1024]{1,0:T(8,128)S(1)} %maximum_bitcast_fusion.1), channel_id=2, replica_groups=mesh['tp'=4,'ep'=2] {'ep','tp'}, dimensions={0}, use_global_device_ids=true | all-gather | bytes 589824 | tf_op jit(solution)/shard_map/all_gather | solution.py:702
  49.2 5.6 constant_dynamic-slice_fusion.2
  54.8 5.6 constant_dynamic-slice_fusion.1
  60.9 6.2 constant_dynamic-slice_fusion
  78.0 6.3 collective-permute-done.2.rest_5_
  84.3 4.5 all-gather.8.cloned.1.call-done.tok_hbm
  88.7 100.7 %forward.3 = (bf16[7424,2048]{1,0:T(8,128)(2,1)}, f32[7424,128]{1,0:T(8,128)}, f32[7424,2816]{1,0:T(8,128)}, bf16[7424,1408]{1,0:T(8,128)(2,1)}, bf16[7424,2048]{1,0:T(8,128)(2,1)}) custom-call(s32[1117]{0:T(1024)} %concatenate.33.table_ref, s32[5,64,128]{2,1,0:T(8,128)} %fusion.14.pos_ref, f32[5,64,128]{2,1,0:T(8,128)} %get-tuple-element.166.prob_ref, ...), custom_call_target="tpu_custom_call" | custom-call | flops 74999996416 | bytes 150000000 | tf_op jit(solution)/shard_map/forward/pallas_call | solution.py:23
  189.5 17.4 %combine.6 = bf16[3072,2048]{1,0:T(8,128)(2,1)} custom-call(s32[1117]{0:T(1024)} %concatenate.33.table_ref, s32[5,64,128]{2,1,0:T(8,128)} %fusion.14.pos_ref, bf16[7424,2048]{1,0:T(8,128)(2,1)} %get-tuple-element.65.rows_hbm), custom_call_target="tpu_custom_call" | custom-call | flops 8999999488 | bytes 35000000 | tf_op jit(solution)/shard_map/combine/pallas_call | solution.py:23
  207.7 81.1 %forward.4 = (bf16[5376,2048]{1,0:T(8,128)(2,1)}, f32[5376,128]{1,0:T(8,128)}, f32[5376,2816]{1,0:T(8,128)}, bf16[5376,1408]{1,0:T(8,128)(2,1)}, bf16[5376,2048]{1,0:T(8,128)(2,1)}) custom-call(s32[1117]{0:T(1024)} %concatenate.33.table_ref, s32[5,64,128]{2,1,0:T(8,128)} %fusion.14.pos_ref, f32[5,64,128]{2,1,0:T(8,128)} %get-tuple-element.166.prob_ref, ...), custom_call_target="tpu_custom_call" | custom-call | flops 74999996416 | bytes 150000000 | tf_op jit(solution)/shard_map/forward/pallas_call | solution.py:23
  288.9 13.3 %combine.7 = bf16[2048,2048]{1,0:T(8,128)(2,1)} custom-call(s32[1117]{0:T(1024)} %concatenate.33.table_ref, s32[5,64,128]{2,1,0:T(8,128)} %fusion.14.pos_ref, bf16[5376,2048]{1,0:T(8,128)(2,1)} %get-tuple-element.68.rows_hbm), custom_call_target="tpu_custom_call" | custom-call | flops 8999999488 | bytes 35000000 | tf_op jit(solution)/shard_map/combine/pallas_call | solution.py:23
  302.2 3.5 reduce-scatter.7.cloned.1.call-done
  307.1 3.1 add_convert_fusion.1
  310.3 106.8 %forward.5 = (bf16[7424,2048]{1,0:T(8,128)(2,1)}, f32[7424,128]{1,0:T(8,128)}, f32[7424,2816]{1,0:T(8,128)}, bf16[7424,1408]{1,0:T(8,128)(2,1)}, bf16[7424,2048]{1,0:T(8,128)(2,1)}) custom-call(s32[1117]{0:T(1024)} %concatenate.33.table_ref, s32[5,64,128]{2,1,0:T(8,128)} %fusion.14.pos_ref, f32[5,64,128]{2,1,0:T(8,128)} %get-tuple-element.166.prob_ref, ...), custom_call_target="tpu_custom_call" | custom-call | flops 74999996416 | bytes 150000000 | tf_op jit(solution)/shard_map/forward/pallas_call | solution.py:23
  417.1 17.4 %combine.8 = bf16[3072,2048]{1,0:T(8,128)(2,1)} custom-call(s32[1117]{0:T(1024)} %concatenate.33.table_ref, s32[5,64,128]{2,1,0:T(8,128)} %fusion.14.pos_ref, bf16[7424,2048]{1,0:T(8,128)(2,1)} %get-tuple-element.72.rows_hbm), custom_call_target="tpu_custom_call" | custom-call | flops 8999999488 | bytes 35000000 | tf_op jit(solution)/shard_map/combine/pallas_call | solution.py:23
  438.5 11.3 all-gather.14.cloned.1.call-done.tok_hbm
  449.8 99.6 %backward.3 = (bf16[7424,2048]{1,0:T(8,128)(2,1)}, bf16[7424,2816]{1,0:T(8,128)(2,1)}, bf16[7424,2048]{1,0:T(8,128)(2,1)}, bf16[7424,2048]{1,0:T(8,128)(2,1)}, f32[7424,128]{1,0:T(8,128)}) custom-call(s32[1117]{0:T(1024)} %concatenate.33.table_ref, s32[5,64,128]{2,1,0:T(8,128)} %fusion.14.pos_ref, bf16[3072,2048]{1,0:T(8,128)(2,1)} %all-gather.14.cloned.1.call-done.tok_hbm, ...), custom_call_target="tpu_custom_call" | custom-call | flops 74999996416 | bytes 150000000 | tf_op jit(solution)/shard_map/backward/pallas_call | solution.py:23
  549.4 3.7 add_convert_fusion
  553.1 33.3 %all-gather.18.cloned.1.call-done.tok_hbm = bf16[2048,2048]{1,0:T(8,128)(2,1)} async-done(((bf16[256,2048]{1,0:T(8,128)(2,1)}), bf16[2048,2048]{1,0:T(8,128)(2,1)}) %all-gather.18.cloned.1.call-update) | async-done | bytes 8388624 | tf_op jit(solution)/shard_map/all_gather | solution.py:684
  586.4 80.7 %backward.4 = (bf16[5376,2048]{1,0:T(8,128)(2,1)}, bf16[5376,2816]{1,0:T(8,128)(2,1)}, bf16[5376,2048]{1,0:T(8,128)(2,1)}, bf16[5376,2048]{1,0:T(8,128)(2,1)}, f32[5376,128]{1,0:T(8,128)}) custom-call(s32[1117]{0:T(1024)} %concatenate.33.table_ref, s32[5,64,128]{2,1,0:T(8,128)} %fusion.14.pos_ref, bf16[2048,2048]{1,0:T(8,128)(2,1)} %all-gather.18.cloned.1.call-done.tok_hbm, ...), custom_call_target="tpu_custom_call" | custom-call | flops 74999996416 | bytes 150000000 | tf_op jit(solution)/shard_map/backward/pallas_call | solution.py:23
  667.1 14.4 %combine.10 = (bf16[2048,2048]{1,0:T(8,128)(2,1)}, f32[2048,128]{1,0:T(8,128)}) custom-call(s32[1117]{0:T(1024)} %concatenate.33.table_ref, s32[5,64,128]{2,1,0:T(8,128)} %fusion.14.pos_ref, bf16[5376,2048]{1,0:T(8,128)(2,1)} %get-tuple-element.87.rows_hbm, f32[5376,128]{1,0:T(8,128)} %get-tuple-element.88.rest_0_), custom_call_target="tpu_custom_call" | custom-call | flops 8999999488 | bytes 35000000 | tf_op jit(solution)/shard_map/combine/pallas_call | solution.py:23
  682.1 18.9 %combine.9 = (bf16[3072,2048]{1,0:T(8,128)(2,1)}, f32[3072,128]{1,0:T(8,128)}) custom-call(s32[1117]{0:T(1024)} %concatenate.33.table_ref, s32[5,64,128]{2,1,0:T(8,128)} %fusion.14.pos_ref, bf16[7424,2048]{1,0:T(8,128)(2,1)} %get-tuple-element.80.rows_hbm, f32[7424,128]{1,0:T(8,128)} %get-tuple-element.81.rest_0_), custom_call_target="tpu_custom_call" | custom-call | flops 8999999488 | bytes 35000000 | tf_op jit(solution)/shard_map/combine/pallas_call | solution.py:23
  701.2 105.6 %backward.5 = (bf16[7424,2048]{1,0:T(8,128)(2,1)}, bf16[7424,2816]{1,0:T(8,128)(2,1)}, bf16[7424,2048]{1,0:T(8,128)(2,1)}, bf16[7424,2048]{1,0:T(8,128)(2,1)}, f32[7424,128]{1,0:T(8,128)}) custom-call(s32[1117]{0:T(1024)} %concatenate.33.table_ref, s32[5,64,128]{2,1,0:T(8,128)} %fusion.14.pos_ref, bf16[3072,2048]{1,0:T(8,128)(2,1)} %all-gather.16.cloned.1.call-done.tok_hbm, ...), custom_call_target="tpu_custom_call" | custom-call | flops 74999996416 | bytes 150000000 | tf_op jit(solution)/shard_map/backward/pallas_call | solution.py:23
  806.7 18.9 %combine.11 = (bf16[3072,2048]{1,0:T(8,128)(2,1)}, f32[3072,128]{1,0:T(8,128)}) custom-call(s32[1117]{0:T(1024)} %concatenate.33.table_ref, s32[5,64,128]{2,1,0:T(8,128)} %fusion.14.pos_ref, bf16[7424,2048]{1,0:T(8,128)(2,1)} %get-tuple-element.94.rows_hbm, f32[7424,128]{1,0:T(8,128)} %get-tuple-element.95.rest_0_), custom_call_target="tpu_custom_call" | custom-call | flops 8999999488 | bytes 35000000 | tf_op jit(solution)/shard_map/combine/pallas_call | solution.py:23
  825.7 145.1 %weight_grad.2 = (bf16[4,2048,1408]{2,1,0:T(8,128)(2,1)}, bf16[4,2048,1408]{2,1,0:T(8,128)(2,1)}, bf16[1,2048,1408]{2,1,0:T(8,128)(2,1)}, bf16[1,2048,1408]{2,1,0:T(8,128)(2,1)}) custom-call(s32[1117]{0:T(1024)} %concatenate.33.table_ref, bf16[7424,2048]{1,0:T(8,128)(2,1)} %get-tuple-element.98.rest_0_, bf16[5376,2048]{1,0:T(8,128)(2,1)} %get-tuple-element.99.rest_1_, ...), custom_call_target="tpu_custom_call" | custom-call | flops 103809024000 | bytes 100000000 | tf_op jit(solution)/shard_map/weight_grad/pallas_call | solution.py:23
  970.9 74.7 %weight_grad.3 = (bf16[4,1408,2048]{2,1,0:T(8,128)(2,1)}, bf16[1,1408,2048]{2,1,0:T(8,128)(2,1)}) custom-call(s32[1117]{0:T(1024)} %concatenate.33.table_ref, bf16[7424,1408]{1,0:T(8,128)(2,1)} %get-tuple-element.76.h_hbm.rest_0_, bf16[5376,1408]{1,0:T(8,128)(2,1)} %get-tuple-element.85.h_hbm.rest_1_, bf16[7424,1408]{1,0:T(8,128)(2,1)} %get-tuple-element.92.h_hbm.rest_2_, ...), custom_call_target="tpu_custom_call" | custom-call | flops 51904512000 | bytes 100000000 | tf_op jit(solution)/shard_map/weight_grad/pallas_call | solution.py:23
  1061.1 34.6 %all-reduce.5.cloned.1.call-done = f32[8,8192]{1,0:T(8,128)} async-done(((f32[8,8192]{1,0:T(8,128)}), f32[8,8192]{1,0:T(8,128)}) %all-reduce.5.cloned.1.call-update) | async-done | bytes 262160
  1102.8 12.3 %multiply_reduce_fusion = (f32[]{:T(128)}, bf16[1024,2048]{1,0:T(8,128)(2,1)}, f32[1024]{0:T(1024)S(1)}, f32[2048]{0:T(1024)S(1)}, f32[1024,2048]{1,0:T(8,128)}) fusion(f32[384,2048]{1,0:T(8,128)} %convert_element_type.130, f32[256,2048]{1,0:T(8,128)} %convert_element_type.127, f32[384,2048]{1,0:T(8,128)S(1)} %copy-done.9, bf16[1024,2048]{1,0:T(8,128)(2,1)} %param.9, ...), kind=kOutput, calls=%fused_computation.16 | convolution fusion | flops 75494400 | bytes 29433860 | tf_op jit(solution)/shard_map/se,de->sd/dot_general | solution.py:775
  1115.1 23.6 %all-reduce.2 = (bf16[2048]{0:T(1024)(128)(2,1)}, bf16[2048,8]{0,1:T(8,128)(2,1)}, f32[]{:T(128)}) all-reduce(f32[2048]{0:T(1024)S(1)} %get-tuple-element.161, f32[2048,8]{0,1:T(8,128)S(1)} %fusion.67, f32[]{:T(128)} %get-tuple-element.158), channel_id=1, replica_groups=mesh['tp'=4,'ep'=2] {'tp','ep'}, use_global_device_ids=true, to_apply=%region_52.53 | all-reduce | flops 18433 | bytes 110600 | tf_op jit(solution)/shard_map/psum | solution.py:778
  1138.7 8.7 fusion.8
  1148.1 13.5 %insert.1 = (bf16[4,2048,1408]{2,1,0:T(8,128)(2,1)}, bf16[4,2048,1408]{2,1,0:T(8,128)(2,1)}, bf16[4,1408,2048]{2,1,0:T(8,128)(2,1)}) custom-call(s32[1117]{0:T(1024)} %concatenate.33.table_ref, bf16[1,2048,1408]{2,1,0:T(8,128)(2,1)} %collective-permute-done.3.rest_0_, ...), custom_call_target="tpu_custom_call", output_to_operand_aliasing={{0}: (4, {}), {1}: (5, {}), {2}: (6, {})} | custom-call | flops 1000000000 | bytes 35000000 | tf_op jit(solution)/shard_map/insert/pallas_call | solution.py:524
  (216 shorter events, 52.5 us)
Async XLA Ops:
  7.2 12.3 %copy-start = (bf16[2048,8]{0,1:T(8,128)(2,1)S(1)}, bf16[2048,8]{0,1:T(8,128)(2,1)}, u32[]{:S(2)}) copy-start(bf16[2048,8]{0,1:T(8,128)(2,1)} %param.13) | copy-start | bytes 98308
  7.2 81.5 %all-gather.8.cloned.1.call-start = ((), (), s32[]{:S(2)}) async-start(), calls=%async_computation.6 | async-start | bytes 14155776 | tf_op jit(solution)/shard_map/all_gather | solution.py:684
  16.3 190.6 %all-gather.10.cloned.1.call-start = ((), (), s32[]{:S(2)}) async-start(), calls=%async_computation.7 | async-start | bytes 9437184 | tf_op jit(solution)/shard_map/all_gather | solution.py:684
  18.7 188.9 %all-gather.12.cloned.1.call-start = ((), (), s32[]{:S(2)}) async-start(), calls=%async_computation.8 | async-start | bytes 14155776 | tf_op jit(solution)/shard_map/all_gather | solution.py:684
  19.4 286.2 %reduce-scatter.7.cloned.1.call-start = ((), (), s32[]{:S(2)}) async-start(), calls=%async_computation.9 | async-start | bytes 14155776 | tf_op jit(solution)/shard_map/reduce_scatter | solution.py:687
  22.9 19.3 %copy-start.13 = (f32[1024]{0:T(1024)}, f32[1024]{0:T(1024)S(1)}, u32[]{:S(2)}) copy-start(f32[1024]{0:T(1024)S(1)} %get-tuple-element.173) | copy-start | bytes 12292
  42.3 24.8 %copy-start.3 = (f32[128,1024]{1,0:T(8,128)}, f32[128,1024]{1,0:T(8,128)S(1)}, u32[]{:S(2)}) copy-start(f32[128,1024]{1,0:T(8,128)S(1)} %all-gather) | copy-start | bytes 1572868
  54.8 23.2 %collective-permute-start = (bf16[1,2048,1408]{2,1,0:T(8,128)(2,1)}, bf16[1,2048,1408]{2,1,0:T(8,128)(2,1)}, u32[]{:S(2)}, u32[]{:S(2)}) collective-permute-start(bf16[1,2048,1408]{2,1,0:T(8,128)(2,1)} %constant_dynamic-slice_fusion.2), channel_id=1, source_target_pairs={{0,1},{1,0},{2,3},{3,2},{4,5},{5,4},{6,7},{7,6}} | collective-permute-start | bytes 17301512 | tf_op jit(solution)/shard_map/ppermute | solution.py:723
  60.4 17.6 %collective-permute-start.1 = (bf16[1,2048,1408]{2,1,0:T(8,128)(2,1)}, bf16[1,2048,1408]{2,1,0:T(8,128)(2,1)}, u32[]{:S(2)}, u32[]{:S(2)}) collective-permute-start(bf16[1,2048,1408]{2,1,0:T(8,128)(2,1)} %constant_dynamic-slice_fusion.1), channel_id=1, source_target_pairs={{0,1},{1,0},{2,3},{3,2},{4,5},{5,4},{6,7},{7,6}} | collective-permute-start | bytes 17301512 | tf_op jit(solution)/shard_map/ppermute | solution.py:723
  67.0 17.2 %collective-permute-start.2 = (bf16[1,1408,2048]{2,1,0:T(8,128)(2,1)}, bf16[1,1408,2048]{2,1,0:T(8,128)(2,1)}, u32[]{:S(2)}, u32[]{:S(2)}) collective-permute-start(bf16[1,1408,2048]{2,1,0:T(8,128)(2,1)} %constant_dynamic-slice_fusion), channel_id=1, source_target_pairs={{0,1},{1,0},{2,3},{3,2},{4,5},{5,4},{6,7},{7,6}} | collective-permute-start | bytes 17301512 | tf_op jit(solution)/shard_map/ppermute | solution.py:723
  207.7 226.9 %reduce-scatter.9.cloned.1.call-start = ((), (), s32[]{:S(2)}) async-start(), calls=%async_computation.10 | async-start | bytes 9437184 | tf_op jit(solution)/shard_map/reduce_scatter | solution.py:687
  305.7 144.1 %all-gather.14.cloned.1.call-start = ((), (), s32[]{:S(2)}) async-start(), calls=%async_computation.12 | async-start | bytes 14155776 | tf_op jit(solution)/shard_map/all_gather | solution.py:684
  310.3 239.1 %reduce-scatter.11.cloned.1.call-start = ((), (), s32[]{:S(2)}) async-start(), calls=%async_computation.11 | async-start | bytes 14155776 | tf_op jit(solution)/shard_map/reduce_scatter | solution.py:687
  434.6 151.9 %all-gather.18.cloned.1.call-start = ((), (), s32[]{:S(2)}) async-start(), calls=%async_computation.15 | async-start | bytes 9437184 | tf_op jit(solution)/shard_map/all_gather | solution.py:684
  438.4 262.7 %all-gather.16.cloned.1.call-start = ((), (), s32[]{:S(2)}) async-start(), calls=%async_computation.13 | async-start | bytes 14155776 | tf_op jit(solution)/shard_map/all_gather | solution.py:684
  553.1 496.8 %reduce-scatter.15.cloned.1.call-start = ((), (), s32[]{:S(2)}) async-start(), calls=%async_computation.16 | async-start | bytes 9437184 | tf_op jit(solution)/shard_map/reduce_scatter | solution.py:687
  681.6 368.3 %reduce-scatter.13.cloned.1.call-start = ((), (), s32[]{:S(2)}) async-start(), calls=%async_computation.14 | async-start | bytes 14155776 | tf_op jit(solution)/shard_map/reduce_scatter | solution.py:687
  701.1 348.8 %reduce-scatter.17.cloned.1.call-start = ((), (), s32[]{:S(2)}) async-start(), calls=%async_computation.17 | async-start | bytes 14155776 | tf_op jit(solution)/shard_map/reduce_scatter | solution.py:687
  825.7 270.1 %all-reduce.5.cloned.1.call-start = ((), (), s32[]{:S(2)}) async-start(), calls=%async_computation.18 | async-start | bytes 524288
  970.9 75.3 %copy-start.23 = (u32[8]{0:T(128)S(1)}, u32[8]{0:T(128)}, u32[]{:S(2)}) copy-start(u32[8]{0:T(128)} %constant.171) | copy-start | bytes 100
  970.9 75.9 %copy-start.4 = (f32[128,1024]{1,0:T(8,128)S(1)}, f32[128,1024]{1,0:T(8,128)}, u32[]{:S(2)}) copy-start(f32[128,1024]{1,0:T(8,128)} %copy-done.3) | copy-start | bytes 1572868
  970.9 76.1 %copy-start.10 = (f32[2048,128]{1,0:T(8,128)S(1)}, f32[2048,128]{1,0:T(8,128)}, u32[]{:S(2)}) copy-start(f32[2048,128]{1,0:T(8,128)} %get-tuple-element.106) | copy-start | bytes 3145732
  1045.6 102.4 %collective-permute-start.5 = (bf16[1,1408,2048]{2,1,0:T(8,128)(2,1)}, bf16[1,1408,2048]{2,1,0:T(8,128)(2,1)}, u32[]{:S(2)}, u32[]{:S(2)}) collective-permute-start(bf16[1,1408,2048]{2,1,0:T(8,128)(2,1)} %get-tuple-element.115), channel_id=1, source_target_pairs={{0,1},{1,0},{2,3},{3,2},{4,5},{5,4},{6,7},{7,6}} | collective-permute-start | bytes 17301512 | tf_op jit(solution)/shard_map/ppermute | solution.py:765
  1045.7 102.4 %collective-permute-start.3 = (bf16[1,2048,1408]{2,1,0:T(8,128)(2,1)}, bf16[1,2048,1408]{2,1,0:T(8,128)(2,1)}, u32[]{:S(2)}, u32[]{:S(2)}) collective-permute-start(bf16[1,2048,1408]{2,1,0:T(8,128)(2,1)} %get-tuple-element.109), channel_id=1, source_target_pairs={{0,1},{1,0},{2,3},{3,2},{4,5},{5,4},{6,7},{7,6}} | collective-permute-start | bytes 17301512 | tf_op jit(solution)/shard_map/ppermute | solution.py:762
  1046.2 101.9 %collective-permute-start.4 = (bf16[1,2048,1408]{2,1,0:T(8,128)(2,1)}, bf16[1,2048,1408]{2,1,0:T(8,128)(2,1)}, u32[]{:S(2)}, u32[]{:S(2)}) collective-permute-start(bf16[1,2048,1408]{2,1,0:T(8,128)(2,1)} %get-tuple-element.110), channel_id=1, source_target_pairs={{0,1},{1,0},{2,3},{3,2},{4,5},{5,4},{6,7},{7,6}} | collective-permute-start | bytes 17301512 | tf_op jit(solution)/shard_map/ppermute | solution.py:762
  1047.5 11.5 copy-start.7
  1054.2 45.6 %copy-start.12 = (f32[1024,8]{0,1:T(8,128)S(1)}, f32[1024,8]{0,1:T(8,128)}, u32[]{:S(2)}) copy-start(f32[1024,8]{0,1:T(8,128)} %copy-done.11) | copy-start | bytes 98308
  1054.2 45.6 %copy-start.14 = (f32[1024]{0:T(1024)S(1)}, f32[1024]{0:T(1024)}, u32[]{:S(2)}) copy-start(f32[1024]{0:T(1024)} %copy-done.13) | copy-start | bytes 12292
  1054.2 45.6 %copy-start.18 = (f32[1024]{0:T(1024)S(1)}, f32[1024]{0:T(1024)}, u32[]{:S(2)}) copy-start(f32[1024]{0:T(1024)} %copy-done.17) | copy-start | bytes 12292
  1059.1 43.7 %copy-start.16 = (f32[2048]{0:T(1024)S(1)}, f32[2048]{0:T(1024)}, u32[]{:S(2)}) copy-start(f32[2048]{0:T(1024)} %copy-done.15) | copy-start | bytes 24580
  1059.1 43.7 %copy-start.20 = (f32[1024]{0:T(1024)S(1)}, f32[1024]{0:T(1024)}, u32[]{:S(2)}) copy-start(f32[1024]{0:T(1024)} %copy-done.19) | copy-start | bytes 12292
  1061.1 41.7 %copy-start.9 = (f32[384,2048]{1,0:T(8,128)S(1)}, f32[384,2048]{1,0:T(8,128)}, u32[]{:S(2)}) copy-start(f32[384,2048]{1,0:T(8,128)} %convert_element_type.124) | copy-start | bytes 9437188
  (12 other events, 48.9 us)
Sparse Core Ops, SparseCore 0:
  16.4 72.2 all-gather.7
  90.5 48.3 all-gather.9
  141.3 66.2 all-gather.11
  211.5 94.1 reduce-scatter.6
  308.9 72.2 reduce-scatter.8
  383.4 66.2 all-gather.13
  453.8 82.4 reduce-scatter.10
  538.1 48.3 all-gather.17
  588.3 66.2 all-gather.15
  681.7 63.8 reduce-scatter.14
  749.1 82.4 reduce-scatter.12
  834.9 82.6 reduce-scatter.16
  1053.0 42.6 all-reduce.4
where the time goes:
time: 1180 us; the launch traced here: 1170 us
  Pallas kernels  908 us (77%)
  waiting for transfers between devices  95.2 us (8%)
  blocking collectives  42.3 us (4%)
  local copies, waits for them, and re-layouts  41.2 us (3%)
  other arithmetic  39.5 us (3%)
  between operations  22.5 us (2%)
  matrix products  19.6 us (2%)
    pallas_call x14, Pallas kernels, call(): pl.pallas_call(kernel, grid_spec=pltpu.PrefetchScalarGridSpec(num_scalar_...  895 us
    all_gather x6, waiting for transfers between devices, gather(): return lax.all_gather(rows, rows_axes, axis=0, tiled=True)  49.8 us
    unnamed x14, waiting for transfers between devices  35.5 us
    psum x1, blocking collectives, body(): lax.psum((jnp.sum(x_norm_grad * unit, axis=0), jnp.einsum('sd,se->de', x_...  23.6 us
  transfers between devices with their start and end apart: 19, of which 7 were waited for; matrix products, arithmetic and copies ran while one was open for 8% of the time, Pallas kernels for 76%

commit v1 on v0

--- a/solution.py
+++ b/solution.py
@@ -6,6 +6,7 @@
 from jax.experimental import pallas as pl
 from jax.experimental.pallas import tpu as pltpu
 from jax.sharding import PartitionSpec as P
+
 
 NORM_EPS = 1e-6
 ACT_COEF = 1e-5
@@ -16,10 +17,11 @@
 PARTS = (384, 256, 384)
 CHUNKS = len(PARTS)
 WINDOWS = (1, 2, 3, 4)
-VMEM_LIMIT = 62 * 1024 * 1024
-
-
-def call(kernel, name, table, operands, in_specs, out_shape, out_specs, scratch, cost, grid=()):
+STATS_SIZE = 65536
+VMEM_LIMIT = 67_043_328
+
+
+def call(kernel, table, operands, in_specs, out_shape, out_specs, scratch, cost, grid=()):
     return pl.pallas_call(
         kernel,
         grid_spec=pltpu.PrefetchScalarGridSpec(
@@ -28,7 +30,6 @@
         out_shape=out_shape,
         compiler_params=pltpu.CompilerParams(vmem_limit_bytes=VMEM_LIMIT),
         cost_estimate=pl.CostEstimate(flops=cost[0], bytes_accessed=cost[1], transcendentals=0),
-        name=name,
     )(table, *operands)
 
 
@@ -40,76 +41,73 @@
     return pl.BlockSpec((TILE, width), lambda t: (t, 0))
 
 
-def dispatch_phase(at, spans, table_ref, pos_ref, prob_ref, tok_hbm, outs):
-    tokens, dim = tok_hbm.shape
-    blocks = tokens // TILE
-
-    def run(tok, waited, sems):
-        def block_copy(index):
-            rows = pl.ds(index * TILE if isinstance(index, int) else pl.multiple_of(index * TILE, TILE), TILE)
-            return pltpu.make_async_copy(tok_hbm.at[rows, :], tok.at[rows, :], sems.at[index])
-
-        waited[0] = 0
-        for index in range(blocks):
-            block_copy(index).start()
-
-        def await_tokens(stop_span):
-            need = (stop_span * LANES + TILE - 1) // TILE
-
-            @pl.loop(waited[0], need)
-            def _(index):
-                block_copy(index).wait()
-
-            waited[0] = jnp.maximum(waited[0], need)
-
-        def tile_body(x_ref, gate_ref=None):
-            tile = pl.program_id(0)
-            group = table_ref[at["group"] + tile]
-            width = table_ref[at["width"] + tile]
-
-            def window(half, count, start):
-                row_id = lax.broadcasted_iota(jnp.int32, (LANES, LANES), 0) + (tile * TILE + half * LANES)
-                into = pl.ds(half * LANES if isinstance(half, int) else pl.multiple_of(half * LANES, LANES), LANES)
-                hot, gate = [], jnp.zeros((LANES, LANES), jnp.float32)
-                for q in range(count):
-                    span = pl.ds(spans[0] + start + q, 1)
-                    match = pos_ref[group, span, :] == row_id
-                    hot.append(jnp.where(match, 1.0, 0.0).astype(jnp.bfloat16))
-                    if gate_ref is not None:
-                        gate = gate + jnp.where(match, prob_ref[group, span, :], 0.0)
-                rows = tok[pl.ds(pl.multiple_of(start * LANES, LANES), count * LANES), :]
-                out = jnp.dot(jnp.concatenate(hot, axis=1), rows, preferred_element_type=jnp.float32)
-                x_ref[into, :] = out.astype(x_ref.dtype)
+class Dispatch:
+    def __init__(self, at, table_ref, pos_ref, prob_ref, tok_hbm, scratch):
+        self.at, self.table_ref, self.pos_ref, self.prob_ref, self.tok_hbm = at, table_ref, pos_ref, prob_ref, tok_hbm
+        self.tok, self.waited, self.sems = scratch
+        self.first, self.spans = at["spans"]
+
+    def block_copy(self, index):
+        rows = pl.ds(index * TILE if isinstance(index, int) else pl.multiple_of(index * TILE, TILE), TILE)
+        return pltpu.make_async_copy(self.tok_hbm.at[rows, :], self.tok.at[rows, :], self.sems.at[index])
+
+    def begin(self):
+        self.waited[0] = 0
+        for index in range(self.spans * LANES // TILE):
+            self.block_copy(index).start()
+
+    def await_tokens(self, stop_span):
+        need = (stop_span * LANES + TILE - 1) // TILE
+
+        @pl.loop(self.waited[0], need)
+        def _(index):
+            self.block_copy(index).wait()
+
+        self.waited[0] = jnp.maximum(self.waited[0], need)
+
+    def end(self):
+        self.await_tokens(self.spans)
+
+    def tile(self, x_ref, gate_ref=None):
+        tile = pl.program_id(0)
+        group = self.table_ref[self.at["group"] + tile]
+        width = self.table_ref[self.at["width"] + tile]
+
+        def window(half, count, start):
+            row_id = lax.broadcasted_iota(jnp.int32, (LANES, LANES), 0) + (tile * TILE + half * LANES)
+            into = pl.ds(half * LANES if isinstance(half, int) else pl.multiple_of(half * LANES, LANES), LANES)
+            hot, gate = [], jnp.zeros((LANES, LANES), jnp.float32)
+            for q in range(count):
+                span = pl.ds(self.first + start + q, 1)
+                match = self.pos_ref[group, span, :] == row_id
+                hot.append(jnp.where(match, 1.0, 0.0).astype(jnp.bfloat16))
                 if gate_ref is not None:
-                    gate_ref[into, :] = jnp.broadcast_to(jnp.sum(gate, axis=1, keepdims=True), (LANES, LANES))
-
-            @pl.when(width > WINDOWS[-1])
-            def _():
-                await_tokens(spans[1])
-
-                @pl.loop(0, 2)
-                def _(half):
-                    window(half, spans[1], 0)
-
-            for k in WINDOWS:
-                @pl.when(width == k)
-                def _(k=k):
-                    starts = [jnp.minimum(table_ref[at["lo"] + 2 * tile + half], spans[1] - 2 * k) for half in range(2)]
-                    await_tokens(jnp.maximum(starts[0], starts[1]) + 2 * k)
-                    for half in range(2):
-                        window(half, 2 * k, starts[half])
-
-        pltpu.emit_pipeline(
-            tile_body, grid=(table_ref[at["count"]],), out_specs=[row_block(out.shape[1]) for out in outs]
-        )(*outs)
-        await_tokens(spans[1])
-
-    pl.run_scoped(
-        run,
-        pltpu.VMEM((tokens, dim), jnp.bfloat16),
-        pltpu.SMEM((1,), jnp.int32),
-        pltpu.SemaphoreType.DMA((blocks,)),
-    )
+                    gate = gate + jnp.where(match, self.prob_ref[group, span, :], 0.0)
+            rows = self.tok[pl.ds(pl.multiple_of(start * LANES, LANES), count * LANES), :]
+            out = jnp.dot(jnp.concatenate(hot, axis=1), rows, preferred_element_type=jnp.float32)
+            x_ref[into, :] = out.astype(x_ref.dtype)
+            if gate_ref is not None:
+                gate_ref[into, :] = jnp.broadcast_to(jnp.sum(gate, axis=1, keepdims=True), (LANES, LANES))
+
+        @pl.when(width > WINDOWS[-1])
+        def _():
+            self.await_tokens(self.spans)
+
+            @pl.loop(0, 2)
+            def _(half):
+                window(half, self.spans, 0)
+
+        for k in WINDOWS:
+            @pl.when(width == k)
+            def _(k=k):
+                starts = [jnp.minimum(self.table_ref[self.at["lo"] + 2 * tile + half], self.spans - 2 * k) for half in range(2)]
+                self.await_tokens(jnp.maximum(starts[0], starts[1]) + 2 * k)
+                for half in range(2):
+                    window(half, 2 * k, starts[half])
+
+
+def dispatch_scratch(tok):
+    return [pltpu.VMEM(tok.shape, tok.dtype), pltpu.SMEM((1,), jnp.int32), pltpu.SemaphoreType.DMA((tok.shape[0] // TILE,))]
 
 
 def combine_kernel(at, spans, groups, with_gate, table_ref, pos_ref, rows_hbm, *rest):
@@ -235,7 +233,7 @@
         scratch.append(pltpu.VMEM((rows_max, LANES), jnp.float32))
     scratch += [pltpu.SMEM((groups,), jnp.int32), pltpu.SemaphoreType.DMA((2, rows_max // TILE))]
     kernel = functools.partial(combine_kernel, layout[chunk], spans, groups, with_gate)
-    return call(kernel, "combine", table, operands, in_specs, out_shape, out_specs, scratch, (9 * 10**9, 35 * 10**6), (tokens // block,))
+    return call(kernel, table, operands, in_specs, out_shape, out_specs, scratch, (9 * 10**9, 35 * 10**6), (tokens // block,))
 
 
 class WeightStream:
@@ -279,14 +277,23 @@
         return s
 
 
-def forward_kernel(at, spans, table_ref, pos_ref, prob_ref, tok_hbm, *rest):
-    x_hbm, gate_hbm, ab_hbm, h_hbm, out_hbm = rest[6:11]
-    stream = WeightStream(at, table_ref, rest[:6], rest[11:])
+def run_tiles(at, table_ref, tile_body, piped_in, piped_out):
+    pltpu.emit_pipeline(
+        tile_body, grid=(table_ref[at["count"]],),
+        in_specs=[row_block(ref.shape[1]) for ref in piped_in],
+        out_specs=[row_block(ref.shape[1]) for ref in piped_out],
+    )(*piped_in, *piped_out)
+
+
+def forward_kernel(at, table_ref, pos_ref, prob_ref, tok_hbm, *rest):
+    stream = WeightStream(at, table_ref, rest[:6], rest[11:14])
+    dispatch = Dispatch(at, table_ref, pos_ref, prob_ref, tok_hbm, rest[14:])
     wide, down, ffn = stream.wide, stream.down, stream.ffn
+    dispatch.begin()
     stream.begin()
-    dispatch_phase(at, spans, table_ref, pos_ref, prob_ref, tok_hbm, (x_hbm, gate_hbm))
 
     def tile_body(x_ref, gate_ref, ab_ref, h_ref, out_ref):
+        dispatch.tile(x_ref, gate_ref)
         slot = stream.slot()
         x = x_ref[...]
         for j in range(ffn // LANES):
@@ -303,23 +310,21 @@
             cols = slice(j * LANES, (j + 1) * LANES)
             out_ref[:, cols] = (out[:, cols] * gate).astype(out_ref.dtype)
 
-    piped_in, piped_out = (x_hbm, gate_hbm), (ab_hbm, h_hbm, out_hbm)
-    pltpu.emit_pipeline(
-        tile_body, grid=(table_ref[at["count"]],),
-        in_specs=[row_block(ref.shape[1]) for ref in piped_in],
-        out_specs=[row_block(ref.shape[1]) for ref in piped_out],
-    )(*piped_in, *piped_out)
-
-
-def backward_kernel(at, spans, table_ref, pos_ref, tok_hbm, ab_hbm, h_hbm, gate_hbm, *rest):
-    m_hbm, d_hbm, in_hbm, mg_hbm, dgate_hbm = rest[6:11]
-    stream = WeightStream(at, table_ref, rest[:6], rest[11:])
+    run_tiles(at, table_ref, tile_body, (), rest[6:11])
+    dispatch.end()
+
+
+def backward_kernel(at, table_ref, pos_ref, tok_hbm, ab_hbm, h_hbm, gate_hbm, *rest):
+    stream = WeightStream(at, table_ref, rest[:6], rest[10:13])
+    m_ref = rest[13]
+    dispatch = Dispatch(at, table_ref, pos_ref, None, tok_hbm, rest[14:])
     wide, down, ffn = stream.wide, stream.down, stream.ffn
     trans = (((1,), (1,)), ((), ()))
+    dispatch.begin()
     stream.begin()
-    dispatch_phase(at, spans, table_ref, pos_ref, None, tok_hbm, (m_hbm,))
-
-    def tile_body(m_ref, ab_ref, h_ref, gate_ref, d_ref, in_ref, mg_ref, dgate_ref):
+
+    def tile_body(ab_ref, h_ref, gate_ref, d_ref, in_ref, mg_ref, dgate_ref):
+        dispatch.tile(m_ref)
         slot = stream.slot()
         m = m_ref[...]
         gate = gate_ref[...]
@@ -346,12 +351,8 @@
         expert = table_ref[at["expert"] + table_ref[at["group"] + pl.program_id(0)]]
         dgate_ref[...] = jnp.where(lane == expert, jnp.sum(dgate, axis=1, keepdims=True), 0.0)
 
-    piped_in, piped_out = (m_hbm, ab_hbm, h_hbm, gate_hbm), (d_hbm, in_hbm, mg_hbm, dgate_hbm)
-    pltpu.emit_pipeline(
-        tile_body, grid=(table_ref[at["count"]],),
-        in_specs=[row_block(ref.shape[1]) for ref in piped_in],
-        out_specs=[row_block(ref.shape[1]) for ref in piped_out],
-    )(*piped_in, *piped_out)
+    run_tiles(at, table_ref, tile_body, (ab_hbm, h_hbm, gate_hbm), rest[6:10])
+    dispatch.end()
 
 
 def weight_scratch(wg):
@@ -371,21 +372,20 @@
     _, dim, ffn = weights[0].shape
     kinds = ((dim, jnp.bfloat16), (LANES, jnp.float32), (2 * ffn, jnp.float32), (ffn, jnp.bfloat16), (dim, jnp.bfloat16))
     at = layout[chunk]
-    kernel = functools.partial(forward_kernel, at, at["spans"])
     return call(
-        kernel, "forward", table, (pos, prob, tok, *weights), [WHOLE, WHOLE] + [ANY] * 7,
-        shapes(at["rows_max"], *kinds), [ANY] * 5, weight_scratch(weights[0]), (75 * 10**9, 150 * 10**6),
+        functools.partial(forward_kernel, at), table, (pos, prob, tok, *weights), [WHOLE, WHOLE] + [ANY] * 7,
+        shapes(at["rows_max"], *kinds), [ANY] * 5, weight_scratch(weights[0]) + dispatch_scratch(tok), (75 * 10**9, 150 * 10**6),
     )
 
 
 def backward(layout, chunk, table, pos, tok, ab, hidden, gates, weights):
     _, dim, ffn = weights[0].shape
-    kinds = ((dim, jnp.bfloat16), (2 * ffn, jnp.bfloat16), (dim, jnp.bfloat16), (dim, jnp.bfloat16), (LANES, jnp.float32))
+    kinds = ((2 * ffn, jnp.bfloat16), (dim, jnp.bfloat16), (dim, jnp.bfloat16), (LANES, jnp.float32))
     at = layout[chunk]
-    kernel = functools.partial(backward_kernel, at, at["spans"])
+    scratch = [*weight_scratch(weights[0]), pltpu.VMEM((TILE, dim), jnp.bfloat16), *dispatch_scratch(tok)]
     return call(
-        kernel, "backward", table, (pos, tok, ab, hidden, gates, *weights), [WHOLE] + [ANY] * 10,
-        shapes(at["rows_max"], *kinds), [ANY] * 5, weight_scratch(weights[0]), (75 * 10**9, 150 * 10**6),
+        functools.partial(backward_kernel, at), table, (pos, tok, ab, hidden, gates, *weights), [WHOLE] + [ANY] * 10,
+        shapes(at["rows_max"], *kinds), [ANY] * 4, scratch, (75 * 10**9, 150 * 10**6),
     )
 
 
@@ -497,13 +497,13 @@
     ]
     out_shape = [jax.ShapeDtypeStruct((n, left, width), jnp.bfloat16) for n in [experts] * outs + [1] * outs]
     return call(
-        kernel, "weight_grad", table, (*lhs, *rhs), [ANY] * (2 * CHUNKS), out_shape, [ANY] * len(out_shape),
+        kernel, table, (*lhs, *rhs), [ANY] * (2 * CHUNKS), out_shape, [ANY] * len(out_shape),
         scratch, (2 * 9000 * left * right, 100 * 10**6),
     )
 
 
-def insert_kernel(at, table_ref, *rest):
-    back, outs, staged, sems = rest[:3], rest[6:9], rest[9:12], rest[12]
+def insert_kernel(at, size, table_ref, *rest):
+    back, outs, staged, sems = rest[:size], rest[2 * size:3 * size], rest[3 * size:4 * size], rest[4 * size]
     place = table_ref[at]
 
     @pl.when(place >= 0)
@@ -512,7 +512,7 @@
         store = [pltpu.make_async_copy(s, out.at[place], sems.at[1, i]) for i, (s, out) in enumerate(zip(staged, outs))]
         for copy in fetch:
             copy.start()
-        for i in range(3):
+        for i in range(size):
             fetch[i].wait()
             store[i].start()
         for copy in store:
@@ -520,19 +520,19 @@
 
 
 def insert(layout, table, back, grads):
-    kernel = functools.partial(insert_kernel, layout["insert"])
+    size = len(grads)
     return pl.pallas_call(
-        kernel,
+        functools.partial(insert_kernel, layout["insert"], size),
         grid_spec=pltpu.PrefetchScalarGridSpec(
             num_scalar_prefetch=1,
-            in_specs=[ANY] * 6,
-            out_specs=[ANY] * 3,
-            scratch_shapes=[pltpu.VMEM(g.shape[1:], g.dtype) for g in grads] + [pltpu.SemaphoreType.DMA((2, 3))],
+            in_specs=[ANY] * (2 * size),
+            out_specs=[ANY] * size,
+            scratch_shapes=[pltpu.VMEM(g.shape[1:], g.dtype) for g in grads] + [pltpu.SemaphoreType.DMA((2, size))],
         ),
         out_shape=[jax.ShapeDtypeStruct(g.shape, g.dtype) for g in grads],
-        input_output_aliases={4 + i: i for i in range(3)},
+        input_output_aliases={1 + size + i: i for i in range(size)},
         compiler_params=pltpu.CompilerParams(vmem_limit_bytes=VMEM_LIMIT),
-        cost_estimate=pl.CostEstimate(flops=10**9, bytes_accessed=35 * 10**6, transcendentals=0),
+        cost_estimate=pl.CostEstimate(flops=10**9, bytes_accessed=15 * 10**6 * size, transcendentals=0),
         name="insert",
     )(table, *back, *grads)
 
@@ -554,15 +554,14 @@
     return jnp.sum(condition.astype(jnp.int32), axis=axis)
 
 
-def choose_help(tiles, experts):
-    half = [jnp.sum(tiles[:experts]), jnp.sum(tiles[experts:])]
-    gap = jnp.abs(half[0] - half[1])
-    index = jnp.arange(2 * experts, dtype=jnp.int32)
-    on_busier = (index >= experts) == (half[1] > half[0])
-    left = jnp.where(on_busier, jnp.abs(gap - 2 * tiles), gap)
-    best = jnp.min(left)
-    moved = jnp.min(jnp.where(left == best, index, 2 * experts))
-    return jnp.where(best < gap, moved, -1)
+def choose_swap(tiles, experts):
+    none = jnp.zeros((1,), jnp.int32)
+    options = [jnp.concatenate([none, tiles[:experts]]), jnp.concatenate([none, tiles[experts:]])]
+    gap = jnp.sum(tiles[:experts]) - jnp.sum(tiles[experts:])
+    left = jnp.abs(gap - 2 * options[0][:, None] + 2 * options[1][None, :])
+    index = lax.broadcasted_iota(jnp.int32, left.shape, 0) * (experts + 1) + lax.broadcasted_iota(jnp.int32, left.shape, 1)
+    best = jnp.min(jnp.where(left == jnp.min(left), index, left.size))
+    return best // (experts + 1) - 1, best % (experts + 1) - 1
 
 
 def routing(hot, experts_of, place):
@@ -706,21 +705,20 @@
 
         rows_in = jnp.stack([jnp.sum(of_chunk(small[:, :num_experts], c, 2), axis=(0, 2)) for c in range(CHUNKS)])
         tiles_in = jnp.sum((rows_in.astype(jnp.int32) + TILE - 1) // TILE, axis=0)
-        moved = choose_help(tiles_in, local_experts)
+        gives = choose_swap(tiles_in, local_experts)
+        given = jnp.where(my_ep == 0, gives[0], gives[1])
+        taken = jnp.where(my_ep == 0, gives[1], gives[0])
         my_base = my_ep * local_experts
         local = jnp.arange(local_experts, dtype=jnp.int32)
-        giving = jnp.logical_and(moved >= my_base, moved < my_base + local_experts)
-        helping = jnp.logical_and(moved >= 0, jnp.logical_not(giving))
-        given = jnp.where(giving, moved - my_base, 0)
-        group_experts = jnp.concatenate([my_base + local, jnp.maximum(moved, 0).reshape(1)])
-        active = jnp.concatenate([my_base + local != moved, helping.reshape(1)])
+        group_experts = jnp.concatenate([my_base + local, (local_experts - my_base + jnp.maximum(taken, 0)).reshape(1)])
+        active = jnp.concatenate([local != given, (taken >= 0).reshape(1)])
         take = jnp.logical_and(group_experts[:, None] == expert_range, active[:, None])
         spread = jnp.concatenate([of_chunk(small, c, 2).transpose(1, 0, 2).reshape(2 * num_experts, -1) for c in range(CHUNKS)], axis=1)
         spread = spread.reshape(2, 1, num_experts, -1, LANES)
         own = jnp.sum(jnp.where(take[None, :, :, None, None], spread, 0.0), axis=2)
         prob = own[1]
-        pos, table, layout = routing(own[0], group_experts, jnp.where(giving, given, -1))
-        helped = [lax.ppermute(lax.dynamic_slice_in_dim(w, given, 1, axis=0), "ep", swap) for w in (w_gate, w_up, w_down)]
+        pos, table, layout = routing(own[0], group_experts, given)
+        helped = [lax.ppermute(lax.dynamic_slice_in_dim(w, jnp.maximum(given, 0), 1, axis=0), "ep", swap) for w in (w_gate, w_up, w_down)]
         weights = (w_gate, w_up, w_down, *helped)
 
         grad_scale = 2.0 * ACT_COEF / (total_tokens * model_dim)
@@ -748,7 +746,7 @@
             pre.append(ab)
             hidden.append(h)
         for c in range(CHUNKS):
-            _, d, in_rows, mg, dgate = backward(layout, c, table, pos, m_tok[c], pre[c], hidden[c], gate_rows[c], weights)
+            d, in_rows, mg, dgate = backward(layout, c, table, pos, m_tok[c], pre[c], hidden[c], gate_rows[c], weights)
             if c == 0:
                 in_rows = send_cotangent(CHUNKS - 1, in_rows)
             partial, gate_tok = combine(layout, c, table, pos, in_rows, dgate)
@@ -760,32 +758,36 @@
             mg_rows.append(mg)
         *wide_grads, helped_gate, helped_up = weight_grad(layout, table, x_rows, d_rows, local_experts, 2)
         back = [lax.ppermute(g, "ep", swap) for g in (helped_gate, helped_up)]
-        mg_rows[0], _ = after(mg_rows[0], wide_grads[0])
-        down_grad, helped_down = weight_grad(layout, table, hidden, mg_rows, local_experts, 1)
-        back.append(lax.ppermute(helped_down, "ep", swap))
-
+
+        sums = jnp.concatenate([g.reshape(dev_count, -1) for g in gate_part], axis=1)
+        sums, _ = after(sums, in_raw[:CHUNKS - 1])
+        gate_weight_grad = lax.psum_scatter(sums, rows_axes, scatter_dimension=0, tiled=False)
+        gate_weight_grad, (wide_grads, in_raw) = after(gate_weight_grad, (wide_grads, in_raw))
         moe_all = jnp.concatenate(moe_out, axis=0)
         y = (x_float + moe_all).astype(jnp.bfloat16)
-        gate_part[0], _ = after(gate_part[0], (wide_grads[0], in_raw))
-        sums = jnp.concatenate([g.reshape(dev_count, -1) for g in gate_part], axis=1)
-        gate_weight_grad = lax.psum_scatter(sums, rows_axes, scatter_dimension=0, tiled=False)
         prob_grad = gate_weight_grad.reshape(tokens, num_experts) + balance_scale * counts[None, :]
         logit_grad = (route_prob * (prob_grad - jnp.sum(route_prob * prob_grad, axis=-1, keepdims=True))).astype(jnp.bfloat16)
         x_norm_grad = jnp.concatenate(in_raw, axis=0).astype(jnp.float32)
         x_norm_grad = x_norm_grad + jnp.einsum("se,de->sd", logit_grad, w_router, preferred_element_type=jnp.float32)
         unit_grad = x_norm_grad * gain
         x_grad = y_grad.astype(jnp.float32) + inv_rms * (unit_grad - unit * jnp.mean(unit_grad * unit, axis=-1, keepdims=True))
-        gain_sum, router_sum, act_sum = lax.psum(
-            (
-                jnp.sum(x_norm_grad * unit, axis=0),
-                jnp.einsum("sd,se->de", x_norm, logit_grad, preferred_element_type=jnp.float32),
-                jnp.sum(moe_all * moe_all),
-            ),
-            ("tp", "ep"),
+        x_grad = x_grad.astype(jnp.bfloat16)
+        stats = (
+            jnp.sum(x_norm_grad * unit, axis=0),
+            jnp.einsum("sd,se->de", x_norm, logit_grad, preferred_element_type=jnp.float32).reshape(-1),
+            jnp.sum(moe_all * moe_all).reshape(1),
         )
-        table, _ = after(table, (x_grad, gain_sum))
-        act_loss = ACT_COEF * act_sum / (total_tokens * model_dim)
-        gate_grad, up_grad, down_grad = insert(layout, table, back, (*wide_grads, down_grad))
-        return (y, x_grad.astype(jnp.bfloat16), gain_sum.astype(jnp.bfloat16), router_sum.astype(jnp.bfloat16), gate_grad, up_grad, down_grad, balance_loss, act_loss)
+        size = sum(s.size for s in stats)
+        stats = jnp.concatenate([*stats, jnp.zeros((STATS_SIZE - size,), jnp.float32)]).reshape(dev_count, -1)
+        gate_grad, up_grad = insert(layout, table, back, wide_grads)
+        stats, (mg_rows[0], x_grad, gate_grad) = after(stats, (mg_rows[0], x_grad, gate_grad))
+        down_grad, helped_down = weight_grad(layout, table, hidden, mg_rows, local_experts, 1)
+        (down_grad,) = insert(layout, table, [lax.ppermute(helped_down, "ep", swap)], [down_grad])
+        stats = lax.psum(stats, ("tp", "ep"))
+        stats = stats.reshape(-1)
+        gain_sum = stats[:model_dim]
+        router_sum = stats[model_dim:size - 1].reshape(model_dim, num_experts)
+        act_loss = ACT_COEF * stats[size - 1] / (total_tokens * model_dim)
+        return (y, x_grad, gain_sum.astype(jnp.bfloat16), router_sum.astype(jnp.bfloat16), gate_grad, up_grad, down_grad, balance_loss, act_loss)
 
     return jax.shard_map(body, mesh=mesh, in_specs=(row_spec, row_spec, row_spec, P(), P(), wide_spec, wide_spec, down_spec), out_specs=(row_spec, row_spec, P(), P(), wide_spec, wide_spec, down_spec, P(), P()), check_vma=False)

time: 1180 us -> 1190 us (level)
  Pallas kernels: 908 us -> 932 us
  blocking collectives: 42.3 us -> 19.1 us
    psum x0 -> x1, waiting for transfers between devices: none -> 42.6 us  [body(): stats = lax.psum(stats, ('tp', 'ep'))]
    unnamed x14 -> x15, waiting for transfers between devices: 35.5 us -> 1.58 us
    psum x1 -> x0, blocking collectives: 23.6 us -> none  [body(): lax.psum((jnp.sum(x_norm_grad * unit, axis=0), jnp.einsum('sd,se->de', x_...]
    pallas_call x14, Pallas kernels: 895 us -> 917 us  [call(): pl.pallas_call(kernel, grid_spec=pltpu.PrefetchScalarGridSpec(num_scalar_...]
    all_gather x6, waiting for transfers between devices: 49.8 us -> 34.4 us  [gather(): return lax.all_gather(rows, rows_axes, axis=0, tiled=True)]
  transfers between devices with their start and end apart: 19 -> 20, of which waited for: 7 -> 6; matrix products, arithmetic and copies ran while one was open for 8% -> 8% of each run, Pallas kernels for 76% -> 71%
where the time goes in v1:
time: 1190 us; the launch traced here: 1180 us
  Pallas kernels  932 us (78%)
  waiting for transfers between devices  93.1 us (8%)
  local copies, waits for them, and re-layouts  51.5 us (4%)
  other arithmetic  46.3 us (4%)
  between operations  21.8 us (2%)
  blocking collectives  19.1 us (2%)
  matrix products  15.7 us (1%)
    pallas_call x14, Pallas kernels, call(): pl.pallas_call(kernel, grid_spec=pltpu.PrefetchScalarGridSpec(num_scalar_...  917 us
    psum x1, waiting for transfers between devices, body(): stats = lax.psum(stats, ('tp', 'ep'))  42.6 us
    all_gather x6, waiting for transfers between devices, gather(): return lax.all_gather(rows, rows_axes, axis=0, tiled=True)  34.4 us
  transfers between devices with their start and end apart: 20, of which 6 were waited for; matrix products, arithmetic and copies ran while one was open for 8% of the time, Pallas kernels for 71%

profile of v1, /device:TPU:0, one launch (start us, length us, event | category | flops | bytes accessed | tf_op | source)
XLA Modules:
  0.0 1181.4 jit_solution(11684381723570296215)
XLA Ops:
  7.2 3.2 fusion.11
  19.6 3.4 fusion.70
  23.7 19.1 %all-gather = f32[128,1024]{1,0:T(8,128)S(1)} all-gather(f32[16,1024]{1,0:T(8,128)S(1)} %maximum_bitcast_fusion.1), channel_id=2, replica_groups=mesh['tp'=4,'ep'=2] {'ep','tp'}, dimensions={0}, use_global_device_ids=true | all-gather | bytes 589824 | tf_op jit(solution)/shard_map/all_gather | solution.py:701
  49.2 6.6 constant_dynamic-slice_fusion
  55.8 5.6 constant_dynamic-slice_fusion.2
  62.0 6.3 constant_dynamic-slice_fusion.1
  79.3 6.4 collective-permute-done.2.rest_5_
  88.8 109.8 %shard_map.160 = (bf16[7424,2048]{1,0:T(8,128)(2,1)}, f32[7424,128]{1,0:T(8,128)}, f32[7424,2816]{1,0:T(8,128)}, bf16[7424,1408]{1,0:T(8,128)(2,1)}, bf16[7424,2048]{1,0:T(8,128)(2,1)}) custom-call(s32[1117]{0:T(1024)} %concatenate.52.table_ref, s32[5,64,128]{2,1,0:T(8,128)} %fusion.15.pos_ref, f32[5,64,128]{2,1,0:T(8,128)} %get-tuple-element.210.prob_ref, ...), custom_call_target="tpu_custom_call" | custom-call | flops 74999996416 | bytes 150000000 | tf_op jit(solution)/shard_map/pallas_call | solution.py:25
  198.7 17.7 %shard_map.161 = bf16[3072,2048]{1,0:T(8,128)(2,1)} custom-call(s32[1117]{0:T(1024)} %concatenate.52.table_ref, s32[5,64,128]{2,1,0:T(8,128)} %fusion.15.pos_ref, bf16[7424,2048]{1,0:T(8,128)(2,1)} %get-tuple-element.72.rows_hbm), custom_call_target="tpu_custom_call" | custom-call | flops 8999999488 | bytes 35000000 | tf_op jit(solution)/shard_map/pallas_call | solution.py:25
  216.5 78.6 %shard_map.162 = (bf16[5376,2048]{1,0:T(8,128)(2,1)}, f32[5376,128]{1,0:T(8,128)}, f32[5376,2816]{1,0:T(8,128)}, bf16[5376,1408]{1,0:T(8,128)(2,1)}, bf16[5376,2048]{1,0:T(8,128)(2,1)}) custom-call(s32[1117]{0:T(1024)} %concatenate.52.table_ref, s32[5,64,128]{2,1,0:T(8,128)} %fusion.15.pos_ref, f32[5,64,128]{2,1,0:T(8,128)} %get-tuple-element.210.prob_ref, ...), custom_call_target="tpu_custom_call" | custom-call | flops 74999996416 | bytes 150000000 | tf_op jit(solution)/shard_map/pallas_call | solution.py:25
  295.1 13.7 %shard_map.163 = bf16[2048,2048]{1,0:T(8,128)(2,1)} custom-call(s32[1117]{0:T(1024)} %concatenate.52.table_ref, s32[5,64,128]{2,1,0:T(8,128)} %fusion.15.pos_ref, bf16[5376,2048]{1,0:T(8,128)(2,1)} %get-tuple-element.75.rows_hbm), custom_call_target="tpu_custom_call" | custom-call | flops 8999999488 | bytes 35000000 | tf_op jit(solution)/shard_map/pallas_call | solution.py:25
  313.4 109.5 %shard_map.164 = (bf16[7424,2048]{1,0:T(8,128)(2,1)}, f32[7424,128]{1,0:T(8,128)}, f32[7424,2816]{1,0:T(8,128)}, bf16[7424,1408]{1,0:T(8,128)(2,1)}, bf16[7424,2048]{1,0:T(8,128)(2,1)}) custom-call(s32[1117]{0:T(1024)} %concatenate.52.table_ref, s32[5,64,128]{2,1,0:T(8,128)} %fusion.15.pos_ref, f32[5,64,128]{2,1,0:T(8,128)} %get-tuple-element.210.prob_ref, ...), custom_call_target="tpu_custom_call" | custom-call | flops 74999996416 | bytes 150000000 | tf_op jit(solution)/shard_map/pallas_call | solution.py:25
  422.9 17.7 %shard_map.165 = bf16[3072,2048]{1,0:T(8,128)(2,1)} custom-call(s32[1117]{0:T(1024)} %concatenate.52.table_ref, s32[5,64,128]{2,1,0:T(8,128)} %fusion.15.pos_ref, bf16[7424,2048]{1,0:T(8,128)(2,1)} %get-tuple-element.79.rows_hbm), custom_call_target="tpu_custom_call" | custom-call | flops 8999999488 | bytes 35000000 | tf_op jit(solution)/shard_map/pallas_call | solution.py:25
  444.6 8.3 all-gather.14.cloned.1.call-done.tok_hbm
  453.0 111.0 %shard_map.166 = (bf16[7424,2816]{1,0:T(8,128)(2,1)}, bf16[7424,2048]{1,0:T(8,128)(2,1)}, bf16[7424,2048]{1,0:T(8,128)(2,1)}, f32[7424,128]{1,0:T(8,128)}) custom-call(s32[1117]{0:T(1024)} %concatenate.52.table_ref, s32[5,64,128]{2,1,0:T(8,128)} %fusion.15.pos_ref, bf16[3072,2048]{1,0:T(8,128)(2,1)} %all-gather.14.cloned.1.call-done.tok_hbm, ...), custom_call_target="tpu_custom_call" | custom-call | flops 74999996416 | bytes 150000000 | tf_op jit(solution)/shard_map/pallas_call | solution.py:25
  564.0 4.5 add_convert_fusion
  568.6 22.9 %all-gather.16.cloned.1.call-done.tok_hbm = bf16[2048,2048]{1,0:T(8,128)(2,1)} async-done(((bf16[256,2048]{1,0:T(8,128)(2,1)}), bf16[2048,2048]{1,0:T(8,128)(2,1)}) %all-gather.16.cloned.1.call-update) | async-done | bytes 8388624 | tf_op jit(solution)/shard_map/all_gather | solution.py:683
  591.5 74.4 %shard_map.168 = (bf16[5376,2816]{1,0:T(8,128)(2,1)}, bf16[5376,2048]{1,0:T(8,128)(2,1)}, bf16[5376,2048]{1,0:T(8,128)(2,1)}, f32[5376,128]{1,0:T(8,128)}) custom-call(s32[1117]{0:T(1024)} %concatenate.52.table_ref, s32[5,64,128]{2,1,0:T(8,128)} %fusion.15.pos_ref, bf16[2048,2048]{1,0:T(8,128)(2,1)} %all-gather.16.cloned.1.call-done.tok_hbm, ...), custom_call_target="tpu_custom_call" | custom-call | flops 74999996416 | bytes 150000000 | tf_op jit(solution)/shard_map/pallas_call | solution.py:25
  665.9 14.7 %shard_map.169 = (bf16[2048,2048]{1,0:T(8,128)(2,1)}, f32[2048,128]{1,0:T(8,128)}) custom-call(s32[1117]{0:T(1024)} %concatenate.52.table_ref, s32[5,64,128]{2,1,0:T(8,128)} %fusion.15.pos_ref, bf16[5376,2048]{1,0:T(8,128)(2,1)} %get-tuple-element.93.rows_hbm, f32[5376,128]{1,0:T(8,128)} %get-tuple-element.94.rest_0_), custom_call_target="tpu_custom_call" | custom-call | flops 8999999488 | bytes 35000000 | tf_op jit(solution)/shard_map/pallas_call | solution.py:25
  680.7 19.3 %shard_map.167 = (bf16[3072,2048]{1,0:T(8,128)(2,1)}, f32[3072,128]{1,0:T(8,128)}) custom-call(s32[1117]{0:T(1024)} %concatenate.52.table_ref, s32[5,64,128]{2,1,0:T(8,128)} %fusion.15.pos_ref, bf16[7424,2048]{1,0:T(8,128)(2,1)} %get-tuple-element.87.rows_hbm, f32[7424,128]{1,0:T(8,128)} %get-tuple-element.88.rest_0_), custom_call_target="tpu_custom_call" | custom-call | flops 8999999488 | bytes 35000000 | tf_op jit(solution)/shard_map/pallas_call | solution.py:25
  704.0 110.3 %shard_map.170 = (bf16[7424,2816]{1,0:T(8,128)(2,1)}, bf16[7424,2048]{1,0:T(8,128)(2,1)}, bf16[7424,2048]{1,0:T(8,128)(2,1)}, f32[7424,128]{1,0:T(8,128)}) custom-call(s32[1117]{0:T(1024)} %concatenate.52.table_ref, s32[5,64,128]{2,1,0:T(8,128)} %fusion.15.pos_ref, bf16[3072,2048]{1,0:T(8,128)(2,1)} %all-gather.18.cloned.1.call-done.tok_hbm, ...), custom_call_target="tpu_custom_call" | custom-call | flops 74999996416 | bytes 150000000 | tf_op jit(solution)/shard_map/pallas_call | solution.py:25
  814.4 19.4 %shard_map.171 = (bf16[3072,2048]{1,0:T(8,128)(2,1)}, f32[3072,128]{1,0:T(8,128)}) custom-call(s32[1117]{0:T(1024)} %concatenate.52.table_ref, s32[5,64,128]{2,1,0:T(8,128)} %fusion.15.pos_ref, bf16[7424,2048]{1,0:T(8,128)(2,1)} %get-tuple-element.101.rows_hbm, f32[7424,128]{1,0:T(8,128)} %get-tuple-element.102.rest_0_), custom_call_target="tpu_custom_call" | custom-call | flops 8999999488 | bytes 35000000 | tf_op jit(solution)/shard_map/pallas_call | solution.py:25
  837.7 8.0 reduce-scatter.13.cloned.1.call-done
  846.5 145.9 %shard_map.172 = (bf16[4,2048,1408]{2,1,0:T(8,128)(2,1)}, bf16[4,2048,1408]{2,1,0:T(8,128)(2,1)}, bf16[1,2048,1408]{2,1,0:T(8,128)(2,1)}, bf16[1,2048,1408]{2,1,0:T(8,128)(2,1)}) custom-call(s32[1117]{0:T(1024)} %concatenate.52.table_ref, bf16[7424,2048]{1,0:T(8,128)(2,1)} %get-tuple-element.107.rest_0_, bf16[5376,2048]{1,0:T(8,128)(2,1)} %get-tuple-element.108.rest_1_, ...), custom_call_target="tpu_custom_call" | custom-call | flops 103809024000 | bytes 100000000 | tf_op jit(solution)/shard_map/pallas_call | solution.py:25
  996.3 3.5 convert_element_type.120
  1005.6 3.5 fusion.71
  1009.7 7.8 fusion.6
  1018.1 11.2 multiply_reduce_fusion
  1031.7 9.3 insert.2
  1041.1 75.1 %shard_map.173 = (bf16[4,1408,2048]{2,1,0:T(8,128)(2,1)}, bf16[1,1408,2048]{2,1,0:T(8,128)(2,1)}) custom-call(s32[1117]{0:T(1024)} %concatenate.52.table_ref, bf16[7424,1408]{1,0:T(8,128)(2,1)} %get-tuple-element.83.h_hbm.rest_0_, bf16[5376,1408]{1,0:T(8,128)(2,1)} %get-tuple-element.91.h_hbm.rest_1_, bf16[7424,1408]{1,0:T(8,128)(2,1)} %get-tuple-element.99.h_hbm.rest_2_, ...), custom_call_target="tpu_custom_call" | custom-call | flops 51904512000 | bytes 100000000 | tf_op jit(solution)/shard_map/pallas_call | solution.py:25
  1116.9 42.6 %all-reduce.5.cloned.1.call-done = f32[8,8192]{1,0:T(8,128)} async-done(((f32[8,8192]{1,0:T(8,128)}), f32[8,8192]{1,0:T(8,128)}) %all-reduce.5.cloned.1.call-update) | async-done | bytes 262160 | tf_op jit(solution)/shard_map/psum | solution.py:786
  1166.5 5.9 insert.3
  (235 shorter events, 64.5 us)
Async XLA Ops:
  7.2 81.7 %all-gather.8.cloned.1.call-start = ((), (), s32[]{:S(2)}) async-start(), calls=%async_computation.6 | async-start | bytes 14155776 | tf_op jit(solution)/shard_map/all_gather | solution.py:683
  16.3 200.1 %all-gather.10.cloned.1.call-start = ((), (), s32[]{:S(2)}) async-start(), calls=%async_computation.7 | async-start | bytes 9437184 | tf_op jit(solution)/shard_map/all_gather | solution.py:683
  18.7 197.7 %all-gather.12.cloned.1.call-start = ((), (), s32[]{:S(2)}) async-start(), calls=%async_computation.8 | async-start | bytes 14155776 | tf_op jit(solution)/shard_map/all_gather | solution.py:683
  19.5 289.3 %reduce-scatter.7.cloned.1.call-start = ((), (), s32[]{:S(2)}) async-start(), calls=%async_computation.9 | async-start | bytes 14155776 | tf_op jit(solution)/shard_map/reduce_scatter | solution.py:686
  23.0 19.8 %copy-start.13 = (f32[1024]{0:T(1024)}, f32[1024]{0:T(1024)S(1)}, u32[]{:S(2)}) copy-start(f32[1024]{0:T(1024)S(1)} %get-tuple-element.219) | copy-start | bytes 12292
  42.8 25.7 %copy-start.4 = (f32[128,1024]{1,0:T(8,128)}, f32[128,1024]{1,0:T(8,128)S(1)}, u32[]{:S(2)}) copy-start(f32[128,1024]{1,0:T(8,128)S(1)} %all-gather) | copy-start | bytes 1572868
  55.8 23.5 %collective-permute-start = (bf16[1,2048,1408]{2,1,0:T(8,128)(2,1)}, bf16[1,2048,1408]{2,1,0:T(8,128)(2,1)}, u32[]{:S(2)}, u32[]{:S(2)}) collective-permute-start(bf16[1,2048,1408]{2,1,0:T(8,128)(2,1)} %constant_dynamic-slice_fusion), channel_id=1, source_target_pairs={{0,1},{1,0},{2,3},{3,2},{4,5},{5,4},{6,7},{7,6}} | collective-permute-start | bytes 17301512 | tf_op jit(solution)/shard_map/ppermute | solution.py:721
  61.4 17.9 %collective-permute-start.1 = (bf16[1,2048,1408]{2,1,0:T(8,128)(2,1)}, bf16[1,2048,1408]{2,1,0:T(8,128)(2,1)}, u32[]{:S(2)}, u32[]{:S(2)}) collective-permute-start(bf16[1,2048,1408]{2,1,0:T(8,128)(2,1)} %constant_dynamic-slice_fusion.2), channel_id=1, source_target_pairs={{0,1},{1,0},{2,3},{3,2},{4,5},{5,4},{6,7},{7,6}} | collective-permute-start | bytes 17301512 | tf_op jit(solution)/shard_map/ppermute | solution.py:721
  68.3 8.3 copy-start.24
  68.3 17.4 %collective-permute-start.2 = (bf16[1,1408,2048]{2,1,0:T(8,128)(2,1)}, bf16[1,1408,2048]{2,1,0:T(8,128)(2,1)}, u32[]{:S(2)}, u32[]{:S(2)}) collective-permute-start(bf16[1,1408,2048]{2,1,0:T(8,128)(2,1)} %constant_dynamic-slice_fusion.1), channel_id=1, source_target_pairs={{0,1},{1,0},{2,3},{3,2},{4,5},{5,4},{6,7},{7,6}} | collective-permute-start | bytes 17301512 | tf_op jit(solution)/shard_map/ppermute | solution.py:721
  216.4 224.2 %reduce-scatter.9.cloned.1.call-start = ((), (), s32[]{:S(2)}) async-start(), calls=%async_computation.10 | async-start | bytes 9437184 | tf_op jit(solution)/shard_map/reduce_scatter | solution.py:686
  308.8 144.2 %all-gather.14.cloned.1.call-start = ((), (), s32[]{:S(2)}) async-start(), calls=%async_computation.12 | async-start | bytes 14155776 | tf_op jit(solution)/shard_map/all_gather | solution.py:683
  313.3 250.7 %reduce-scatter.11.cloned.1.call-start = ((), (), s32[]{:S(2)}) async-start(), calls=%async_computation.11 | async-start | bytes 14155776 | tf_op jit(solution)/shard_map/reduce_scatter | solution.py:686
  440.7 150.8 %all-gather.16.cloned.1.call-start = ((), (), s32[]{:S(2)}) async-start(), calls=%async_computation.13 | async-start | bytes 9437184 | tf_op jit(solution)/shard_map/all_gather | solution.py:683
  444.6 255.4 %all-gather.18.cloned.1.call-start = ((), (), s32[]{:S(2)}) async-start(), calls=%async_computation.14 | async-start | bytes 14155776 | tf_op jit(solution)/shard_map/all_gather | solution.py:683
  568.6 269.1 %reduce-scatter.15.cloned.1.call-start = ((), (), s32[]{:S(2)}) async-start(), calls=%async_computation.16 | async-start | bytes 9437184 | tf_op jit(solution)/shard_map/reduce_scatter | solution.py:686
  680.6 165.1 %reduce-scatter.13.cloned.1.call-start = ((), (), s32[]{:S(2)}) async-start(), calls=%async_computation.15 | async-start | bytes 14155776 | tf_op jit(solution)/shard_map/reduce_scatter | solution.py:686
  700.0 303.3 %all-reduce.7.cloned.1.call-start = ((), (), s32[]{:S(2)}) async-start(), calls=%async_computation.19 | async-start | bytes 524288
  845.7 159.2 %reduce-scatter.17.cloned.1.call-start = ((), (), s32[]{:S(2)}) async-start(), calls=%async_computation.17 | async-start | bytes 14155776 | tf_op jit(solution)/shard_map/reduce_scatter | solution.py:686
  846.5 312.9 %all-reduce.5.cloned.1.call-start = ((), (), s32[]{:S(2)}) async-start(), calls=%async_computation.18 | async-start | bytes 524288 | tf_op jit(solution)/shard_map/psum | solution.py:786
  992.4 8.9 copy-start.6
  992.4 39.3 %collective-permute-start.3 = (bf16[1,2048,1408]{2,1,0:T(8,128)(2,1)}, bf16[1,2048,1408]{2,1,0:T(8,128)(2,1)}, u32[]{:S(2)}, u32[]{:S(2)}) collective-permute-start(bf16[1,2048,1408]{2,1,0:T(8,128)(2,1)} %get-tuple-element.121), channel_id=1, source_target_pairs={{0,1},{1,0},{2,3},{3,2},{4,5},{5,4},{6,7},{7,6}} | collective-permute-start | bytes 17301512 | tf_op jit(solution)/shard_map/ppermute | solution.py:760
  992.5 39.3 %collective-permute-start.4 = (bf16[1,2048,1408]{2,1,0:T(8,128)(2,1)}, bf16[1,2048,1408]{2,1,0:T(8,128)(2,1)}, u32[]{:S(2)}, u32[]{:S(2)}) collective-permute-start(bf16[1,2048,1408]{2,1,0:T(8,128)(2,1)} %get-tuple-element.122), channel_id=1, source_target_pairs={{0,1},{1,0},{2,3},{3,2},{4,5},{5,4},{6,7},{7,6}} | collective-permute-start | bytes 17301512 | tf_op jit(solution)/shard_map/ppermute | solution.py:760
  996.3 9.2 copy-start.12
  996.3 9.2 copy-start.14
  996.3 9.2 copy-start.18
  1001.3 8.3 copy-start.16
  1001.3 8.3 copy-start.20
  1001.4 8.3 copy-start.22
  1009.6 7.8 copy-start.2
  1009.7 8.4 copy-start.3
  1116.1 50.3 %collective-permute-start.5 = (bf16[1,1408,2048]{2,1,0:T(8,128)(2,1)}, bf16[1,1408,2048]{2,1,0:T(8,128)(2,1)}, u32[]{:S(2)}, u32[]{:S(2)}) collective-permute-start(bf16[1,1408,2048]{2,1,0:T(8,128)(2,1)} %get-tuple-element.133), channel_id=1, source_target_pairs={{0,1},{1,0},{2,3},{3,2},{4,5},{5,4},{6,7},{7,6}} | collective-permute-start | bytes 17301512 | tf_op jit(solution)/shard_map/ppermute | solution.py:785
  (14 other events, 50.6 us)
Sparse Core Ops, SparseCore 0:
  16.4 72.3 all-gather.7
  90.7 48.6 all-gather.9
  141.8 66.4 all-gather.11
  216.6 83.9 reduce-scatter.6
  308.9 75.2 reduce-scatter.8
  386.5 66.4 all-gather.13
  456.9 83.9 reduce-scatter.10
  542.7 48.6 all-gather.15
  593.3 66.4 all-gather.17
  680.7 76.9 reduce-scatter.14
  761.7 83.9 reduce-scatter.12
  849.2 42.8 all-reduce.6
  895.4 83.3 reduce-scatter.16
  1116.3 43.0 all-reduce.4

commit v2 on v1

--- a/solution.py
+++ b/solution.py
@@ -14,10 +14,10 @@
 TILE = 256
 LANES = 128
 GROUP = 4
+REACH = 96
 PARTS = (384, 256, 384)
 CHUNKS = len(PARTS)
 WINDOWS = (1, 2, 3, 4)
-STATS_SIZE = 65536
 VMEM_LIMIT = 67_043_328
 
 
@@ -42,28 +42,29 @@
 
 
 class Dispatch:
-    def __init__(self, at, table_ref, pos_ref, prob_ref, tok_hbm, scratch):
+    def __init__(self, at, place, table_ref, pos_ref, prob_ref, tok_hbm, scratch):
         self.at, self.table_ref, self.pos_ref, self.prob_ref, self.tok_hbm = at, table_ref, pos_ref, prob_ref, tok_hbm
         self.tok, self.waited, self.sems = scratch
         self.first, self.spans = at["spans"]
-
-    def block_copy(self, index):
-        rows = pl.ds(index * TILE if isinstance(index, int) else pl.multiple_of(index * TILE, TILE), TILE)
-        return pltpu.make_async_copy(self.tok_hbm.at[rows, :], self.tok.at[rows, :], self.sems.at[index])
+        self.offset, self.stride = place
+        self.part = at["part"]
+
+    def span_copy(self, index, row):
+        into = pl.ds(index * LANES if isinstance(index, int) else pl.multiple_of(index * LANES, LANES), LANES)
+        return pltpu.make_async_copy(self.tok_hbm.at[pl.ds(row, LANES), :], self.tok.at[into, :], self.sems.at[index])
 
     def begin(self):
         self.waited[0] = 0
-        for index in range(self.spans * LANES // TILE):
-            self.block_copy(index).start()
+        for index in range(self.spans):
+            device, token = divmod(index * LANES, self.part)
+            self.span_copy(index, device * self.stride + self.offset + token).start()
 
     def await_tokens(self, stop_span):
-        need = (stop_span * LANES + TILE - 1) // TILE
-
-        @pl.loop(self.waited[0], need)
+        @pl.loop(self.waited[0], stop_span)
         def _(index):
-            self.block_copy(index).wait()
-
-        self.waited[0] = jnp.maximum(self.waited[0], need)
+            self.span_copy(index, 0).wait()
+
+        self.waited[0] = jnp.maximum(self.waited[0], stop_span)
 
     def end(self):
         self.await_tokens(self.spans)
@@ -106,8 +107,9 @@
                     window(half, 2 * k, starts[half])
 
 
-def dispatch_scratch(tok):
-    return [pltpu.VMEM(tok.shape, tok.dtype), pltpu.SMEM((1,), jnp.int32), pltpu.SemaphoreType.DMA((tok.shape[0] // TILE,))]
+def dispatch_scratch(at, tok):
+    spans = at["spans"][1]
+    return [pltpu.VMEM((spans * LANES, tok.shape[1]), tok.dtype), pltpu.SMEM((1,), jnp.int32), pltpu.SemaphoreType.DMA((spans,))]
 
 
 def combine_kernel(at, spans, groups, with_gate, table_ref, pos_ref, rows_hbm, *rest):
@@ -117,7 +119,7 @@
         out_ref, rows, waited, sems = rest
     step = pl.program_id(0)
     steps = pl.num_programs(0)
-    row_iota = lax.broadcasted_iota(jnp.int32, (LANES, LANES), 0)
+    row_iota = lax.broadcasted_iota(jnp.int32, (REACH, LANES), 0)
     over = table_ref[at["over"] + step]
 
     def region(g):
@@ -153,7 +155,7 @@
 
     for g in range(groups):
         stop = region(g)[1]
-        need = jnp.minimum((start_of(g, (step + 1) * GROUP - 1) + LANES + over * LANES + TILE - 1) // TILE, stop)
+        need = jnp.minimum((start_of(g, (step + 1) * GROUP - 1) + REACH + over * REACH + TILE - 1) // TILE, stop)
         need = jnp.where(step == steps - 1, stop, need)
 
         @pl.loop(waited[g], need)
@@ -170,16 +172,16 @@
             begin = place = start_of(g, span)
             if second:
                 first, stop = region(g)
-                place = pl.multiple_of(jnp.where(first == stop, begin, jnp.minimum(begin + LANES, stop * TILE - LANES)), 16)
-                begin = begin + LANES
+                place = pl.multiple_of(jnp.where(first == stop, begin, jnp.minimum(begin + REACH, stop * TILE - REACH)), 16)
+                begin = begin + REACH
             row = row_iota + place
             match = pos_ref[g, pl.ds(spans[0] + span, 1), :] == row
             if second:
                 match = jnp.logical_and(match, row >= begin)
             hot.append(jnp.where(match, 1.0, 0.0).astype(jnp.bfloat16))
-            data.append(rows[pl.ds(place, LANES), :])
+            data.append(rows[pl.ds(place, REACH), :])
             if with_gate:
-                gdata.append(gates[pl.ds(place, LANES), :])
+                gdata.append(gates[pl.ds(place, REACH), :])
         hot = jnp.concatenate(hot, axis=0)
         dims = (((0,), (0,)), ((), ()))
         out = lax.dot_general(hot, jnp.concatenate(data, axis=0), dims, preferred_element_type=jnp.float32)
@@ -285,9 +287,9 @@
     )(*piped_in, *piped_out)
 
 
-def forward_kernel(at, table_ref, pos_ref, prob_ref, tok_hbm, *rest):
+def forward_kernel(at, place, table_ref, pos_ref, prob_ref, tok_hbm, *rest):
     stream = WeightStream(at, table_ref, rest[:6], rest[11:14])
-    dispatch = Dispatch(at, table_ref, pos_ref, prob_ref, tok_hbm, rest[14:])
+    dispatch = Dispatch(at, place, table_ref, pos_ref, prob_ref, tok_hbm, rest[14:])
     wide, down, ffn = stream.wide, stream.down, stream.ffn
     dispatch.begin()
     stream.begin()
@@ -295,29 +297,44 @@
     def tile_body(x_ref, gate_ref, ab_ref, h_ref, out_ref):
         dispatch.tile(x_ref, gate_ref)
         slot = stream.slot()
-        x = x_ref[...]
-        for j in range(ffn // LANES):
-            cols = slice(j * LANES, (j + 1) * LANES)
-            ucols = slice(ffn + j * LANES, ffn + (j + 1) * LANES)
-            both = jnp.dot(x, jnp.concatenate([wide[slot, :, cols], wide[slot, :, ucols]], axis=1), preferred_element_type=jnp.float32)
-            a, b = both[:, :LANES], both[:, LANES:]
-            ab_ref[:, cols] = a
-            ab_ref[:, ucols] = b
-            h_ref[:, cols] = (a * jax.nn.sigmoid(a) * b).astype(h_ref.dtype)
-        out = jnp.dot(h_ref[...], down[slot], preferred_element_type=jnp.float32)
-        gate = gate_ref[...]
-        for j in range(out.shape[1] // LANES):
-            cols = slice(j * LANES, (j + 1) * LANES)
-            out_ref[:, cols] = (out[:, cols] * gate).astype(out_ref.dtype)
+
+        def matmuls(height):
+            used = slice(0, height)
+            x = x_ref[used, :]
+            for j in range(ffn // LANES):
+                cols = slice(j * LANES, (j + 1) * LANES)
+                ucols = slice(ffn + j * LANES, ffn + (j + 1) * LANES)
+                both = jnp.dot(x, jnp.concatenate([wide[slot, :, cols], wide[slot, :, ucols]], axis=1), preferred_element_type=jnp.float32)
+                a, b = both[:, :LANES], both[:, LANES:]
+                ab_ref[used, cols] = a
+                ab_ref[used, ucols] = b
+                h_ref[used, cols] = (a * jax.nn.sigmoid(a) * b).astype(h_ref.dtype)
+            out = jnp.dot(h_ref[used, :], down[slot], preferred_element_type=jnp.float32)
+            gate = gate_ref[used, :]
+            for j in range(out.shape[1] // LANES):
+                cols = slice(j * LANES, (j + 1) * LANES)
+                out_ref[used, cols] = (out[:, cols] * gate).astype(out_ref.dtype)
+
+        half = table_ref[at["half"] + pl.program_id(0)] != 0
+
+        @pl.when(jnp.logical_not(half))
+        def _():
+            matmuls(TILE)
+
+        @pl.when(half)
+        def _():
+            matmuls(TILE // 2)
+            for ref in (ab_ref, h_ref, out_ref):
+                ref[TILE // 2:, :] = jnp.zeros((TILE // 2, ref.shape[1]), ref.dtype)
 
     run_tiles(at, table_ref, tile_body, (), rest[6:11])
     dispatch.end()
 
 
-def backward_kernel(at, table_ref, pos_ref, tok_hbm, ab_hbm, h_hbm, gate_hbm, *rest):
+def backward_kernel(at, place, table_ref, pos_ref, tok_hbm, ab_hbm, h_hbm, gate_hbm, *rest):
     stream = WeightStream(at, table_ref, rest[:6], rest[10:13])
     m_ref = rest[13]
-    dispatch = Dispatch(at, table_ref, pos_ref, None, tok_hbm, rest[14:])
+    dispatch = Dispatch(at, place, table_ref, pos_ref, None, tok_hbm, rest[14:])
     wide, down, ffn = stream.wide, stream.down, stream.ffn
     trans = (((1,), (1,)), ((), ()))
     dispatch.begin()
@@ -368,13 +385,14 @@
     return [jax.ShapeDtypeStruct((rows_max, width), dtype) for width, dtype in kinds]
 
 
-def forward(layout, chunk, table, pos, prob, tok, weights):
+def forward(layout, chunk, table, pos, prob, tokens, weights):
     _, dim, ffn = weights[0].shape
     kinds = ((dim, jnp.bfloat16), (LANES, jnp.float32), (2 * ffn, jnp.float32), (ffn, jnp.bfloat16), (dim, jnp.bfloat16))
     at = layout[chunk]
+    tok, place = tokens
     return call(
-        functools.partial(forward_kernel, at), table, (pos, prob, tok, *weights), [WHOLE, WHOLE] + [ANY] * 7,
-        shapes(at["rows_max"], *kinds), [ANY] * 5, weight_scratch(weights[0]) + dispatch_scratch(tok), (75 * 10**9, 150 * 10**6),
+        functools.partial(forward_kernel, at, place), table, (pos, prob, tok, *weights), [WHOLE, WHOLE] + [ANY] * 7,
+        shapes(at["rows_max"], *kinds), [ANY] * 5, weight_scratch(weights[0]) + dispatch_scratch(at, tok), (75 * 10**9, 150 * 10**6),
     )
 
 
@@ -382,9 +400,9 @@
     _, dim, ffn = weights[0].shape
     kinds = ((2 * ffn, jnp.bfloat16), (dim, jnp.bfloat16), (dim, jnp.bfloat16), (LANES, jnp.float32))
     at = layout[chunk]
-    scratch = [*weight_scratch(weights[0]), pltpu.VMEM((TILE, dim), jnp.bfloat16), *dispatch_scratch(tok)]
+    scratch = [*weight_scratch(weights[0]), pltpu.VMEM((TILE, dim), jnp.bfloat16), *dispatch_scratch(at, tok)]
     return call(
-        functools.partial(backward_kernel, at), table, (pos, tok, ab, hidden, gates, *weights), [WHOLE] + [ANY] * 10,
+        functools.partial(backward_kernel, at, (0, at["part"])), table, (pos, tok, ab, hidden, gates, *weights), [WHOLE] + [ANY] * 10,
         shapes(at["rows_max"], *kinds), [ANY] * 4, scratch, (75 * 10**9, 150 * 10**6),
     )
 
@@ -537,6 +555,110 @@
     )(table, *back, *grads)
 
 
+def row_blocks(height, dim):
+    specs, first = [], 0
+    for part in PARTS:
+        blocks = part // height
+        specs.append(pl.BlockSpec((height, dim), lambda t, *_, first=first, last=blocks - 1: (jnp.clip(t - first, 0, last), 0)))
+        first += blocks
+    return specs
+
+
+def of_this_chunk(height, refs):
+    step, first, value = pl.program_id(0), 0, None
+    for part, ref in zip(PARTS, refs):
+        value = ref[...] if value is None else jnp.where(step >= first, ref[...], value)
+        first += part // height
+    return value
+
+
+def norm_kernel(x_ref, gain_ref, head_ref, tail_ref):
+    step = pl.program_id(0)
+    x = x_ref[...].astype(jnp.float32)
+    inv_rms = lax.rsqrt(jnp.mean(x * x, axis=-1, keepdims=True) + NORM_EPS)
+    x_norm = (x * inv_rms * gain_ref[...]).astype(jnp.bfloat16)
+    head = PARTS[0] // x.shape[0]
+
+    @pl.when(step < head)
+    def _():
+        head_ref[...] = x_norm
+
+    @pl.when(step >= head)
+    def _():
+        tail_ref[...] = x_norm
+
+
+def normalize(x, gain):
+    tokens, dim = x.shape
+    height, head = LANES, PARTS[0] // LANES
+    return pl.pallas_call(
+        norm_kernel,
+        grid=(tokens // height,),
+        in_specs=[pl.BlockSpec((height, dim), lambda t: (t, 0)), pl.BlockSpec((1, dim), lambda t: (0, 0))],
+        out_specs=[
+            pl.BlockSpec((height, dim), lambda t: (jnp.minimum(t, head - 1), 0)),
+            pl.BlockSpec((height, dim), lambda t: (jnp.maximum(t - head, 0), 0)),
+        ],
+        out_shape=[jax.ShapeDtypeStruct((n, dim), jnp.bfloat16) for n in (PARTS[0], tokens - PARTS[0])],
+        cost_estimate=pl.CostEstimate(flops=10**7, bytes_accessed=8 * 10**6, transcendentals=0),
+        name="normalize",
+    )(x, gain.reshape(1, dim))
+
+
+def finish_kernel(x_ref, y_grad_ref, logit_ref, gain_ref, router_ref, *rest):
+    in_refs, out_refs, (y_ref, x_grad_ref, stats_ref) = rest[:CHUNKS], rest[CHUNKS:2 * CHUNKS], rest[2 * CHUNKS:]
+    height = x_ref.shape[0]
+    x = x_ref[...].astype(jnp.float32)
+    inv_rms = lax.rsqrt(jnp.mean(x * x, axis=-1, keepdims=True) + NORM_EPS)
+    unit = x * inv_rms
+    gain = gain_ref[...]
+    moe_out = of_this_chunk(height, out_refs).astype(jnp.float32)
+    y_ref[...] = (x + moe_out).astype(y_ref.dtype)
+    logit_grad = logit_ref[...]
+    routed = lax.dot_general(logit_grad, router_ref[...], (((1,), (1,)), ((), ())), preferred_element_type=jnp.float32)
+    x_norm_grad = of_this_chunk(height, in_refs).astype(jnp.float32) + routed
+    unit_grad = x_norm_grad * gain
+    x_grad = y_grad_ref[...].astype(jnp.float32) + inv_rms * (unit_grad - unit * jnp.mean(unit_grad * unit, axis=-1, keepdims=True))
+    x_grad_ref[...] = x_grad.astype(x_grad_ref.dtype)
+    x_norm = (unit * gain).astype(jnp.bfloat16)
+    by_expert = lax.dot_general(logit_grad, x_norm, (((0,), (0,)), ((), ())), preferred_element_type=jnp.float32)
+
+    @pl.when(pl.program_id(0) == 0)
+    def _():
+        stats_ref[...] = jnp.zeros_like(stats_ref)
+
+    def folded(values):
+        return jnp.sum(values.reshape(height // 8, 8, values.shape[1]), axis=0)
+
+    stats_ref[0:8, :] += by_expert[0:8, :]
+    stats_ref[8:16, :] += folded(x_norm_grad * unit)
+    stats_ref[16:24, :] += folded(moe_out * moe_out)
+
+
+def finish(x, y_grad, logit_grad, gain, w_router, in_raw, out_raw):
+    tokens, dim = x.shape
+    height = LANES
+    rows = pl.BlockSpec((height, dim), lambda t: (t, 0))
+    wide = jnp.pad(logit_grad, ((0, 0), (0, LANES - logit_grad.shape[1])))
+    router = jnp.pad(w_router, ((0, 0), (0, LANES - w_router.shape[1])))
+    return pl.pallas_call(
+        finish_kernel,
+        grid=(tokens // height,),
+        in_specs=[
+            rows, rows, pl.BlockSpec((height, LANES), lambda t: (t, 0)), pl.BlockSpec((1, dim), lambda t: (0, 0)),
+            pl.BlockSpec((dim, LANES), lambda t: (0, 0)), *row_blocks(height, dim), *row_blocks(height, dim),
+        ],
+        out_specs=[rows, rows, pl.BlockSpec((32, dim), lambda t: (0, 0))],
+        out_shape=[
+            jax.ShapeDtypeStruct((tokens, dim), jnp.bfloat16), jax.ShapeDtypeStruct((tokens, dim), jnp.bfloat16),
+            jax.ShapeDtypeStruct((32, dim), jnp.float32),
+        ],
+        compiler_params=pltpu.CompilerParams(vmem_limit_bytes=VMEM_LIMIT),
+        cost_estimate=pl.CostEstimate(flops=10**9, bytes_accessed=25 * 10**6, transcendentals=0),
+        name="finish",
+    )(x, y_grad, wide, gain.reshape(1, dim), router, *in_raw, *out_raw)
+
+
 def below(size, strict):
     i = lax.broadcasted_iota(jnp.int32, (size, size), 0)
     j = lax.broadcasted_iota(jnp.int32, (size, size), 1)
@@ -601,6 +723,8 @@
     follow = jnp.where(follow == groups, -1, follow)
     fresh = jnp.sum(jnp.where(mine, begin[:, None, :], 0), axis=2) == tile
     slot = jnp.sum(jnp.where(mine, ordinal[:, None, :], 0), axis=2) % 2
+    rows_left = jnp.sum(jnp.where(mine, (total + begin * TILE)[:, None, :], 0), axis=2) - tile * TILE
+    half = rows_left <= TILE // 2
 
     half_mine = jnp.repeat(mine, 2, axis=1)
     stops = jnp.sum(jnp.where(half_mine[..., None], span_stop[None, None], 0), axis=2)
@@ -609,11 +733,11 @@
     lo = count(jnp.logical_and(inside, stops <= row0), 2)
     hi = jnp.minimum(count(jnp.logical_and(inside, stops < row0 + LANES), 2), jnp.array(spans_of, jnp.int32)[:, None] - 1)
     width = jnp.maximum(jnp.max(((hi - lo + 2) // 2).reshape(CHUNKS, tiles_max, 2), axis=2), 1)
-    start = jnp.minimum(span_first // 16 * 16, to_spans(stop) * TILE - LANES)
+    start = jnp.minimum(span_first // 16 * 16, to_spans(stop) * TILE - REACH)
     empty = to_spans(tiles) == 0
     leading = jnp.logical_and(jnp.logical_not(empty), to_spans(ordinal) == 0)
     start = jnp.where(empty, jnp.sum(jnp.where(leading, start, 0), axis=0), start)
-    over = jnp.any(jnp.logical_and(jnp.logical_not(empty), span_stop - start > LANES), axis=0)
+    over = jnp.any(jnp.logical_and(jnp.logical_not(empty), span_stop - start > REACH), axis=0)
     over = jnp.any(over.reshape(-1, GROUP), axis=1)
 
     in_chunks = running(tiles.T)
@@ -637,7 +761,7 @@
 
     sections = (
         ("expert", experts_of), ("insert", place.reshape(1)), ("steps", step_stop[-1:]), ("owner", owner), ("src", src),
-        ("count", stop[:, -1:]), ("group", group), ("slot", slot), ("fresh", fresh), ("next", follow), ("lo", lo), ("width", width),
+        ("count", stop[:, -1:]), ("group", group), ("slot", slot), ("fresh", fresh), ("half", half), ("next", follow), ("lo", lo), ("width", width),
         ("first", jnp.concatenate([jnp.zeros((CHUNKS, 1), jnp.int32), stop], axis=1)), ("start", start), ("over", over),
     )
     table = jnp.concatenate([values.reshape(-1).astype(jnp.int32) for _, values in sections])
@@ -647,9 +771,9 @@
         at += values.size
     layout = {}
     for c in range(CHUNKS):
-        layout[c] = {name: places[name] + c * (sizes_of[name] // CHUNKS) for name in ("count", "group", "slot", "fresh", "next", "lo", "width", "first")}
+        layout[c] = {name: places[name] + c * (sizes_of[name] // CHUNKS) for name in ("count", "group", "slot", "fresh", "half", "next", "lo", "width", "first")}
         layout[c] |= {
-            "expert": places["expert"], "spans": (firsts[c], spans_of[c]), "rows_max": tiles_of[c] * TILE,
+            "expert": places["expert"], "spans": (firsts[c], spans_of[c]), "part": PARTS[c], "rows_max": tiles_of[c] * TILE,
             "start": [places["start"] + g * span_total + firsts[c] for g in range(groups)],
             "over": places["over"] + firsts[c] // GROUP,
         }
@@ -688,13 +812,13 @@
         def after(values, first):
             return lax.optimization_barrier((values, first))
 
-        x_float = x.astype(jnp.float32)
-        inv_rms = lax.rsqrt(jnp.mean(x_float * x_float, axis=-1, keepdims=True) + NORM_EPS)
-        unit = x_float * inv_rms
         gain = norm_gain.astype(jnp.float32)
-        x_norm = (unit * gain).astype(jnp.bfloat16)
-        tok = [gather(of_chunk(x_norm, c)) for c in range(CHUNKS)]
-
+        head, tail = normalize(x, gain)
+        rest = tokens - PARTS[0]
+        gathered = [gather(head), gather(tail)]
+        tok = [(gathered[0], (0, PARTS[0]))] + [(gathered[1], (firsts[c] - PARTS[0], rest)) for c in range(1, CHUNKS)]
+
+        x_norm = jnp.concatenate([head, tail], axis=0)
         route_prob = jax.nn.softmax(jnp.dot(x_norm, w_router, preferred_element_type=jnp.float32), axis=-1)
         expert_range = jnp.arange(num_experts, dtype=jnp.int32)
         choice = jnp.sum((expert_ids[:, :, None] == expert_range[None, None, :]).astype(jnp.float32), axis=1)
@@ -727,8 +851,8 @@
 
         def send_cotangent(c, gate):
             raw, (gate, _) = after(out_raw[c], (gate, m_own[-1:]))
-            moe_out.append(raw.astype(jnp.float32))
-            moe_grad = of_chunk(y_grad, c).astype(jnp.float32) + grad_scale * moe_out[c]
+            moe_out.append(raw)
+            moe_grad = of_chunk(y_grad, c).astype(jnp.float32) + grad_scale * raw.astype(jnp.float32)
             m_own.append(moe_grad.astype(jnp.bfloat16))
             m_tok.append(gather(m_own[c]))
             return gate
@@ -737,7 +861,8 @@
             rows, gates, ab, h, out_rows = forward(layout, c, table, pos, prob, tok[c], weights)
             (partial,) = combine(layout, c, table, pos, out_rows)
             if c == 0:
-                partial, tok[1:] = after(partial, tok[1:])
+                partial, later = after(partial, gathered[1])
+                tok[1:] = [(later, place) for _, place in tok[1:]]
             else:
                 partial = send_cotangent(c - 1, partial)
             out_raw.append(scatter(partial))
@@ -751,6 +876,7 @@
                 in_rows = send_cotangent(CHUNKS - 1, in_rows)
             partial, gate_tok = combine(layout, c, table, pos, in_rows, dgate)
             if c == 0:
+                m_tok[1], partial = after(m_tok[1], partial)
                 partial, m_tok[-1] = after(partial, m_tok[-1])
             in_raw.append(scatter(partial))
             gate_part.append(gate_tok[:, :num_experts])
@@ -760,34 +886,20 @@
         back = [lax.ppermute(g, "ep", swap) for g in (helped_gate, helped_up)]
 
         sums = jnp.concatenate([g.reshape(dev_count, -1) for g in gate_part], axis=1)
-        sums, _ = after(sums, in_raw[:CHUNKS - 1])
-        gate_weight_grad = lax.psum_scatter(sums, rows_axes, scatter_dimension=0, tiled=False)
+        gate_weight_grad = lax.psum(sums, ("tp", "ep"))
+        gate_weight_grad = lax.dynamic_index_in_dim(gate_weight_grad, my_ep * tp_size + lax.axis_index("tp"), axis=0, keepdims=False)
         gate_weight_grad, (wide_grads, in_raw) = after(gate_weight_grad, (wide_grads, in_raw))
-        moe_all = jnp.concatenate(moe_out, axis=0)
-        y = (x_float + moe_all).astype(jnp.bfloat16)
         prob_grad = gate_weight_grad.reshape(tokens, num_experts) + balance_scale * counts[None, :]
         logit_grad = (route_prob * (prob_grad - jnp.sum(route_prob * prob_grad, axis=-1, keepdims=True))).astype(jnp.bfloat16)
-        x_norm_grad = jnp.concatenate(in_raw, axis=0).astype(jnp.float32)
-        x_norm_grad = x_norm_grad + jnp.einsum("se,de->sd", logit_grad, w_router, preferred_element_type=jnp.float32)
-        unit_grad = x_norm_grad * gain
-        x_grad = y_grad.astype(jnp.float32) + inv_rms * (unit_grad - unit * jnp.mean(unit_grad * unit, axis=-1, keepdims=True))
-        x_grad = x_grad.astype(jnp.bfloat16)
-        stats = (
-            jnp.sum(x_norm_grad * unit, axis=0),
-            jnp.einsum("sd,se->de", x_norm, logit_grad, preferred_element_type=jnp.float32).reshape(-1),
-            jnp.sum(moe_all * moe_all).reshape(1),
-        )
-        size = sum(s.size for s in stats)
-        stats = jnp.concatenate([*stats, jnp.zeros((STATS_SIZE - size,), jnp.float32)]).reshape(dev_count, -1)
+        y, x_grad, stats = finish(x, y_grad, logit_grad, gain, w_router, in_raw, moe_out)
         gate_grad, up_grad = insert(layout, table, back, wide_grads)
         stats, (mg_rows[0], x_grad, gate_grad) = after(stats, (mg_rows[0], x_grad, gate_grad))
         down_grad, helped_down = weight_grad(layout, table, hidden, mg_rows, local_experts, 1)
         (down_grad,) = insert(layout, table, [lax.ppermute(helped_down, "ep", swap)], [down_grad])
         stats = lax.psum(stats, ("tp", "ep"))
-        stats = stats.reshape(-1)
-        gain_sum = stats[:model_dim]
-        router_sum = stats[model_dim:size - 1].reshape(model_dim, num_experts)
-        act_loss = ACT_COEF * stats[size - 1] / (total_tokens * model_dim)
+        router_sum = stats[:num_experts].T
+        gain_sum = jnp.sum(stats[8:16], axis=0)
+        act_loss = ACT_COEF * jnp.sum(stats[16:24]) / (total_tokens * model_dim)
         return (y, x_grad, gain_sum.astype(jnp.bfloat16), router_sum.astype(jnp.bfloat16), gate_grad, up_grad, down_grad, balance_loss, act_loss)
 
     return jax.shard_map(body, mesh=mesh, in_specs=(row_spec, row_spec, row_spec, P(), P(), wide_spec, wide_spec, down_spec), out_specs=(row_spec, row_spec, P(), P(), wide_spec, wide_spec, down_spec, P(), P()), check_vma=False)

time: 1190 us -> 1250 us (1.050)
  waiting for transfers between devices: 93.1 us -> 206 us
  other arithmetic: 46.3 us -> 29.2 us
    reduce_scatter x6, waiting for transfers between devices: 8.13 us -> 134 us  [scatter(): return lax.psum_scatter(rows, rows_axes, scatter_dimension=0, tiled=True)]
    pallas_call x14, Pallas kernels: 917 us -> 883 us  [call(): pl.pallas_call(kernel, grid_spec=pltpu.PrefetchScalarGridSpec(num_scalar_...]
    pallas_call x0 -> x2, Pallas kernels: none -> 22 us  [the longest x1 14.5 us: finish(): pl.pallas_call(finish_kernel, grid=(tokens // height,), in_specs=[rows, r...]
    all_gather x6 -> x5, waiting for transfers between devices: 34.4 us -> 20.9 us  [gather(): return lax.all_gather(rows, rows_axes, axis=0, tiled=True)]
  transfers between devices with their start and end apart: 20 -> 19, of which waited for: 6 -> 7; matrix products, arithmetic and copies ran while one was open for 8% -> 5% of each run, Pallas kernels for 71% -> 56%
where the time goes in v2:
time: 1250 us; the launch traced here: 1240 us
  Pallas kernels  920 us (74%)
  waiting for transfers between devices  206 us (16%)
  local copies, waits for them, and re-layouts  39.5 us (3%)
  other arithmetic  29.2 us (2%)
  between operations  21.8 us (2%)
  blocking collectives  18.9 us (2%)
    pallas_call x14, Pallas kernels, call(): pl.pallas_call(kernel, grid_spec=pltpu.PrefetchScalarGridSpec(num_scalar_...  883 us
    reduce_scatter x6, waiting for transfers between devices, scatter(): return lax.psum_scatter(rows, rows_axes, scatter_dimension=0, tiled=True)  134 us
    psum x1, waiting for transfers between devices, body(): stats = lax.psum(stats, ('tp', 'ep'))  42.5 us
  transfers between devices with their start and end apart: 19, of which 7 were waited for; matrix products, arithmetic and copies ran while one was open for 5% of the time, Pallas kernels for 56%

profile of v2, /device:TPU:0, one launch (start us, length us, event | category | flops | bytes accessed | tf_op | source)
XLA Modules:
  0.0 1241.8 jit_solution(9494081485270384557)
XLA Ops:
  8.5 7.5 normalize.1
  16.9 3.4 fusion.61
  22.0 18.9 %all-gather = f32[128,1024]{1,0:T(8,128)S(1)} all-gather(f32[16,1024]{1,0:T(8,128)S(1)} %maximum_bitcast_fusion.1), channel_id=2, replica_groups=mesh['tp'=4,'ep'=2] {'ep','tp'}, dimensions={0}, use_global_device_ids=true | all-gather | bytes 589824 | tf_op jit(solution)/shard_map/all_gather | solution.py:825
  47.4 6.3 constant_dynamic-slice_fusion.2
  53.7 5.6 constant_dynamic-slice_fusion.1
  59.8 6.2 constant_dynamic-slice_fusion
  77.9 5.9 collective-permute-done.2.rest_5_
  83.8 4.8 all-gather.7.cloned.1.call-done.tok_hbm
  88.6 104.6 %shard_map.160 = (bf16[7424,2048]{1,0:T(8,128)(2,1)}, f32[7424,128]{1,0:T(8,128)}, f32[7424,2816]{1,0:T(8,128)}, bf16[7424,1408]{1,0:T(8,128)(2,1)}, bf16[7424,2048]{1,0:T(8,128)(2,1)}) custom-call(s32[1204]{0:T(1024)} %concatenate.47.table_ref, s32[5,64,128]{2,1,0:T(8,128)} %fusion.6.pos_ref, f32[5,64,128]{2,1,0:T(8,128)} %get-tuple-element.182.prob_ref, ...), custom_call_target="tpu_custom_call" | custom-call | flops 74999996416 | bytes 150000000 | tf_op jit(solution)/shard_map/pallas_call | solution.py:25
  193.2 14.5 %shard_map.161 = bf16[3072,2048]{1,0:T(8,128)(2,1)} custom-call(s32[1204]{0:T(1024)} %concatenate.47.table_ref, s32[5,64,128]{2,1,0:T(8,128)} %fusion.6.pos_ref, bf16[7424,2048]{1,0:T(8,128)(2,1)} %get-tuple-element.79.rows_hbm), custom_call_target="tpu_custom_call" | custom-call | flops 8999999488 | bytes 35000000 | tf_op jit(solution)/shard_map/pallas_call | solution.py:25
  207.9 74.8 %shard_map.162 = (bf16[5376,2048]{1,0:T(8,128)(2,1)}, f32[5376,128]{1,0:T(8,128)}, f32[5376,2816]{1,0:T(8,128)}, bf16[5376,1408]{1,0:T(8,128)(2,1)}, bf16[5376,2048]{1,0:T(8,128)(2,1)}) custom-call(s32[1204]{0:T(1024)} %concatenate.47.table_ref, s32[5,64,128]{2,1,0:T(8,128)} %fusion.6.pos_ref, f32[5,64,128]{2,1,0:T(8,128)} %get-tuple-element.182.prob_ref, ...), custom_call_target="tpu_custom_call" | custom-call | flops 74999996416 | bytes 150000000 | tf_op jit(solution)/shard_map/pallas_call | solution.py:25
  282.6 11.6 shard_map.163
  295.6 3.1 add_convert_fusion.1
  298.9 105.0 %shard_map.164 = (bf16[7424,2048]{1,0:T(8,128)(2,1)}, f32[7424,128]{1,0:T(8,128)}, f32[7424,2816]{1,0:T(8,128)}, bf16[7424,1408]{1,0:T(8,128)(2,1)}, bf16[7424,2048]{1,0:T(8,128)(2,1)}) custom-call(s32[1204]{0:T(1024)} %concatenate.47.table_ref, s32[5,64,128]{2,1,0:T(8,128)} %fusion.6.pos_ref, f32[5,64,128]{2,1,0:T(8,128)} %get-tuple-element.182.prob_ref, ...), custom_call_target="tpu_custom_call" | custom-call | flops 74999996416 | bytes 150000000 | tf_op jit(solution)/shard_map/pallas_call | solution.py:25
  403.8 14.5 %shard_map.165 = bf16[3072,2048]{1,0:T(8,128)(2,1)} custom-call(s32[1204]{0:T(1024)} %concatenate.47.table_ref, s32[5,64,128]{2,1,0:T(8,128)} %fusion.6.pos_ref, bf16[7424,2048]{1,0:T(8,128)(2,1)} %get-tuple-element.84.rows_hbm), custom_call_target="tpu_custom_call" | custom-call | flops 8999999488 | bytes 35000000 | tf_op jit(solution)/shard_map/pallas_call | solution.py:25
  422.3 12.2 all-gather.11.cloned.1.call-done.tok_hbm
  434.5 111.2 %shard_map.166 = (bf16[7424,2816]{1,0:T(8,128)(2,1)}, bf16[7424,2048]{1,0:T(8,128)(2,1)}, bf16[7424,2048]{1,0:T(8,128)(2,1)}, f32[7424,128]{1,0:T(8,128)}) custom-call(s32[1204]{0:T(1024)} %concatenate.47.table_ref, s32[5,64,128]{2,1,0:T(8,128)} %fusion.6.pos_ref, bf16[3072,2048]{1,0:T(8,128)(2,1)} %all-gather.11.cloned.1.call-done.tok_hbm, ...), custom_call_target="tpu_custom_call" | custom-call | flops 74999996416 | bytes 150000000 | tf_op jit(solution)/shard_map/pallas_call | solution.py:25
  545.7 4.6 add_convert_fusion
  550.4 15.7 %shard_map.167 = (bf16[3072,2048]{1,0:T(8,128)(2,1)}, f32[3072,128]{1,0:T(8,128)}) custom-call(s32[1204]{0:T(1024)} %concatenate.47.table_ref, s32[5,64,128]{2,1,0:T(8,128)} %fusion.6.pos_ref, bf16[7424,2048]{1,0:T(8,128)(2,1)} %get-tuple-element.92.rows_hbm, f32[7424,128]{1,0:T(8,128)} %get-tuple-element.93.rest_0_), custom_call_target="tpu_custom_call" | custom-call | flops 8999999488 | bytes 35000000 | tf_op jit(solution)/shard_map/pallas_call | solution.py:25
  569.0 3.9 all-gather.13.cloned.1.call-done.tok_hbm
  572.9 74.5 %shard_map.168 = (bf16[5376,2816]{1,0:T(8,128)(2,1)}, bf16[5376,2048]{1,0:T(8,128)(2,1)}, bf16[5376,2048]{1,0:T(8,128)(2,1)}, f32[5376,128]{1,0:T(8,128)}) custom-call(s32[1204]{0:T(1024)} %concatenate.47.table_ref, s32[5,64,128]{2,1,0:T(8,128)} %fusion.6.pos_ref, bf16[2048,2048]{1,0:T(8,128)(2,1)} %all-gather.13.cloned.1.call-done.tok_hbm, ...), custom_call_target="tpu_custom_call" | custom-call | flops 74999996416 | bytes 150000000 | tf_op jit(solution)/shard_map/pallas_call | solution.py:25
  647.4 12.3 shard_map.169
  662.1 107.1 %shard_map.170 = (bf16[7424,2816]{1,0:T(8,128)(2,1)}, bf16[7424,2048]{1,0:T(8,128)(2,1)}, bf16[7424,2048]{1,0:T(8,128)(2,1)}, f32[7424,128]{1,0:T(8,128)}) custom-call(s32[1204]{0:T(1024)} %concatenate.47.table_ref, s32[5,64,128]{2,1,0:T(8,128)} %fusion.6.pos_ref, bf16[3072,2048]{1,0:T(8,128)(2,1)} %all-gather.15.cloned.1.call-done.tok_hbm, ...), custom_call_target="tpu_custom_call" | custom-call | flops 74999996416 | bytes 150000000 | tf_op jit(solution)/shard_map/pallas_call | solution.py:25
  769.3 15.7 %shard_map.171 = (bf16[3072,2048]{1,0:T(8,128)(2,1)}, f32[3072,128]{1,0:T(8,128)}) custom-call(s32[1204]{0:T(1024)} %concatenate.47.table_ref, s32[5,64,128]{2,1,0:T(8,128)} %fusion.6.pos_ref, bf16[7424,2048]{1,0:T(8,128)(2,1)} %get-tuple-element.109.rows_hbm, f32[7424,128]{1,0:T(8,128)} %get-tuple-element.110.rest_0_), custom_call_target="tpu_custom_call" | custom-call | flops 8999999488 | bytes 35000000 | tf_op jit(solution)/shard_map/pallas_call | solution.py:25
  790.9 146.1 %shard_map.172 = (bf16[4,2048,1408]{2,1,0:T(8,128)(2,1)}, bf16[4,2048,1408]{2,1,0:T(8,128)(2,1)}, bf16[1,2048,1408]{2,1,0:T(8,128)(2,1)}, bf16[1,2048,1408]{2,1,0:T(8,128)(2,1)}) custom-call(s32[1204]{0:T(1024)} %concatenate.47.table_ref, bf16[7424,2048]{1,0:T(8,128)(2,1)} %get-tuple-element.112.rest_0_, bf16[5376,2048]{1,0:T(8,128)(2,1)} %get-tuple-element.113.rest_1_, ...), custom_call_target="tpu_custom_call" | custom-call | flops 103809024000 | bytes 100000000 | tf_op jit(solution)/shard_map/pallas_call | solution.py:25
  942.5 46.8 %reduce-scatter.13.cloned.1.call-done.rest_0_ = bf16[384,2048]{1,0:T(8,128)(2,1)} async-done(((bf16[3072,2048]{1,0:T(8,128)(2,1)}), bf16[384,2048]{1,0:T(8,128)(2,1)}) %reduce-scatter.13.cloned.1.call-update) | async-done | bytes 1572880 | tf_op jit(solution)/shard_map/reduce_scatter | solution.py:810
  989.3 87.3 %reduce-scatter.17.cloned.1.call-done.rest_2_ = bf16[384,2048]{1,0:T(8,128)(2,1)} async-done(((bf16[3072,2048]{1,0:T(8,128)(2,1)}), bf16[384,2048]{1,0:T(8,128)(2,1)}) %reduce-scatter.17.cloned.1.call-update) | async-done | bytes 1572880 | tf_op jit(solution)/shard_map/reduce_scatter | solution.py:810
  1080.7 14.5 %finish.1 = (bf16[1024,2048]{1,0:T(8,128)(2,1)}, bf16[1024,2048]{1,0:T(8,128)(2,1)}, f32[32,2048]{1,0:T(8,128)}) custom-call(bf16[1024,2048]{1,0:T(8,128)(2,1)} %x_ref.3, bf16[1024,2048]{1,0:T(8,128)(2,1)} %y_grad_ref.1, bf16[1024,128]{1,0:T(8,128)(2,1)} %pad.9.logit_ref, f32[1,2048]{1,0:T(1,128)} %bitcast.86, bf16[2048,128]{1,0:T(8,128)(2,1)} %pad.10.router_ref, ...), custom_call_target="tpu_custom_call" | custom-call | flops 1000000000 | bytes 25000000 | tf_op jit(solution)/shard_map/finish/pallas_call | solution.py:644
  1095.3 9.3 insert.2
  1104.6 75.1 %shard_map.173 = (bf16[4,1408,2048]{2,1,0:T(8,128)(2,1)}, bf16[1,1408,2048]{2,1,0:T(8,128)(2,1)}) custom-call(s32[1204]{0:T(1024)} %concatenate.47.table_ref, bf16[7424,1408]{1,0:T(8,128)(2,1)} %get-tuple-element.88.h_hbm.rest_0_, bf16[5376,1408]{1,0:T(8,128)(2,1)} %get-tuple-element.98.h_hbm.rest_1_, bf16[7424,1408]{1,0:T(8,128)(2,1)} %get-tuple-element.107.h_hbm.rest_2_, ...), custom_call_target="tpu_custom_call" | custom-call | flops 51904512000 | bytes 100000000 | tf_op jit(solution)/shard_map/pallas_call | solution.py:25
  1180.4 42.5 %all-reduce.8.cloned.1.call-done = f32[32,2048]{1,0:T(8,128)} async-done(((f32[32,2048]{1,0:T(8,128)}), f32[32,2048]{1,0:T(8,128)}) %all-reduce.8.cloned.1.call-update) | async-done | bytes 262160 | tf_op jit(solution)/shard_map/psum | solution.py:899
  1226.6 5.9 insert.3
  (189 shorter events, 48.6 us)
Async XLA Ops:
  7.2 9.7 copy-start.6
  7.2 81.4 %all-gather.7.cloned.1.call-start = ((), (), s32[]{:S(2)}) async-start(), calls=%async_computation.6 | async-start | bytes 14155776 | tf_op jit(solution)/shard_map/all_gather | solution.py:807
  16.0 191.7 %all-gather.9.cloned.1.call-start = ((), (), s32[]{:S(2)}) async-start(), calls=%async_computation.7 | async-start | bytes 23592960 | tf_op jit(solution)/shard_map/all_gather | solution.py:807
  16.8 277.4 %reduce-scatter.7.cloned.1.call-start = ((), (), s32[]{:S(2)}) async-start(), calls=%async_computation.8 | async-start | bytes 14155776 | tf_op jit(solution)/shard_map/reduce_scatter | solution.py:810
  16.9 5.1 copy-start.7
  20.3 0.6 copy-start.4
  20.5 33.2 %copy-start = (f32[1024,8]{1,0:T(8,128)}, f32[1024,8]{1,0:T(8,128)S(1)}, u32[]{:S(2)}) copy-start(f32[1024,8]{1,0:T(8,128)S(1)} %copy.99) | copy-start | bytes 98308
  20.9 0.6 copy-start.5
  40.9 25.3 %copy-start.1 = (f32[128,1024]{1,0:T(8,128)}, f32[128,1024]{1,0:T(8,128)S(1)}, u32[]{:S(2)}) copy-start(f32[128,1024]{1,0:T(8,128)S(1)} %all-gather) | copy-start | bytes 1572868
  53.7 24.2 %collective-permute-start = (bf16[1,2048,1408]{2,1,0:T(8,128)(2,1)}, bf16[1,2048,1408]{2,1,0:T(8,128)(2,1)}, u32[]{:S(2)}, u32[]{:S(2)}) collective-permute-start(bf16[1,2048,1408]{2,1,0:T(8,128)(2,1)} %constant_dynamic-slice_fusion.2), channel_id=1, source_target_pairs={{0,1},{1,0},{2,3},{3,2},{4,5},{5,4},{6,7},{7,6}} | collective-permute-start | bytes 17301512 | tf_op jit(solution)/shard_map/ppermute | solution.py:845
  59.3 7.7 copy-start.9
  59.3 18.6 %collective-permute-start.1 = (bf16[1,2048,1408]{2,1,0:T(8,128)(2,1)}, bf16[1,2048,1408]{2,1,0:T(8,128)(2,1)}, u32[]{:S(2)}, u32[]{:S(2)}) collective-permute-start(bf16[1,2048,1408]{2,1,0:T(8,128)(2,1)} %constant_dynamic-slice_fusion.1), channel_id=1, source_target_pairs={{0,1},{1,0},{2,3},{3,2},{4,5},{5,4},{6,7},{7,6}} | collective-permute-start | bytes 17301512 | tf_op jit(solution)/shard_map/ppermute | solution.py:845
  66.0 9.2 copy-start.8
  66.0 17.8 %collective-permute-start.2 = (bf16[1,1408,2048]{2,1,0:T(8,128)(2,1)}, bf16[1,1408,2048]{2,1,0:T(8,128)(2,1)}, u32[]{:S(2)}, u32[]{:S(2)}) collective-permute-start(bf16[1,1408,2048]{2,1,0:T(8,128)(2,1)} %constant_dynamic-slice_fusion), channel_id=1, source_target_pairs={{0,1},{1,0},{2,3},{3,2},{4,5},{5,4},{6,7},{7,6}} | collective-permute-start | bytes 17301512 | tf_op jit(solution)/shard_map/ppermute | solution.py:845
  207.8 210.5 %reduce-scatter.9.cloned.1.call-start = ((), (), s32[]{:S(2)}) async-start(), calls=%async_computation.9 | async-start | bytes 9437184 | tf_op jit(solution)/shard_map/reduce_scatter | solution.py:810
  294.2 1.4 copy-start.2
  294.3 140.2 %all-gather.11.cloned.1.call-start = ((), (), s32[]{:S(2)}) async-start(), calls=%async_computation.11 | async-start | bytes 14155776 | tf_op jit(solution)/shard_map/all_gather | solution.py:807
  298.8 246.8 %reduce-scatter.11.cloned.1.call-start = ((), (), s32[]{:S(2)}) async-start(), calls=%async_computation.10 | async-start | bytes 14155776 | tf_op jit(solution)/shard_map/reduce_scatter | solution.py:810
  418.3 1.2 copy-start.3
  418.4 154.5 %all-gather.13.cloned.1.call-start = ((), (), s32[]{:S(2)}) async-start(), calls=%async_computation.12 | async-start | bytes 9437184 | tf_op jit(solution)/shard_map/all_gather | solution.py:807
  422.2 239.9 %all-gather.15.cloned.1.call-start = ((), (), s32[]{:S(2)}) async-start(), calls=%async_computation.13 | async-start | bytes 14155776 | tf_op jit(solution)/shard_map/all_gather | solution.py:807
  550.3 391.2 %all-reduce.6.cloned.1.call-start = ((), (), s32[]{:S(2)}) async-start(), calls=%async_computation.14 | async-start | bytes 524288 | tf_op jit(solution)/shard_map/psum | solution.py:889
  788.9 153.6 %reduce-scatter.15.cloned.1.call-start = ((), (), s32[]{:S(2)}) async-start(), calls=%async_computation.16 | async-start | bytes 9437184 | tf_op jit(solution)/shard_map/reduce_scatter | solution.py:810
  789.5 199.8 %reduce-scatter.13.cloned.1.call-start = ((), (), s32[]{:S(2)}) async-start(), calls=%async_computation.15 | async-start | bytes 14155776 | tf_op jit(solution)/shard_map/reduce_scatter | solution.py:810
  790.2 286.4 %reduce-scatter.17.cloned.1.call-start = ((), (), s32[]{:S(2)}) async-start(), calls=%async_computation.17 | async-start | bytes 14155776 | tf_op jit(solution)/shard_map/reduce_scatter | solution.py:810
  790.8 432.1 %all-reduce.8.cloned.1.call-start = ((), (), s32[]{:S(2)}) async-start(), calls=%async_computation.18 | async-start | bytes 524288 | tf_op jit(solution)/shard_map/psum | solution.py:899
  936.9 158.3 %collective-permute-start.3 = (bf16[1,2048,1408]{2,1,0:T(8,128)(2,1)}, bf16[1,2048,1408]{2,1,0:T(8,128)(2,1)}, u32[]{:S(2)}, u32[]{:S(2)}) collective-permute-start(bf16[1,2048,1408]{2,1,0:T(8,128)(2,1)} %get-tuple-element.131), channel_id=1, source_target_pairs={{0,1},{1,0},{2,3},{3,2},{4,5},{5,4},{6,7},{7,6}} | collective-permute-start | bytes 17301512 | tf_op jit(solution)/shard_map/ppermute | solution.py:886
  937.7 157.6 %collective-permute-start.4 = (bf16[1,2048,1408]{2,1,0:T(8,128)(2,1)}, bf16[1,2048,1408]{2,1,0:T(8,128)(2,1)}, u32[]{:S(2)}, u32[]{:S(2)}) collective-permute-start(bf16[1,2048,1408]{2,1,0:T(8,128)(2,1)} %get-tuple-element.132), channel_id=1, source_target_pairs={{0,1},{1,0},{2,3},{3,2},{4,5},{5,4},{6,7},{7,6}} | collective-permute-start | bytes 17301512 | tf_op jit(solution)/shard_map/ppermute | solution.py:886
  1179.7 46.9 %collective-permute-start.5 = (bf16[1,1408,2048]{2,1,0:T(8,128)(2,1)}, bf16[1,1408,2048]{2,1,0:T(8,128)(2,1)}, u32[]{:S(2)}, u32[]{:S(2)}) collective-permute-start(bf16[1,1408,2048]{2,1,0:T(8,128)(2,1)} %get-tuple-element.143), channel_id=1, source_target_pairs={{0,1},{1,0},{2,3},{3,2},{4,5},{5,4},{6,7},{7,6}} | collective-permute-start | bytes 17301512 | tf_op jit(solution)/shard_map/ppermute | solution.py:898
Sparse Core Ops, SparseCore 0:
  16.2 72.3 all-gather.6
  91.0 101.8 all-gather.8
  207.9 83.8 reduce-scatter.6
  295.1 70.6 reduce-scatter.8
  368.0 66.4 all-gather.10
  438.3 83.9 reduce-scatter.10
  524.2 48.6 all-gather.12
  574.7 66.4 all-gather.14
  789.0 47.0 all-reduce.5
  839.3 62.4 reduce-scatter.14
  905.3 83.9 reduce-scatter.12
  992.6 83.9 reduce-scatter.16
  1179.9 42.9 all-reduce.7

commit v3 on v2

--- a/solution.py
+++ b/solution.py
@@ -53,9 +53,11 @@
         into = pl.ds(index * LANES if isinstance(index, int) else pl.multiple_of(index * LANES, LANES), LANES)
         return pltpu.make_async_copy(self.tok_hbm.at[pl.ds(row, LANES), :], self.tok.at[into, :], self.sems.at[index])
 
-    def begin(self):
+    def begin(self, stream):
         self.waited[0] = 0
         for index in range(self.spans):
+            if index == 2 * WINDOWS[-1]:
+                stream.begin()
             device, token = divmod(index * LANES, self.part)
             self.span_copy(index, device * self.stride + self.offset + token).start()
 
@@ -291,8 +293,7 @@
     stream = WeightStream(at, table_ref, rest[:6], rest[11:14])
     dispatch = Dispatch(at, place, table_ref, pos_ref, prob_ref, tok_hbm, rest[14:])
     wide, down, ffn = stream.wide, stream.down, stream.ffn
-    dispatch.begin()
-    stream.begin()
+    dispatch.begin(stream)
 
     def tile_body(x_ref, gate_ref, ab_ref, h_ref, out_ref):
         dispatch.tile(x_ref, gate_ref)
@@ -337,8 +338,7 @@
     dispatch = Dispatch(at, place, table_ref, pos_ref, None, tok_hbm, rest[14:])
     wide, down, ffn = stream.wide, stream.down, stream.ffn
     trans = (((1,), (1,)), ((), ()))
-    dispatch.begin()
-    stream.begin()
+    dispatch.begin(stream)
 
     def tile_body(ab_ref, h_ref, gate_ref, d_ref, in_ref, mg_ref, dgate_ref):
         dispatch.tile(m_ref)
@@ -407,10 +407,10 @@
     )
 
 
-def weight_grad_kernel(at, tiles_max, outs, table_ref, *rest):
-    lhs_hbm, rhs_hbm = rest[:CHUNKS], rest[CHUNKS:2 * CHUNKS]
-    own_out, helped_out = rest[2 * CHUNKS:2 * CHUNKS + outs], rest[2 * CHUNKS + outs:2 * CHUNKS + 2 * outs]
-    lhs, rhs, lhs_t, acc, staged, pending, sems, out_sems = rest[2 * CHUNKS + 2 * outs:]
+def weight_grad_kernel(at, tiles_max, outs, carried, table_ref, *rest):
+    lhs_hbm, rhs_hbm, back, rest = rest[:CHUNKS], rest[CHUNKS:2 * CHUNKS], rest[2 * CHUNKS:2 * CHUNKS + carried], rest[2 * CHUNKS + 2 * carried:]
+    own_out, helped_out, filled, rest = rest[:outs], rest[outs:2 * outs], rest[2 * outs:2 * outs + carried], rest[2 * outs + carried:]
+    lhs, rhs, lhs_t, acc, staged, pending, sems, out_sems = rest[:8]
     experts = own_out[0].shape[0]
     steps = table_ref[at["steps"]]
 
@@ -445,6 +445,17 @@
     pending[0] = 0
     start(0, 0)
 
+    place = table_ref[at["insert"]]
+    if carried:
+        bounce, fetch_sems, store_sems = rest[8:]
+        fetch = [pltpu.make_async_copy(back[i].at[0], bounce.at[i], fetch_sems.at[i]) for i in range(carried)]
+        store = [pltpu.make_async_copy(bounce.at[i], filled[i].at[jnp.maximum(place, 0)], store_sems.at[i]) for i in range(carried)]
+
+        @pl.when(place >= 0)
+        def _():
+            for copy in fetch:
+                copy.start()
+
     def accumulate(slot, fresh, depth):
         lhs_t[:, :depth] = jnp.transpose(lhs[slot, :depth, :], (1, 0))
         block = 2 * LANES
@@ -461,6 +472,13 @@
         def _():
             start(step + 1, 1 - slot)
 
+        if carried:
+            @pl.when(jnp.logical_and(place >= 0, step == steps // 2))
+            def _():
+                for one, other in zip(fetch, store):
+                    one.wait()
+                    other.start()
+
         fresh = jnp.logical_or(step == 0, group != table_ref[at["owner"] + jnp.maximum(step - 1, 0)])
         last = jnp.logical_or(step == steps - 1, group != table_ref[at["owner"] + step + 1])
         pair = table_ref[at["src"] + 2 * step + 1] >= 0
@@ -497,12 +515,17 @@
             pending[0] = 1
 
     drain()
-
-
-def weight_grad(layout, table, lhs, rhs, experts, outs):
+    if carried:
+        @pl.when(place >= 0)
+        def _():
+            for copy in store:
+                copy.wait()
+
+
+def weight_grad(layout, table, lhs, rhs, experts, outs, back=(), grads=()):
     left, right = lhs[0].shape[1], rhs[0].shape[1]
     width = right // outs
-    kernel = functools.partial(weight_grad_kernel, layout["grad"], layout["tiles_max"], outs)
+    carried = len(grads)
     scratch = [
         pltpu.VMEM((2, 2 * TILE, left), jnp.bfloat16),
         pltpu.VMEM((2, 2 * TILE, right), jnp.bfloat16),
@@ -513,11 +536,22 @@
         pltpu.SemaphoreType.DMA((2, 2, 2)),
         pltpu.SemaphoreType.DMA((outs,)),
     ]
+    if carried:
+        scratch += [pltpu.VMEM((carried, *grads[0].shape[1:]), jnp.bfloat16), pltpu.SemaphoreType.DMA((carried,)), pltpu.SemaphoreType.DMA((carried,))]
     out_shape = [jax.ShapeDtypeStruct((n, left, width), jnp.bfloat16) for n in [experts] * outs + [1] * outs]
-    return call(
-        kernel, table, (*lhs, *rhs), [ANY] * (2 * CHUNKS), out_shape, [ANY] * len(out_shape),
-        scratch, (2 * 9000 * left * right, 100 * 10**6),
-    )
+    out_shape += [jax.ShapeDtypeStruct(g.shape, g.dtype) for g in grads]
+    operands = (*lhs, *rhs, *back, *grads)
+    return pl.pallas_call(
+        functools.partial(weight_grad_kernel, layout["grad"], layout["tiles_max"], outs, carried),
+        grid_spec=pltpu.PrefetchScalarGridSpec(
+            num_scalar_prefetch=1, in_specs=[ANY] * len(operands), out_specs=[ANY] * len(out_shape), scratch_shapes=scratch
+        ),
+        out_shape=out_shape,
+        input_output_aliases={1 + 2 * CHUNKS + carried + i: 2 * outs + i for i in range(carried)},
+        compiler_params=pltpu.CompilerParams(vmem_limit_bytes=VMEM_LIMIT),
+        cost_estimate=pl.CostEstimate(flops=2 * 9000 * left * right, bytes_accessed=100 * 10**6, transcendentals=0),
+        name="weight_grad",
+    )(table, *operands)
 
 
 def insert_kernel(at, size, table_ref, *rest):
@@ -572,35 +606,22 @@
     return value
 
 
-def norm_kernel(x_ref, gain_ref, head_ref, tail_ref):
-    step = pl.program_id(0)
+def norm_kernel(x_ref, gain_ref, out_ref):
     x = x_ref[...].astype(jnp.float32)
     inv_rms = lax.rsqrt(jnp.mean(x * x, axis=-1, keepdims=True) + NORM_EPS)
-    x_norm = (x * inv_rms * gain_ref[...]).astype(jnp.bfloat16)
-    head = PARTS[0] // x.shape[0]
-
-    @pl.when(step < head)
-    def _():
-        head_ref[...] = x_norm
-
-    @pl.when(step >= head)
-    def _():
-        tail_ref[...] = x_norm
-
-
-def normalize(x, gain):
-    tokens, dim = x.shape
-    height, head = LANES, PARTS[0] // LANES
+    out_ref[...] = (x * inv_rms * gain_ref[...]).astype(out_ref.dtype)
+
+
+def normalize(x, gain, first, count):
+    dim = x.shape[1]
+    height = LANES
     return pl.pallas_call(
         norm_kernel,
-        grid=(tokens // height,),
-        in_specs=[pl.BlockSpec((height, dim), lambda t: (t, 0)), pl.BlockSpec((1, dim), lambda t: (0, 0))],
-        out_specs=[
-            pl.BlockSpec((height, dim), lambda t: (jnp.minimum(t, head - 1), 0)),
-            pl.BlockSpec((height, dim), lambda t: (jnp.maximum(t - head, 0), 0)),
-        ],
-        out_shape=[jax.ShapeDtypeStruct((n, dim), jnp.bfloat16) for n in (PARTS[0], tokens - PARTS[0])],
-        cost_estimate=pl.CostEstimate(flops=10**7, bytes_accessed=8 * 10**6, transcendentals=0),
+        grid=(count // height,),
+        in_specs=[pl.BlockSpec((height, dim), lambda t: (t + first // height, 0)), pl.BlockSpec((1, dim), lambda t: (0, 0))],
+        out_specs=pl.BlockSpec((height, dim), lambda t: (t, 0)),
+        out_shape=jax.ShapeDtypeStruct((count, dim), jnp.bfloat16),
+        cost_estimate=pl.CostEstimate(flops=10**7, bytes_accessed=4 * 10**6, transcendentals=0),
         name="normalize",
     )(x, gain.reshape(1, dim))
 
@@ -676,13 +697,16 @@
     return jnp.sum(condition.astype(jnp.int32), axis=axis)
 
 
-def choose_swap(tiles, experts):
-    none = jnp.zeros((1,), jnp.int32)
-    options = [jnp.concatenate([none, tiles[:experts]]), jnp.concatenate([none, tiles[experts:]])]
-    gap = jnp.sum(tiles[:experts]) - jnp.sum(tiles[experts:])
-    left = jnp.abs(gap - 2 * options[0][:, None] + 2 * options[1][None, :])
-    index = lax.broadcasted_iota(jnp.int32, left.shape, 0) * (experts + 1) + lax.broadcasted_iota(jnp.int32, left.shape, 1)
-    best = jnp.min(jnp.where(left == jnp.min(left), index, left.size))
+def choose_swap(rows, experts):
+    work = 4 * ((rows + TILE - 1) // TILE) + (rows + TILE // 2 - 1) // (TILE // 2)
+    none = jnp.zeros((rows.shape[0], 1), jnp.int32)
+    sides = [work[:, :experts], work[:, experts:]]
+    options = [jnp.concatenate([none, side], axis=1) for side in sides]
+    moved = options[1][:, None, :] - options[0][:, :, None]
+    loads = [jnp.sum(side, axis=1)[:, None, None] for side in sides]
+    cost = jnp.sum(jnp.maximum(loads[0] + moved, loads[1] - moved), axis=0)
+    index = lax.broadcasted_iota(jnp.int32, cost.shape, 0) * (experts + 1) + lax.broadcasted_iota(jnp.int32, cost.shape, 1)
+    best = jnp.min(jnp.where(cost == jnp.min(cost), index, cost.size))
     return best // (experts + 1) - 1, best % (experts + 1) - 1
 
 
@@ -777,7 +801,7 @@
             "start": [places["start"] + g * span_total + firsts[c] for g in range(groups)],
             "over": places["over"] + firsts[c] // GROUP,
         }
-    layout |= {"grad": {name: places[name] for name in ("steps", "owner", "src")}, "insert": places["insert"], "tiles_max": tiles_max}
+    layout |= {"grad": {name: places[name] for name in ("steps", "owner", "src", "insert")}, "insert": places["insert"], "tiles_max": tiles_max}
     return pos, table, layout
 
 
@@ -813,8 +837,8 @@
             return lax.optimization_barrier((values, first))
 
         gain = norm_gain.astype(jnp.float32)
-        head, tail = normalize(x, gain)
         rest = tokens - PARTS[0]
+        head, tail = normalize(x, gain, 0, PARTS[0]), normalize(x, gain, PARTS[0], rest)
         gathered = [gather(head), gather(tail)]
         tok = [(gathered[0], (0, PARTS[0]))] + [(gathered[1], (firsts[c] - PARTS[0], rest)) for c in range(1, CHUNKS)]
 
@@ -828,8 +852,7 @@
         balance_loss = balance_scale * jnp.sum(counts * jnp.sum(small[:, num_experts:], axis=(0, 2)))
 
         rows_in = jnp.stack([jnp.sum(of_chunk(small[:, :num_experts], c, 2), axis=(0, 2)) for c in range(CHUNKS)])
-        tiles_in = jnp.sum((rows_in.astype(jnp.int32) + TILE - 1) // TILE, axis=0)
-        gives = choose_swap(tiles_in, local_experts)
+        gives = choose_swap(rows_in.astype(jnp.int32), local_experts)
         given = jnp.where(my_ep == 0, gives[0], gives[1])
         taken = jnp.where(my_ep == 0, gives[1], gives[0])
         my_base = my_ep * local_experts
@@ -877,7 +900,6 @@
             partial, gate_tok = combine(layout, c, table, pos, in_rows, dgate)
             if c == 0:
                 m_tok[1], partial = after(m_tok[1], partial)
-                partial, m_tok[-1] = after(partial, m_tok[-1])
             in_raw.append(scatter(partial))
             gate_part.append(gate_tok[:, :num_experts])
             d_rows.append(d)
@@ -892,9 +914,8 @@
         prob_grad = gate_weight_grad.reshape(tokens, num_experts) + balance_scale * counts[None, :]
         logit_grad = (route_prob * (prob_grad - jnp.sum(route_prob * prob_grad, axis=-1, keepdims=True))).astype(jnp.bfloat16)
         y, x_grad, stats = finish(x, y_grad, logit_grad, gain, w_router, in_raw, moe_out)
-        gate_grad, up_grad = insert(layout, table, back, wide_grads)
-        stats, (mg_rows[0], x_grad, gate_grad) = after(stats, (mg_rows[0], x_grad, gate_grad))
-        down_grad, helped_down = weight_grad(layout, table, hidden, mg_rows, local_experts, 1)
+        stats, (mg_rows[0], x_grad, back) = after(stats, (mg_rows[0], x_grad, back))
+        down_grad, helped_down, gate_grad, up_grad = weight_grad(layout, table, hidden, mg_rows, local_experts, 1, back, wide_grads)
         (down_grad,) = insert(layout, table, [lax.ppermute(helped_down, "ep", swap)], [down_grad])
         stats = lax.psum(stats, ("tp", "ep"))
         router_sum = stats[:num_experts].T

time: 1250 us -> 1260 us (level)
  Pallas kernels: 920 us -> 876 us
  starting transfers between devices: 2.06 us -> 32.6 us
  waiting for transfers between devices: 206 us -> 228 us
    pallas_call x14 -> x12, Pallas kernels: 883 us -> 631 us  [call(): pl.pallas_call(kernel, grid_spec=pltpu.PrefetchScalarGridSpec(num_scalar_...]
    pallas_call x1 -> x4, Pallas kernels: 7.49 us -> 225 us  [the longest x2 216 us: weight_grad(): pl.pallas_call(functools.partial(weight_grad_kernel, layout['grad'], layo...]
    ppermute x2, starting transfers between devices: 0.8 us -> 27.3 us  [body(): back = [lax.ppermute(g, 'ep', swap) for g in (helped_gate, helped_up)]]
    all_gather x5, waiting for transfers between devices: 20.9 us -> 40.2 us  [gather(): return lax.all_gather(rows, rows_axes, axis=0, tiled=True)]
  transfers between devices with their start and end apart: 19 -> 19, of which waited for: 7 -> 8; matrix products, arithmetic and copies ran while one was open for 5% -> 5% of each run, Pallas kernels for 56% -> 55%
where the time goes in v3:
time: 1260 us; the launch traced here: 1250 us
  Pallas kernels  876 us (70%)
  waiting for transfers between devices  228 us (18%)
  local copies, waits for them, and re-layouts  40.4 us (3%)
  starting transfers between devices  32.6 us (3%)
  other arithmetic  27.6 us (2%)
  between operations  20.5 us (2%)
  blocking collectives  18.9 us (1%)
    pallas_call x12, Pallas kernels, call(): pl.pallas_call(kernel, grid_spec=pltpu.PrefetchScalarGridSpec(num_scalar_...  631 us
    pallas_call x2, Pallas kernels, weight_grad(): pl.pallas_call(functools.partial(weight_grad_kernel, layout['grad'], layo...  216 us
    reduce_scatter x6, waiting for transfers between devices, scatter(): return lax.psum_scatter(rows, rows_axes, scatter_dimension=0, tiled=True)  138 us
    psum x1, waiting for transfers between devices, body(): stats = lax.psum(stats, ('tp', 'ep'))  42.3 us
    all_gather x5, waiting for transfers between devices, gather(): return lax.all_gather(rows, rows_axes, axis=0, tiled=True)  40.2 us
    ppermute x2, starting transfers between devices, body(): back = [lax.ppermute(g, 'ep', swap) for g in (helped_gate, helped_up)]  27.3 us
  transfers between devices with their start and end apart: 19, of which 8 were waited for; matrix products, arithmetic and copies ran while one was open for 5% of the time, Pallas kernels for 55%

profile of v3, /device:TPU:0, one launch (start us, length us, event | category | flops | bytes accessed | tf_op | source)
XLA Modules:
  0.0 1248.4 jit_solution(6708597123310022739)
XLA Ops:
  8.5 3.7 normalize.2
  12.3 5.3 normalize.3
  22.8 18.9 %all-gather = f32[128,1024]{1,0:T(8,128)S(1)} all-gather(f32[16,1024]{1,0:T(8,128)S(1)} %maximum_bitcast_fusion.1), channel_id=2, replica_groups=mesh['tp'=4,'ep'=2] {'ep','tp'}, dimensions={0}, use_global_device_ids=true | all-gather | bytes 589824 | tf_op jit(solution)/shard_map/all_gather | solution.py:849
  46.5 7.1 constant_dynamic-slice_fusion
  53.6 5.7 constant_dynamic-slice_fusion.2
  59.7 6.2 constant_dynamic-slice_fusion.3
  77.7 5.6 collective-permute-done.2.rest_5_
  84.8 99.6 %shard_map.160 = (bf16[7424,2048]{1,0:T(8,128)(2,1)}, f32[7424,128]{1,0:T(8,128)}, f32[7424,2816]{1,0:T(8,128)}, bf16[7424,1408]{1,0:T(8,128)(2,1)}, bf16[7424,2048]{1,0:T(8,128)(2,1)}) custom-call(s32[1204]{0:T(1024)} %concatenate.39.table_ref, s32[5,64,128]{2,1,0:T(8,128)} %fusion.6.pos_ref, f32[5,64,128]{2,1,0:T(8,128)} %get-tuple-element.176.prob_ref, ...), custom_call_target="tpu_custom_call" | custom-call | flops 74999996416 | bytes 150000000 | tf_op jit(solution)/shard_map/pallas_call | solution.py:25
  184.4 14.5 %shard_map.161 = bf16[3072,2048]{1,0:T(8,128)(2,1)} custom-call(s32[1204]{0:T(1024)} %concatenate.39.table_ref, s32[5,64,128]{2,1,0:T(8,128)} %fusion.6.pos_ref, bf16[7424,2048]{1,0:T(8,128)(2,1)} %get-tuple-element.74.rows_hbm), custom_call_target="tpu_custom_call" | custom-call | flops 8999999488 | bytes 35000000 | tf_op jit(solution)/shard_map/pallas_call | solution.py:25
  199.0 73.5 %shard_map.162 = (bf16[5376,2048]{1,0:T(8,128)(2,1)}, f32[5376,128]{1,0:T(8,128)}, f32[5376,2816]{1,0:T(8,128)}, bf16[5376,1408]{1,0:T(8,128)(2,1)}, bf16[5376,2048]{1,0:T(8,128)(2,1)}) custom-call(s32[1204]{0:T(1024)} %concatenate.39.table_ref, s32[5,64,128]{2,1,0:T(8,128)} %fusion.6.pos_ref, f32[5,64,128]{2,1,0:T(8,128)} %get-tuple-element.176.prob_ref, ...), custom_call_target="tpu_custom_call" | custom-call | flops 74999996416 | bytes 150000000 | tf_op jit(solution)/shard_map/pallas_call | solution.py:25
  272.5 11.3 shard_map.163
  283.8 10.0 reduce-scatter.7.cloned.1.call-done.rest_3_
  298.4 93.7 %shard_map.164 = (bf16[7424,2048]{1,0:T(8,128)(2,1)}, f32[7424,128]{1,0:T(8,128)}, f32[7424,2816]{1,0:T(8,128)}, bf16[7424,1408]{1,0:T(8,128)(2,1)}, bf16[7424,2048]{1,0:T(8,128)(2,1)}) custom-call(s32[1204]{0:T(1024)} %concatenate.39.table_ref, s32[5,64,128]{2,1,0:T(8,128)} %fusion.6.pos_ref, f32[5,64,128]{2,1,0:T(8,128)} %get-tuple-element.176.prob_ref, ...), custom_call_target="tpu_custom_call" | custom-call | flops 74999996416 | bytes 150000000 | tf_op jit(solution)/shard_map/pallas_call | solution.py:25
  392.1 14.2 %shard_map.165 = bf16[3072,2048]{1,0:T(8,128)(2,1)} custom-call(s32[1204]{0:T(1024)} %concatenate.39.table_ref, s32[5,64,128]{2,1,0:T(8,128)} %fusion.6.pos_ref, bf16[7424,2048]{1,0:T(8,128)(2,1)} %get-tuple-element.79.rows_hbm), custom_call_target="tpu_custom_call" | custom-call | flops 8999999488 | bytes 35000000 | tf_op jit(solution)/shard_map/pallas_call | solution.py:25
  410.3 28.0 %all-gather.11.cloned.1.call-done.tok_hbm = bf16[3072,2048]{1,0:T(8,128)(2,1)} async-done(((bf16[384,2048]{1,0:T(8,128)(2,1)}), bf16[3072,2048]{1,0:T(8,128)(2,1)}) %all-gather.11.cloned.1.call-update) | async-done | bytes 12582928 | tf_op jit(solution)/shard_map/all_gather | solution.py:831
  438.3 104.3 %shard_map.166 = (bf16[7424,2816]{1,0:T(8,128)(2,1)}, bf16[7424,2048]{1,0:T(8,128)(2,1)}, bf16[7424,2048]{1,0:T(8,128)(2,1)}, f32[7424,128]{1,0:T(8,128)}) custom-call(s32[1204]{0:T(1024)} %concatenate.39.table_ref, s32[5,64,128]{2,1,0:T(8,128)} %fusion.6.pos_ref, bf16[3072,2048]{1,0:T(8,128)(2,1)} %all-gather.11.cloned.1.call-done.tok_hbm, ...), custom_call_target="tpu_custom_call" | custom-call | flops 74999996416 | bytes 150000000 | tf_op jit(solution)/shard_map/pallas_call | solution.py:25
  542.7 3.7 add_convert_fusion
  546.4 16.9 %shard_map.167 = (bf16[3072,2048]{1,0:T(8,128)(2,1)}, f32[3072,128]{1,0:T(8,128)}) custom-call(s32[1204]{0:T(1024)} %concatenate.39.table_ref, s32[5,64,128]{2,1,0:T(8,128)} %fusion.6.pos_ref, bf16[7424,2048]{1,0:T(8,128)(2,1)} %get-tuple-element.87.rows_hbm, f32[7424,128]{1,0:T(8,128)} %get-tuple-element.88.rest_0_), custom_call_target="tpu_custom_call" | custom-call | flops 8999999488 | bytes 35000000 | tf_op jit(solution)/shard_map/pallas_call | solution.py:25
  566.1 10.6 all-gather.13.cloned.1.call-done.tok_hbm
  576.7 81.0 %shard_map.168 = (bf16[5376,2816]{1,0:T(8,128)(2,1)}, bf16[5376,2048]{1,0:T(8,128)(2,1)}, bf16[5376,2048]{1,0:T(8,128)(2,1)}, f32[5376,128]{1,0:T(8,128)}) custom-call(s32[1204]{0:T(1024)} %concatenate.39.table_ref, s32[5,64,128]{2,1,0:T(8,128)} %fusion.6.pos_ref, bf16[2048,2048]{1,0:T(8,128)(2,1)} %all-gather.13.cloned.1.call-done.tok_hbm, ...), custom_call_target="tpu_custom_call" | custom-call | flops 74999996416 | bytes 150000000 | tf_op jit(solution)/shard_map/pallas_call | solution.py:25
  657.7 12.0 shard_map.169
  672.0 94.4 %shard_map.170 = (bf16[7424,2816]{1,0:T(8,128)(2,1)}, bf16[7424,2048]{1,0:T(8,128)(2,1)}, bf16[7424,2048]{1,0:T(8,128)(2,1)}, f32[7424,128]{1,0:T(8,128)}) custom-call(s32[1204]{0:T(1024)} %concatenate.39.table_ref, s32[5,64,128]{2,1,0:T(8,128)} %fusion.6.pos_ref, bf16[3072,2048]{1,0:T(8,128)(2,1)} %all-gather.15.cloned.1.call-done.tok_hbm, ...), custom_call_target="tpu_custom_call" | custom-call | flops 74999996416 | bytes 150000000 | tf_op jit(solution)/shard_map/pallas_call | solution.py:25
  766.4 15.3 %shard_map.171 = (bf16[3072,2048]{1,0:T(8,128)(2,1)}, f32[3072,128]{1,0:T(8,128)}) custom-call(s32[1204]{0:T(1024)} %concatenate.39.table_ref, s32[5,64,128]{2,1,0:T(8,128)} %fusion.6.pos_ref, bf16[7424,2048]{1,0:T(8,128)(2,1)} %get-tuple-element.102.rows_hbm, f32[7424,128]{1,0:T(8,128)} %get-tuple-element.103.rest_0_), custom_call_target="tpu_custom_call" | custom-call | flops 8999999488 | bytes 35000000 | tf_op jit(solution)/shard_map/pallas_call | solution.py:25
  787.6 142.0 %weight_grad.2 = (bf16[4,2048,1408]{2,1,0:T(8,128)(2,1)}, bf16[4,2048,1408]{2,1,0:T(8,128)(2,1)}, bf16[1,2048,1408]{2,1,0:T(8,128)(2,1)}, bf16[1,2048,1408]{2,1,0:T(8,128)(2,1)}) custom-call(s32[1204]{0:T(1024)} %concatenate.39.table_ref, bf16[7424,2048]{1,0:T(8,128)(2,1)} %get-tuple-element.105.rest_0_, bf16[5376,2048]{1,0:T(8,128)(2,1)} %get-tuple-element.106.rest_1_, ...), custom_call_target="tpu_custom_call" | custom-call | flops 103809024000 | bytes 100000000 | tf_op jit(solution)/shard_map/weight_grad/pallas_call | solution.py:544
  929.6 27.2 %collective-permute-start.3 = (bf16[1,2048,1408]{2,1,0:T(8,128)(2,1)}, bf16[1,2048,1408]{2,1,0:T(8,128)(2,1)}, u32[]{:S(2)}, u32[]{:S(2)}) collective-permute-start(bf16[1,2048,1408]{2,1,0:T(8,128)(2,1)} %get-tuple-element.124), channel_id=1, source_target_pairs={{0,1},{1,0},{2,3},{3,2},{4,5},{5,4},{6,7},{7,6}} | collective-permute-start | bytes 17301512 | tf_op jit(solution)/shard_map/ppermute | solution.py:908
  961.6 40.2 %reduce-scatter.13.cloned.1.call-done.rest_0_ = bf16[384,2048]{1,0:T(8,128)(2,1)} async-done(((bf16[3072,2048]{1,0:T(8,128)(2,1)}), bf16[384,2048]{1,0:T(8,128)(2,1)}) %reduce-scatter.13.cloned.1.call-update) | async-done | bytes 1572880 | tf_op jit(solution)/shard_map/reduce_scatter | solution.py:834
  1001.8 87.3 %reduce-scatter.17.cloned.1.call-done.rest_2_ = bf16[384,2048]{1,0:T(8,128)(2,1)} async-done(((bf16[3072,2048]{1,0:T(8,128)(2,1)}), bf16[384,2048]{1,0:T(8,128)(2,1)}) %reduce-scatter.17.cloned.1.call-update) | async-done | bytes 1572880 | tf_op jit(solution)/shard_map/reduce_scatter | solution.py:834
  1093.2 14.5 %finish.1 = (bf16[1024,2048]{1,0:T(8,128)(2,1)}, bf16[1024,2048]{1,0:T(8,128)(2,1)}, f32[32,2048]{1,0:T(8,128)}) custom-call(bf16[1024,2048]{1,0:T(8,128)(2,1)} %x_ref.5, bf16[1024,2048]{1,0:T(8,128)(2,1)} %y_grad_ref.1, bf16[1024,128]{1,0:T(8,128)(2,1)} %pad.11.logit_ref, f32[1,2048]{1,0:T(1,128)} %bitcast.84, bf16[2048,128]{1,0:T(8,128)(2,1)} %pad.12.router_ref, ...), custom_call_target="tpu_custom_call" | custom-call | flops 1000000000 | bytes 25000000 | tf_op jit(solution)/shard_map/finish/pallas_call | solution.py:665
  1107.8 74.4 %weight_grad.3 = (bf16[4,1408,2048]{2,1,0:T(8,128)(2,1)}, bf16[1,1408,2048]{2,1,0:T(8,128)(2,1)}, bf16[4,2048,1408]{2,1,0:T(8,128)(2,1)}, bf16[4,2048,1408]{2,1,0:T(8,128)(2,1)}) custom-call(s32[1204]{0:T(1024)} %concatenate.39.table_ref, bf16[7424,1408]{1,0:T(8,128)(2,1)} %get-tuple-element.83.h_hbm.rest_0_, ...), custom_call_target="tpu_custom_call", output_to_operand_aliasing={{2}: (9, {}), {3}: (10, {})} | custom-call | flops 51904512000 | bytes 100000000 | tf_op jit(solution)/shard_map/weight_grad/pallas_call | solution.py:544
  1182.2 4.3 collective-permute-start.5
  1187.2 42.3 %all-reduce.10.cloned.1.call-done = f32[32,2048]{1,0:T(8,128)} async-done(((f32[32,2048]{1,0:T(8,128)}), f32[32,2048]{1,0:T(8,128)}) %all-reduce.10.cloned.1.call-update) | async-done | bytes 262160 | tf_op jit(solution)/shard_map/psum | solution.py:920
  1233.2 5.9 insert.1
  (193 shorter events, 54.4 us)
Async XLA Ops:
  7.2 77.6 %all-gather.7.cloned.1.call-start = ((), (), s32[]{:S(2)}) async-start(), calls=%async_computation.6 | async-start | bytes 14155776 | tf_op jit(solution)/shard_map/all_gather | solution.py:831
  12.2 5.5 copy-start.2
  12.2 5.5 copy-start.7
  12.3 186.7 %all-gather.9.cloned.1.call-start = ((), (), s32[]{:S(2)}) async-start(), calls=%async_computation.7 | async-start | bytes 23592960 | tf_op jit(solution)/shard_map/all_gather | solution.py:831
  17.7 276.1 %reduce-scatter.7.cloned.1.call-start = ((), (), s32[]{:S(2)}) async-start(), calls=%async_computation.8 | async-start | bytes 14155776 | tf_op jit(solution)/shard_map/reduce_scatter | solution.py:834
  17.8 5.0 copy-start.8
  21.1 32.5 %copy-start.5 = (f32[1024]{0:T(1024)}, f32[1024]{0:T(1024)S(1)}, u32[]{:S(2)}) copy-start(f32[1024]{0:T(1024)S(1)} %get-tuple-element.185) | copy-start | bytes 12292
  21.3 32.3 %copy-start = (f32[1024,8]{1,0:T(8,128)}, f32[1024,8]{1,0:T(8,128)S(1)}, u32[]{:S(2)}) copy-start(f32[1024,8]{1,0:T(8,128)S(1)} %copy.100) | copy-start | bytes 98308
  21.7 0.6 copy-start.6
  41.8 24.2 %copy-start.1 = (f32[128,1024]{1,0:T(8,128)}, f32[128,1024]{1,0:T(8,128)S(1)}, u32[]{:S(2)}) copy-start(f32[128,1024]{1,0:T(8,128)S(1)} %all-gather) | copy-start | bytes 1572868
  53.6 24.1 %collective-permute-start = (bf16[1,2048,1408]{2,1,0:T(8,128)(2,1)}, bf16[1,2048,1408]{2,1,0:T(8,128)(2,1)}, u32[]{:S(2)}, u32[]{:S(2)}) collective-permute-start(bf16[1,2048,1408]{2,1,0:T(8,128)(2,1)} %constant_dynamic-slice_fusion), channel_id=1, source_target_pairs={{0,1},{1,0},{2,3},{3,2},{4,5},{5,4},{6,7},{7,6}} | collective-permute-start | bytes 17301512 | tf_op jit(solution)/shard_map/ppermute | solution.py:868
  59.3 7.5 copy-start.10
  59.3 18.4 %collective-permute-start.1 = (bf16[1,2048,1408]{2,1,0:T(8,128)(2,1)}, bf16[1,2048,1408]{2,1,0:T(8,128)(2,1)}, u32[]{:S(2)}, u32[]{:S(2)}) collective-permute-start(bf16[1,2048,1408]{2,1,0:T(8,128)(2,1)} %constant_dynamic-slice_fusion.2), channel_id=1, source_target_pairs={{0,1},{1,0},{2,3},{3,2},{4,5},{5,4},{6,7},{7,6}} | collective-permute-start | bytes 17301512 | tf_op jit(solution)/shard_map/ppermute | solution.py:868
  65.9 9.1 copy-start.9
  65.9 17.4 %collective-permute-start.2 = (bf16[1,1408,2048]{2,1,0:T(8,128)(2,1)}, bf16[1,1408,2048]{2,1,0:T(8,128)(2,1)}, u32[]{:S(2)}, u32[]{:S(2)}) collective-permute-start(bf16[1,1408,2048]{2,1,0:T(8,128)(2,1)} %constant_dynamic-slice_fusion.3), channel_id=1, source_target_pairs={{0,1},{1,0},{2,3},{3,2},{4,5},{5,4},{6,7},{7,6}} | collective-permute-start | bytes 17301512 | tf_op jit(solution)/shard_map/ppermute | solution.py:868
  199.0 207.3 %reduce-scatter.9.cloned.1.call-start = ((), (), s32[]{:S(2)}) async-start(), calls=%async_computation.9 | async-start | bytes 9437184 | tf_op jit(solution)/shard_map/reduce_scatter | solution.py:834
  293.7 1.4 copy-start.3
  293.8 144.5 %all-gather.11.cloned.1.call-start = ((), (), s32[]{:S(2)}) async-start(), calls=%async_computation.11 | async-start | bytes 14155776 | tf_op jit(solution)/shard_map/all_gather | solution.py:831
  298.3 244.3 %reduce-scatter.11.cloned.1.call-start = ((), (), s32[]{:S(2)}) async-start(), calls=%async_computation.10 | async-start | bytes 14155776 | tf_op jit(solution)/shard_map/reduce_scatter | solution.py:834
  406.3 1.2 copy-start.4
  406.4 170.3 %all-gather.13.cloned.1.call-start = ((), (), s32[]{:S(2)}) async-start(), calls=%async_computation.12 | async-start | bytes 9437184 | tf_op jit(solution)/shard_map/all_gather | solution.py:831
  410.2 261.8 %all-gather.15.cloned.1.call-start = ((), (), s32[]{:S(2)}) async-start(), calls=%async_computation.13 | async-start | bytes 14155776 | tf_op jit(solution)/shard_map/all_gather | solution.py:831
  546.4 414.3 %all-reduce.8.cloned.1.call-start = ((), (), s32[]{:S(2)}) async-start(), calls=%async_computation.14 | async-start | bytes 524288 | tf_op jit(solution)/shard_map/psum | solution.py:911
  785.6 176.0 %reduce-scatter.15.cloned.1.call-start = ((), (), s32[]{:S(2)}) async-start(), calls=%async_computation.16 | async-start | bytes 9437184 | tf_op jit(solution)/shard_map/reduce_scatter | solution.py:834
  786.2 215.6 %reduce-scatter.13.cloned.1.call-start = ((), (), s32[]{:S(2)}) async-start(), calls=%async_computation.15 | async-start | bytes 14155776 | tf_op jit(solution)/shard_map/reduce_scatter | solution.py:834
  786.9 302.2 %reduce-scatter.17.cloned.1.call-start = ((), (), s32[]{:S(2)}) async-start(), calls=%async_computation.17 | async-start | bytes 14155776 | tf_op jit(solution)/shard_map/reduce_scatter | solution.py:834
  787.5 442.0 %all-reduce.10.cloned.1.call-start = ((), (), s32[]{:S(2)}) async-start(), calls=%async_computation.18 | async-start | bytes 524288 | tf_op jit(solution)/shard_map/psum | solution.py:920
  929.6 178.2 %collective-permute-start.3 = (bf16[1,2048,1408]{2,1,0:T(8,128)(2,1)}, bf16[1,2048,1408]{2,1,0:T(8,128)(2,1)}, u32[]{:S(2)}, u32[]{:S(2)}) collective-permute-start(bf16[1,2048,1408]{2,1,0:T(8,128)(2,1)} %get-tuple-element.124), channel_id=1, source_target_pairs={{0,1},{1,0},{2,3},{3,2},{4,5},{5,4},{6,7},{7,6}} | collective-permute-start | bytes 17301512 | tf_op jit(solution)/shard_map/ppermute | solution.py:908
  956.8 151.0 %collective-permute-start.4 = (bf16[1,2048,1408]{2,1,0:T(8,128)(2,1)}, bf16[1,2048,1408]{2,1,0:T(8,128)(2,1)}, u32[]{:S(2)}, u32[]{:S(2)}) collective-permute-start(bf16[1,2048,1408]{2,1,0:T(8,128)(2,1)} %get-tuple-element.125), channel_id=1, source_target_pairs={{0,1},{1,0},{2,3},{3,2},{4,5},{5,4},{6,7},{7,6}} | collective-permute-start | bytes 17301512 | tf_op jit(solution)/shard_map/ppermute | solution.py:908
  1182.2 51.0 %collective-permute-start.5 = (bf16[1,1408,2048]{2,1,0:T(8,128)(2,1)}, bf16[1,1408,2048]{2,1,0:T(8,128)(2,1)}, u32[]{:S(2)}, u32[]{:S(2)}) collective-permute-start(bf16[1,1408,2048]{2,1,0:T(8,128)(2,1)} %get-tuple-element.137), channel_id=1, source_target_pairs={{0,1},{1,0},{2,3},{3,2},{4,5},{5,4},{6,7},{7,6}} | collective-permute-start | bytes 17301512 | tf_op jit(solution)/shard_map/ppermute | solution.py:919
Sparse Core Ops, SparseCore 0:
  12.4 72.3 all-gather.6
  87.2 101.8 all-gather.8
  199.1 94.5 reduce-scatter.6
  297.0 72.5 reduce-scatter.8
  371.8 66.4 all-gather.10
  442.1 83.9 reduce-scatter.10
  528.0 48.7 all-gather.12
  578.5 66.4 all-gather.14
  785.7 62.8 all-reduce.7
  851.9 62.4 reduce-scatter.14
  917.8 83.9 reduce-scatter.12
  1005.1 83.9 reduce-scatter.16
  1186.7 42.8 all-reduce.9

commit v4 on v3

--- a/solution.py
+++ b/solution.py
@@ -204,7 +204,7 @@
         into = pl.ds(q * LANES if isinstance(q, int) else pl.multiple_of(q * LANES, LANES), LANES)
         out_ref[into, :] = out.astype(out_ref.dtype)
         if with_gate:
-            gout_ref[into, :] = gate
+            gout_ref[:, into] = jnp.transpose(gate, (1, 0))[:8, :]
 
     @pl.when(over == 0)
     def _():
@@ -232,8 +232,8 @@
     if with_gate:
         operands.append(gate_rows)
         in_specs.append(ANY)
-        out_shape.append(jax.ShapeDtypeStruct((tokens, LANES), jnp.float32))
-        out_specs.append(pl.BlockSpec((block, LANES), lambda t, *_: (t, 0)))
+        out_shape.append(jax.ShapeDtypeStruct((8, tokens), jnp.float32))
+        out_specs.append(pl.BlockSpec((8, block), lambda t, *_: (0, t)))
         scratch.append(pltpu.VMEM((rows_max, LANES), jnp.float32))
     scratch += [pltpu.SMEM((groups,), jnp.int32), pltpu.SemaphoreType.DMA((2, rows_max // TILE))]
     kernel = functools.partial(combine_kernel, layout[chunk], spans, groups, with_gate)
@@ -407,12 +407,15 @@
     )
 
 
-def weight_grad_kernel(at, tiles_max, outs, carried, table_ref, *rest):
-    lhs_hbm, rhs_hbm, back, rest = rest[:CHUNKS], rest[CHUNKS:2 * CHUNKS], rest[2 * CHUNKS:2 * CHUNKS + carried], rest[2 * CHUNKS + 2 * carried:]
-    own_out, helped_out, filled, rest = rest[:outs], rest[outs:2 * outs], rest[2 * outs:2 * outs + carried], rest[2 * outs + carried:]
+def weight_grad_kernel(at, tiles_max, outs, groups, carried, table_ref, *rest):
+    lhs_hbm, rhs_hbm, back, rest = rest[:CHUNKS], rest[CHUNKS:2 * CHUNKS], rest[2 * CHUNKS:2 * CHUNKS + carried], rest[2 * CHUNKS + 2 * carried - bool(carried):]
+    own_out, rest = (rest[:outs], rest[outs:]) if groups != "helped" else ((), rest)
+    helped_out, rest = (rest[:outs], rest[outs:]) if groups != "own" else ((), rest)
+    filled, rest = ((*rest[:carried - 1], own_out[0]), rest[carried - 1:]) if carried else ((), rest)
     lhs, rhs, lhs_t, acc, staged, pending, sems, out_sems = rest[:8]
-    experts = own_out[0].shape[0]
-    steps = table_ref[at["steps"]]
+    experts = at["experts"]
+    begin = table_ref[at["own_steps"]] if groups == "helped" else 0
+    steps = table_ref[at["own_steps" if groups == "own" else "steps"]]
 
     def copies(chunk, row, s, half):
         source = pl.ds(pl.multiple_of(row, TILE), TILE)
@@ -437,19 +440,22 @@
     def drain():
         @pl.when(pending[0] != 0)
         def _():
-            for copy in out_copies([out.at[0] for out in own_out]):
+            for copy in out_copies([out.at[0] for out in (own_out or helped_out)]):
                 copy.wait()
 
         pending[0] = 0
 
     pending[0] = 0
-    start(0, 0)
+
+    @pl.when(begin < steps)
+    def _():
+        start(begin, lax.rem(begin, 2))
 
     place = table_ref[at["insert"]]
     if carried:
-        bounce, fetch_sems, store_sems = rest[8:]
-        fetch = [pltpu.make_async_copy(back[i].at[0], bounce.at[i], fetch_sems.at[i]) for i in range(carried)]
-        store = [pltpu.make_async_copy(bounce.at[i], filled[i].at[jnp.maximum(place, 0)], store_sems.at[i]) for i in range(carried)]
+        *bounce, fetch_sems, store_sems = rest[8:]
+        fetch = [pltpu.make_async_copy(back[i].at[0], bounce[i], fetch_sems.at[i]) for i in range(carried)]
+        store = [pltpu.make_async_copy(bounce[i], filled[i].at[jnp.maximum(place, 0)], store_sems.at[i]) for i in range(carried)]
 
         @pl.when(place >= 0)
         def _():
@@ -463,7 +469,7 @@
             part = jnp.dot(lhs_t[:, :depth], rhs[slot, :depth, c:c + block], preferred_element_type=jnp.float32)
             acc[:, c:c + block] = jnp.where(fresh, 0.0, acc[:, c:c + block]) + part
 
-    @pl.loop(0, steps)
+    @pl.loop(begin, steps)
     def _(step):
         slot = lax.rem(step, 2)
         group = table_ref[at["owner"] + step]
@@ -473,13 +479,13 @@
             start(step + 1, 1 - slot)
 
         if carried:
-            @pl.when(jnp.logical_and(place >= 0, step == steps // 2))
+            @pl.when(jnp.logical_and(place >= 0, step == begin + (steps - begin) // 2))
             def _():
                 for one, other in zip(fetch, store):
                     one.wait()
                     other.start()
 
-        fresh = jnp.logical_or(step == 0, group != table_ref[at["owner"] + jnp.maximum(step - 1, 0)])
+        fresh = jnp.logical_or(step == begin, group != table_ref[at["owner"] + jnp.maximum(step - 1, 0)])
         last = jnp.logical_or(step == steps - 1, group != table_ref[at["owner"] + step + 1])
         pair = table_ref[at["src"] + 2 * step + 1] >= 0
         for copy in copies(0, 0, slot, 0):
@@ -502,15 +508,17 @@
             for i in range(outs):
                 staged[i, :, :] = acc[:, i * width:(i + 1) * width].astype(staged.dtype)
 
-            @pl.when(group < experts)
-            def _():
-                for copy in out_copies([out.at[group] for out in own_out]):
-                    copy.start()
-
-            @pl.when(group == experts)
-            def _():
-                for copy in out_copies([out.at[0] for out in helped_out]):
-                    copy.start()
+            if own_out:
+                @pl.when(group < experts)
+                def _():
+                    for copy in out_copies([out.at[group] for out in own_out]):
+                        copy.start()
+
+            if helped_out:
+                @pl.when(group == experts)
+                def _():
+                    for copy in out_copies([out.at[0] for out in helped_out]):
+                        copy.start()
 
             pending[0] = 1
 
@@ -518,14 +526,20 @@
     if carried:
         @pl.when(place >= 0)
         def _():
+            @pl.when(begin >= steps)
+            def _():
+                for one, other in zip(fetch, store):
+                    one.wait()
+                    other.start()
+
             for copy in store:
                 copy.wait()
 
 
-def weight_grad(layout, table, lhs, rhs, experts, outs, back=(), grads=()):
+def weight_grad(layout, table, lhs, rhs, experts, outs, groups="all", back=(), grads=()):
     left, right = lhs[0].shape[1], rhs[0].shape[1]
     width = right // outs
-    carried = len(grads)
+    carried = len(back)
     scratch = [
         pltpu.VMEM((2, 2 * TILE, left), jnp.bfloat16),
         pltpu.VMEM((2, 2 * TILE, right), jnp.bfloat16),
@@ -537,56 +551,25 @@
         pltpu.SemaphoreType.DMA((outs,)),
     ]
     if carried:
-        scratch += [pltpu.VMEM((carried, *grads[0].shape[1:]), jnp.bfloat16), pltpu.SemaphoreType.DMA((carried,)), pltpu.SemaphoreType.DMA((carried,))]
-    out_shape = [jax.ShapeDtypeStruct((n, left, width), jnp.bfloat16) for n in [experts] * outs + [1] * outs]
+        scratch += [pltpu.VMEM(b.shape[1:], b.dtype) for b in back]
+        scratch += [pltpu.SemaphoreType.DMA((carried,)), pltpu.SemaphoreType.DMA((carried,))]
+    counts = ([experts] * outs if groups != "helped" else []) + ([1] * outs if groups != "own" else [])
+    out_shape = [jax.ShapeDtypeStruct((n, left, width), jnp.bfloat16) for n in counts]
+    first = len(out_shape)
     out_shape += [jax.ShapeDtypeStruct(g.shape, g.dtype) for g in grads]
     operands = (*lhs, *rhs, *back, *grads)
+    at = layout["grad"] | {"experts": experts}
     return pl.pallas_call(
-        functools.partial(weight_grad_kernel, layout["grad"], layout["tiles_max"], outs, carried),
+        functools.partial(weight_grad_kernel, at, layout["tiles_max"], outs, groups, carried),
         grid_spec=pltpu.PrefetchScalarGridSpec(
             num_scalar_prefetch=1, in_specs=[ANY] * len(operands), out_specs=[ANY] * len(out_shape), scratch_shapes=scratch
         ),
         out_shape=out_shape,
-        input_output_aliases={1 + 2 * CHUNKS + carried + i: 2 * outs + i for i in range(carried)},
+        input_output_aliases={1 + 2 * CHUNKS + carried + i: first + i for i in range(len(grads))},
         compiler_params=pltpu.CompilerParams(vmem_limit_bytes=VMEM_LIMIT),
-        cost_estimate=pl.CostEstimate(flops=2 * 9000 * left * right, bytes_accessed=100 * 10**6, transcendentals=0),
+        cost_estimate=pl.CostEstimate(flops=(400 if groups == "helped" else 2000) * 9 * left * right, bytes_accessed=100 * 10**6, transcendentals=0),
         name="weight_grad",
     )(table, *operands)
-
-
-def insert_kernel(at, size, table_ref, *rest):
-    back, outs, staged, sems = rest[:size], rest[2 * size:3 * size], rest[3 * size:4 * size], rest[4 * size]
-    place = table_ref[at]
-
-    @pl.when(place >= 0)
-    def _():
-        fetch = [pltpu.make_async_copy(b.at[0], s, sems.at[0, i]) for i, (b, s) in enumerate(zip(back, staged))]
-        store = [pltpu.make_async_copy(s, out.at[place], sems.at[1, i]) for i, (s, out) in enumerate(zip(staged, outs))]
-        for copy in fetch:
-            copy.start()
-        for i in range(size):
-            fetch[i].wait()
-            store[i].start()
-        for copy in store:
-            copy.wait()
-
-
-def insert(layout, table, back, grads):
-    size = len(grads)
-    return pl.pallas_call(
-        functools.partial(insert_kernel, layout["insert"], size),
-        grid_spec=pltpu.PrefetchScalarGridSpec(
-            num_scalar_prefetch=1,
-            in_specs=[ANY] * (2 * size),
-            out_specs=[ANY] * size,
-            scratch_shapes=[pltpu.VMEM(g.shape[1:], g.dtype) for g in grads] + [pltpu.SemaphoreType.DMA((2, size))],
-        ),
-        out_shape=[jax.ShapeDtypeStruct(g.shape, g.dtype) for g in grads],
-        input_output_aliases={1 + size + i: i for i in range(size)},
-        compiler_params=pltpu.CompilerParams(vmem_limit_bytes=VMEM_LIMIT),
-        cost_estimate=pl.CostEstimate(flops=10**9, bytes_accessed=15 * 10**6 * size, transcendentals=0),
-        name="insert",
-    )(table, *back, *grads)
 
 
 def row_blocks(height, dim):
@@ -626,23 +609,24 @@
     )(x, gain.reshape(1, dim))
 
 
-def finish_kernel(x_ref, y_grad_ref, logit_ref, gain_ref, router_ref, *rest):
+def finish_kernel(x_ref, y_grad_ref, prob_ref, gate_grad_ref, balance_ref, gain_ref, router_ref, *rest):
     in_refs, out_refs, (y_ref, x_grad_ref, stats_ref) = rest[:CHUNKS], rest[CHUNKS:2 * CHUNKS], rest[2 * CHUNKS:]
     height = x_ref.shape[0]
+    prob = prob_ref[...]
+    prob_grad = gate_grad_ref[...] + balance_ref[...]
+    logit_grad = (prob * (prob_grad - jnp.sum(prob * prob_grad, axis=0, keepdims=True))).astype(jnp.bfloat16)
     x = x_ref[...].astype(jnp.float32)
     inv_rms = lax.rsqrt(jnp.mean(x * x, axis=-1, keepdims=True) + NORM_EPS)
     unit = x * inv_rms
     gain = gain_ref[...]
     moe_out = of_this_chunk(height, out_refs).astype(jnp.float32)
     y_ref[...] = (x + moe_out).astype(y_ref.dtype)
-    logit_grad = logit_ref[...]
-    routed = lax.dot_general(logit_grad, router_ref[...], (((1,), (1,)), ((), ())), preferred_element_type=jnp.float32)
+    routed = lax.dot_general(logit_grad, router_ref[...], (((0,), (0,)), ((), ())), preferred_element_type=jnp.float32)
     x_norm_grad = of_this_chunk(height, in_refs).astype(jnp.float32) + routed
     unit_grad = x_norm_grad * gain
     x_grad = y_grad_ref[...].astype(jnp.float32) + inv_rms * (unit_grad - unit * jnp.mean(unit_grad * unit, axis=-1, keepdims=True))
     x_grad_ref[...] = x_grad.astype(x_grad_ref.dtype)
     x_norm = (unit * gain).astype(jnp.bfloat16)
-    by_expert = lax.dot_general(logit_grad, x_norm, (((0,), (0,)), ((), ())), preferred_element_type=jnp.float32)
 
     @pl.when(pl.program_id(0) == 0)
     def _():
@@ -651,23 +635,22 @@
     def folded(values):
         return jnp.sum(values.reshape(height // 8, 8, values.shape[1]), axis=0)
 
-    stats_ref[0:8, :] += by_expert[0:8, :]
+    stats_ref[0:8, :] += jnp.dot(logit_grad, x_norm, preferred_element_type=jnp.float32)
     stats_ref[8:16, :] += folded(x_norm_grad * unit)
     stats_ref[16:24, :] += folded(moe_out * moe_out)
 
 
-def finish(x, y_grad, logit_grad, gain, w_router, in_raw, out_raw):
+def finish(x, y_grad, prob, gate_grad, balance, gain, router, in_raw, out_raw):
     tokens, dim = x.shape
     height = LANES
     rows = pl.BlockSpec((height, dim), lambda t: (t, 0))
-    wide = jnp.pad(logit_grad, ((0, 0), (0, LANES - logit_grad.shape[1])))
-    router = jnp.pad(w_router, ((0, 0), (0, LANES - w_router.shape[1])))
+    of_tokens = pl.BlockSpec((8, height), lambda t: (0, t))
     return pl.pallas_call(
         finish_kernel,
         grid=(tokens // height,),
         in_specs=[
-            rows, rows, pl.BlockSpec((height, LANES), lambda t: (t, 0)), pl.BlockSpec((1, dim), lambda t: (0, 0)),
-            pl.BlockSpec((dim, LANES), lambda t: (0, 0)), *row_blocks(height, dim), *row_blocks(height, dim),
+            rows, rows, of_tokens, of_tokens, pl.BlockSpec((8, height), lambda t: (0, 0)), pl.BlockSpec((1, dim), lambda t: (0, 0)),
+            pl.BlockSpec((8, dim), lambda t: (0, 0)), *row_blocks(height, dim), *row_blocks(height, dim),
         ],
         out_specs=[rows, rows, pl.BlockSpec((32, dim), lambda t: (0, 0))],
         out_shape=[
@@ -677,7 +660,7 @@
         compiler_params=pltpu.CompilerParams(vmem_limit_bytes=VMEM_LIMIT),
         cost_estimate=pl.CostEstimate(flops=10**9, bytes_accessed=25 * 10**6, transcendentals=0),
         name="finish",
-    )(x, y_grad, wide, gain.reshape(1, dim), router, *in_raw, *out_raw)
+    )(x, y_grad, prob, gate_grad, balance, gain.reshape(1, dim), router, *in_raw, *out_raw)
 
 
 def below(size, strict):
@@ -784,7 +767,7 @@
     src = jnp.sum(jnp.where(found, of_step(begin.T) + offset + chunk_at + 1, 0), axis=2) - 1
 
     sections = (
-        ("expert", experts_of), ("insert", place.reshape(1)), ("steps", step_stop[-1:]), ("owner", owner), ("src", src),
+        ("expert", experts_of), ("insert", place.reshape(1)), ("steps", step_stop[-1:]), ("own_steps", step_first[-1:]), ("owner", owner), ("src", src),
         ("count", stop[:, -1:]), ("group", group), ("slot", slot), ("fresh", fresh), ("half", half), ("next", follow), ("lo", lo), ("width", width),
         ("first", jnp.concatenate([jnp.zeros((CHUNKS, 1), jnp.int32), stop], axis=1)), ("start", start), ("over", over),
     )
@@ -801,7 +784,7 @@
             "start": [places["start"] + g * span_total + firsts[c] for g in range(groups)],
             "over": places["over"] + firsts[c] // GROUP,
         }
-    layout |= {"grad": {name: places[name] for name in ("steps", "owner", "src", "insert")}, "insert": places["insert"], "tiles_max": tiles_max}
+    layout |= {"grad": {name: places[name] for name in ("steps", "own_steps", "owner", "src", "insert")}, "insert": places["insert"], "tiles_max": tiles_max}
     return pos, table, layout
 
 
@@ -832,6 +815,9 @@
 
         def scatter(rows):
             return lax.psum_scatter(rows, rows_axes, scatter_dimension=0, tiled=True)
+
+        def of_chunk_span(values, c):
+            return values[:, firsts[c] * dev_count:(firsts[c] + PARTS[c]) * dev_count]
 
         def after(values, first):
             return lax.optimization_barrier((values, first))
@@ -869,6 +855,11 @@
         weights = (w_gate, w_up, w_down, *helped)
 
         grad_scale = 2.0 * ACT_COEF / (total_tokens * model_dim)
+        own_prob = route_prob.T
+        balance_row = jnp.broadcast_to(balance_scale * counts[:, None], (num_experts, LANES))
+        router = w_router.T
+        first_tok, (own_prob, balance_row, router, balance_loss) = after(tok[0][0], (own_prob, balance_row, router, balance_loss))
+        tok[0] = (first_tok, tok[0][1])
         x_rows, gate_rows, pre, hidden, d_rows, mg_rows = [], [], [], [], [], []
         out_raw, moe_out, m_own, m_tok, in_raw, gate_part = [], [], [], [], [], []
 
@@ -882,11 +873,13 @@
 
         for c in range(CHUNKS):
             rows, gates, ab, h, out_rows = forward(layout, c, table, pos, prob, tok[c], weights)
+            if c == 1:
+                out_rows = send_cotangent(0, out_rows)
             (partial,) = combine(layout, c, table, pos, out_rows)
             if c == 0:
                 partial, later = after(partial, gathered[1])
                 tok[1:] = [(later, place) for _, place in tok[1:]]
-            else:
+            if c > 1:
                 partial = send_cotangent(c - 1, partial)
             out_raw.append(scatter(partial))
             x_rows.append(rows)
@@ -897,26 +890,32 @@
             d, in_rows, mg, dgate = backward(layout, c, table, pos, m_tok[c], pre[c], hidden[c], gate_rows[c], weights)
             if c == 0:
                 in_rows = send_cotangent(CHUNKS - 1, in_rows)
-            partial, gate_tok = combine(layout, c, table, pos, in_rows, dgate)
+            partial, gate_terms = combine(layout, c, table, pos, in_rows, dgate)
             if c == 0:
                 m_tok[1], partial = after(m_tok[1], partial)
             in_raw.append(scatter(partial))
-            gate_part.append(gate_tok[:, :num_experts])
+            gate_part.append(gate_terms)
             d_rows.append(d)
             mg_rows.append(mg)
         *wide_grads, helped_gate, helped_up = weight_grad(layout, table, x_rows, d_rows, local_experts, 2)
-        back = [lax.ppermute(g, "ep", swap) for g in (helped_gate, helped_up)]
-
-        sums = jnp.concatenate([g.reshape(dev_count, -1) for g in gate_part], axis=1)
-        gate_weight_grad = lax.psum(sums, ("tp", "ep"))
-        gate_weight_grad = lax.dynamic_index_in_dim(gate_weight_grad, my_ep * tp_size + lax.axis_index("tp"), axis=0, keepdims=False)
-        gate_weight_grad, (wide_grads, in_raw) = after(gate_weight_grad, (wide_grads, in_raw))
-        prob_grad = gate_weight_grad.reshape(tokens, num_experts) + balance_scale * counts[None, :]
-        logit_grad = (route_prob * (prob_grad - jnp.sum(route_prob * prob_grad, axis=-1, keepdims=True))).astype(jnp.bfloat16)
-        y, x_grad, stats = finish(x, y_grad, logit_grad, gain, w_router, in_raw, moe_out)
-        stats, (mg_rows[0], x_grad, back) = after(stats, (mg_rows[0], x_grad, back))
-        down_grad, helped_down, gate_grad, up_grad = weight_grad(layout, table, hidden, mg_rows, local_experts, 1, back, wide_grads)
-        (down_grad,) = insert(layout, table, [lax.ppermute(helped_down, "ep", swap)], [down_grad])
+        back = []
+        for grad in (helped_gate, helped_up):
+            back.append(lax.ppermute(grad, "ep", swap))
+
+        mg_rows[0], _ = after(mg_rows[0], wide_grads[0])
+        (helped_down,) = weight_grad(layout, table, hidden, mg_rows, local_experts, 1, "helped")
+        back.append(lax.ppermute(helped_down, "ep", swap))
+
+        gate_sums = lax.psum(jnp.concatenate(gate_part, axis=1), ("tp", "ep"))
+        device = my_ep * tp_size + lax.axis_index("tp")
+        gate_sums = [
+            lax.dynamic_slice_in_dim(of_chunk_span(gate_sums, c), device * PARTS[c], PARTS[c], axis=1) for c in range(CHUNKS)
+        ]
+        gate_weight_grad = jnp.concatenate(gate_sums, axis=1)
+        gate_weight_grad, (helped_down, in_raw) = after(gate_weight_grad, (helped_down, in_raw))
+        y, x_grad, stats = finish(x, y_grad, own_prob, gate_weight_grad, balance_row, gain, router, in_raw, moe_out)
+        stats, (mg_rows[0], x_grad) = after(stats, (mg_rows[0], x_grad))
+        down_grad, gate_grad, up_grad = weight_grad(layout, table, hidden, mg_rows, local_experts, 1, "own", back, wide_grads)
         stats = lax.psum(stats, ("tp", "ep"))
         router_sum = stats[:num_experts].T
         gain_sum = jnp.sum(stats[8:16], axis=0)

time: 1260 us -> 1180 us (0.937)
  waiting for transfers between devices: 228 us -> 153 us
    psum x1, waiting for transfers between devices: 42.3 us -> 0.02 us  [body(): stats = lax.psum(stats, ('tp', 'ep'))]
    reduce_scatter x6, waiting for transfers between devices: 138 us -> 119 us  [scatter(): return lax.psum_scatter(rows, rows_axes, scatter_dimension=0, tiled=True)]
  transfers between devices with their start and end apart: 19 -> 19, of which waited for: 8 -> 6; matrix products, arithmetic and copies ran while one was open for 5% -> 4% of each run, Pallas kernels for 55% -> 64%
where the time goes in v4:
time: 1180 us; the launch traced here: 1170 us
  Pallas kernels  880 us (75%)
  waiting for transfers between devices  153 us (13%)
  starting transfers between devices  40.6 us (3%)
  local copies, waits for them, and re-layouts  31.1 us (3%)
  other arithmetic  24.1 us (2%)
  between operations  20.2 us (2%)
  blocking collectives  18.9 us (2%)
    pallas_call x12, Pallas kernels, call(): pl.pallas_call(kernel, grid_spec=pltpu.PrefetchScalarGridSpec(num_scalar_...  633 us
    pallas_call x3, Pallas kernels, weight_grad(): pl.pallas_call(functools.partial(weight_grad_kernel, at, layout['tiles_ma...  224 us
    reduce_scatter x6, waiting for transfers between devices, scatter(): return lax.psum_scatter(rows, rows_axes, scatter_dimension=0, tiled=True)  119 us
    ppermute x1, starting transfers between devices, body(): back.append(lax.ppermute(helped_down, 'ep', swap))  39 us
    all_gather x5, waiting for transfers between devices, gather(): return lax.all_gather(rows, rows_axes, axis=0, tiled=True)  32.8 us
  transfers between devices with their start and end apart: 19, of which 6 were waited for; matrix products, arithmetic and copies ran while one was open for 4% of the time, Pallas kernels for 64%

profile of v4, /device:TPU:0, one launch (start us, length us, event | category | flops | bytes accessed | tf_op | source)
XLA Modules:
  0.0 1173.1 jit_solution(15514909194730839044)
XLA Ops:
  8.5 3.7 normalize.2
  12.3 5.4 normalize.3
  17.8 3.3 fusion.62
  21.2 18.9 %all-gather = f32[128,1024]{1,0:T(8,128)S(1)} all-gather(f32[16,1024]{1,0:T(8,128)S(1)} %maximum_bitcast_fusion.1), channel_id=2, replica_groups=mesh['tp'=4,'ep'=2] {'ep','tp'}, dimensions={0}, use_global_device_ids=true | all-gather | bytes 589824 | tf_op jit(solution)/shard_map/all_gather | solution.py:835
  44.9 6.2 constant_dynamic-slice_fusion.3
  51.0 5.6 constant_dynamic-slice_fusion.2
  57.2 6.3 constant_dynamic-slice_fusion.1
  78.7 6.1 all-gather.7.cloned.1.call-done.tok_hbm
  85.5 99.6 %shard_map.160 = (bf16[7424,2048]{1,0:T(8,128)(2,1)}, f32[7424,128]{1,0:T(8,128)}, f32[7424,2816]{1,0:T(8,128)}, bf16[7424,1408]{1,0:T(8,128)(2,1)}, bf16[7424,2048]{1,0:T(8,128)(2,1)}) custom-call(s32[1205]{0:T(1024)} %concatenate.42.table_ref, s32[5,64,128]{2,1,0:T(8,128)} %fusion.6.pos_ref, f32[5,64,128]{2,1,0:T(8,128)} %get-tuple-element.178.prob_ref, ...), custom_call_target="tpu_custom_call" | custom-call | flops 74999996416 | bytes 150000000 | tf_op jit(solution)/shard_map/pallas_call | solution.py:25
  185.1 14.4 %shard_map.161 = bf16[3072,2048]{1,0:T(8,128)(2,1)} custom-call(s32[1205]{0:T(1024)} %concatenate.42.table_ref, s32[5,64,128]{2,1,0:T(8,128)} %fusion.6.pos_ref, bf16[7424,2048]{1,0:T(8,128)(2,1)} %get-tuple-element.77.rows_hbm), custom_call_target="tpu_custom_call" | custom-call | flops 8999999488 | bytes 35000000 | tf_op jit(solution)/shard_map/pallas_call | solution.py:25
  199.7 73.4 %shard_map.162 = (bf16[5376,2048]{1,0:T(8,128)(2,1)}, f32[5376,128]{1,0:T(8,128)}, f32[5376,2816]{1,0:T(8,128)}, bf16[5376,1408]{1,0:T(8,128)(2,1)}, bf16[5376,2048]{1,0:T(8,128)(2,1)}) custom-call(s32[1205]{0:T(1024)} %concatenate.42.table_ref, s32[5,64,128]{2,1,0:T(8,128)} %fusion.6.pos_ref, f32[5,64,128]{2,1,0:T(8,128)} %get-tuple-element.178.prob_ref, ...), custom_call_target="tpu_custom_call" | custom-call | flops 74999996416 | bytes 150000000 | tf_op jit(solution)/shard_map/pallas_call | solution.py:25
  273.1 21.4 %reduce-scatter.7.cloned.1.call-done.rest_3_ = bf16[384,2048]{1,0:T(8,128)(2,1)} async-done(((bf16[3072,2048]{1,0:T(8,128)(2,1)}), bf16[384,2048]{1,0:T(8,128)(2,1)}) %reduce-scatter.7.cloned.1.call-update) | async-done | bytes 1572880 | tf_op jit(solution)/shard_map/reduce_scatter | solution.py:817
  294.5 11.1 shard_map.163
  307.0 3.2 add_convert_fusion.1
  310.3 96.7 %shard_map.164 = (bf16[7424,2048]{1,0:T(8,128)(2,1)}, f32[7424,128]{1,0:T(8,128)}, f32[7424,2816]{1,0:T(8,128)}, bf16[7424,1408]{1,0:T(8,128)(2,1)}, bf16[7424,2048]{1,0:T(8,128)(2,1)}) custom-call(s32[1205]{0:T(1024)} %concatenate.42.table_ref, s32[5,64,128]{2,1,0:T(8,128)} %fusion.6.pos_ref, f32[5,64,128]{2,1,0:T(8,128)} %get-tuple-element.178.prob_ref, ...), custom_call_target="tpu_custom_call" | custom-call | flops 74999996416 | bytes 150000000 | tf_op jit(solution)/shard_map/pallas_call | solution.py:25
  407.0 14.2 %shard_map.165 = bf16[3072,2048]{1,0:T(8,128)(2,1)} custom-call(s32[1205]{0:T(1024)} %concatenate.42.table_ref, s32[5,64,128]{2,1,0:T(8,128)} %fusion.6.pos_ref, bf16[7424,2048]{1,0:T(8,128)(2,1)} %get-tuple-element.82.rows_hbm), custom_call_target="tpu_custom_call" | custom-call | flops 8999999488 | bytes 35000000 | tf_op jit(solution)/shard_map/pallas_call | solution.py:25
  425.1 13.3 %all-gather.11.cloned.1.call-done.tok_hbm = bf16[3072,2048]{1,0:T(8,128)(2,1)} async-done(((bf16[384,2048]{1,0:T(8,128)(2,1)}), bf16[3072,2048]{1,0:T(8,128)(2,1)}) %all-gather.11.cloned.1.call-update) | async-done | bytes 12582928 | tf_op jit(solution)/shard_map/all_gather | solution.py:814
  438.4 104.3 %shard_map.166 = (bf16[7424,2816]{1,0:T(8,128)(2,1)}, bf16[7424,2048]{1,0:T(8,128)(2,1)}, bf16[7424,2048]{1,0:T(8,128)(2,1)}, f32[7424,128]{1,0:T(8,128)}) custom-call(s32[1205]{0:T(1024)} %concatenate.42.table_ref, s32[5,64,128]{2,1,0:T(8,128)} %fusion.6.pos_ref, bf16[3072,2048]{1,0:T(8,128)(2,1)} %all-gather.11.cloned.1.call-done.tok_hbm, ...), custom_call_target="tpu_custom_call" | custom-call | flops 74999996416 | bytes 150000000 | tf_op jit(solution)/shard_map/pallas_call | solution.py:25
  542.8 3.7 add_convert_fusion
  546.5 16.9 %shard_map.167 = (bf16[3072,2048]{1,0:T(8,128)(2,1)}, f32[8,3072]{1,0:T(8,128)}) custom-call(s32[1205]{0:T(1024)} %concatenate.42.table_ref, s32[5,64,128]{2,1,0:T(8,128)} %fusion.6.pos_ref, bf16[7424,2048]{1,0:T(8,128)(2,1)} %get-tuple-element.90.rows_hbm, f32[7424,128]{1,0:T(8,128)} %get-tuple-element.91.rest_0_), custom_call_target="tpu_custom_call" | custom-call | flops 8999999488 | bytes 35000000 | tf_op jit(solution)/shard_map/pallas_call | solution.py:25
  563.4 13.4 %all-gather.13.cloned.1.call-done.tok_hbm = bf16[2048,2048]{1,0:T(8,128)(2,1)} async-done(((bf16[256,2048]{1,0:T(8,128)(2,1)}), bf16[2048,2048]{1,0:T(8,128)(2,1)}) %all-gather.13.cloned.1.call-update) | async-done | bytes 8388624 | tf_op jit(solution)/shard_map/all_gather | solution.py:814
  576.8 81.0 %shard_map.168 = (bf16[5376,2816]{1,0:T(8,128)(2,1)}, bf16[5376,2048]{1,0:T(8,128)(2,1)}, bf16[5376,2048]{1,0:T(8,128)(2,1)}, f32[5376,128]{1,0:T(8,128)}) custom-call(s32[1205]{0:T(1024)} %concatenate.42.table_ref, s32[5,64,128]{2,1,0:T(8,128)} %fusion.6.pos_ref, bf16[2048,2048]{1,0:T(8,128)(2,1)} %all-gather.13.cloned.1.call-done.tok_hbm, ...), custom_call_target="tpu_custom_call" | custom-call | flops 74999996416 | bytes 150000000 | tf_op jit(solution)/shard_map/pallas_call | solution.py:25
  657.8 11.9 %shard_map.169 = (bf16[2048,2048]{1,0:T(8,128)(2,1)}, f32[8,2048]{1,0:T(8,128)}) custom-call(s32[1205]{0:T(1024)} %concatenate.42.table_ref, s32[5,64,128]{2,1,0:T(8,128)} %fusion.6.pos_ref, bf16[5376,2048]{1,0:T(8,128)(2,1)} %get-tuple-element.98.rows_hbm, f32[5376,128]{1,0:T(8,128)} %get-tuple-element.99.rest_0_), custom_call_target="tpu_custom_call" | custom-call | flops 8999999488 | bytes 35000000 | tf_op jit(solution)/shard_map/pallas_call | solution.py:25
  669.7 94.4 %shard_map.170 = (bf16[7424,2816]{1,0:T(8,128)(2,1)}, bf16[7424,2048]{1,0:T(8,128)(2,1)}, bf16[7424,2048]{1,0:T(8,128)(2,1)}, f32[7424,128]{1,0:T(8,128)}) custom-call(s32[1205]{0:T(1024)} %concatenate.42.table_ref, s32[5,64,128]{2,1,0:T(8,128)} %fusion.6.pos_ref, bf16[3072,2048]{1,0:T(8,128)(2,1)} %all-gather.15.cloned.1.call-done.tok_hbm, ...), custom_call_target="tpu_custom_call" | custom-call | flops 74999996416 | bytes 150000000 | tf_op jit(solution)/shard_map/pallas_call | solution.py:25
  764.2 15.3 %shard_map.171 = (bf16[3072,2048]{1,0:T(8,128)(2,1)}, f32[8,3072]{1,0:T(8,128)}) custom-call(s32[1205]{0:T(1024)} %concatenate.42.table_ref, s32[5,64,128]{2,1,0:T(8,128)} %fusion.6.pos_ref, bf16[7424,2048]{1,0:T(8,128)(2,1)} %get-tuple-element.105.rows_hbm, f32[7424,128]{1,0:T(8,128)} %get-tuple-element.106.rest_0_), custom_call_target="tpu_custom_call" | custom-call | flops 8999999488 | bytes 35000000 | tf_op jit(solution)/shard_map/pallas_call | solution.py:25
  783.1 142.3 %weight_grad.3 = (bf16[4,2048,1408]{2,1,0:T(8,128)(2,1)}, bf16[4,2048,1408]{2,1,0:T(8,128)(2,1)}, bf16[1,2048,1408]{2,1,0:T(8,128)(2,1)}, bf16[1,2048,1408]{2,1,0:T(8,128)(2,1)}) custom-call(s32[1205]{0:T(1024)} %concatenate.42.table_ref, bf16[7424,2048]{1,0:T(8,128)(2,1)} %get-tuple-element.109.rest_0_, bf16[5376,2048]{1,0:T(8,128)(2,1)} %get-tuple-element.110.rest_1_, ...), custom_call_target="tpu_custom_call" | custom-call | flops 103809024000 | bytes 100000000 | tf_op jit(solution)/shard_map/weight_grad/pallas_call | solution.py:562
  925.5 21.2 %weight_grad.4 = bf16[1,1408,2048]{2,1,0:T(8,128)(2,1)} custom-call(s32[1205]{0:T(1024)} %concatenate.42.table_ref, bf16[7424,1408]{1,0:T(8,128)(2,1)} %get-tuple-element.86.h_hbm.rest_0_, bf16[5376,1408]{1,0:T(8,128)(2,1)} %get-tuple-element.96.h_hbm.rest_1_, bf16[7424,1408]{1,0:T(8,128)(2,1)} %get-tuple-element.103.h_hbm.rest_2_, ...), custom_call_target="tpu_custom_call" | custom-call | flops 10380902400 | bytes 100000000 | tf_op jit(solution)/shard_map/weight_grad/pallas_call | solution.py:562
  946.6 39.0 %collective-permute-start.5 = (bf16[1,1408,2048]{2,1,0:T(8,128)(2,1)}, bf16[1,1408,2048]{2,1,0:T(8,128)(2,1)}, u32[]{:S(2)}, u32[]{:S(2)}) collective-permute-start(bf16[1,1408,2048]{2,1,0:T(8,128)(2,1)} %weight_grad.4), channel_id=1, source_target_pairs={{0,1},{1,0},{2,3},{3,2},{4,5},{5,4},{6,7},{7,6}} | collective-permute-start | bytes 17301512 | tf_op jit(solution)/shard_map/ppermute | solution.py:907
  988.6 6.4 reduce-scatter.13.cloned.1.call-done.rest_0_
  995.0 90.9 %reduce-scatter.17.cloned.1.call-done.rest_2_ = bf16[384,2048]{1,0:T(8,128)(2,1)} async-done(((bf16[3072,2048]{1,0:T(8,128)(2,1)}), bf16[384,2048]{1,0:T(8,128)(2,1)}) %reduce-scatter.17.cloned.1.call-update) | async-done | bytes 1572880 | tf_op jit(solution)/shard_map/reduce_scatter | solution.py:817
  1085.9 13.8 %finish.1 = (bf16[1024,2048]{1,0:T(8,128)(2,1)}, bf16[1024,2048]{1,0:T(8,128)(2,1)}, f32[32,2048]{1,0:T(8,128)}) custom-call(bf16[1024,2048]{1,0:T(8,128)(2,1)} %x_ref.5, bf16[1024,2048]{1,0:T(8,128)(2,1)} %y_grad_ref.1, f32[8,1024]{1,0:T(8,128)} %fusion.65.prob_ref, f32[8,1024]{1,0:T(8,128)} %pad_maximum_fusion.1.gate_grad_ref, ...), custom_call_target="tpu_custom_call" | custom-call | flops 1000000000 | bytes 25000000 | tf_op jit(solution)/shard_map/finish/pallas_call | solution.py:648
  1099.8 60.5 %weight_grad.5 = (bf16[4,1408,2048]{2,1,0:T(8,128)(2,1)}, bf16[4,2048,1408]{2,1,0:T(8,128)(2,1)}, bf16[4,2048,1408]{2,1,0:T(8,128)(2,1)}) custom-call(s32[1205]{0:T(1024)} %concatenate.42.table_ref, bf16[7424,1408]{1,0:T(8,128)(2,1)} %get-tuple-element.86.h_hbm.rest_0_, ...), custom_call_target="tpu_custom_call", output_to_operand_aliasing={{1}: (10, {}), {2}: (11, {})} | custom-call | flops 51904512000 | bytes 100000000 | tf_op jit(solution)/shard_map/weight_grad/pallas_call | solution.py:562
  (182 shorter events, 34.9 us)
Async XLA Ops:
  7.2 77.7 %all-gather.7.cloned.1.call-start = ((), (), s32[]{:S(2)}) async-start(), calls=%async_computation.6 | async-start | bytes 14155776 | tf_op jit(solution)/shard_map/all_gather | solution.py:814
  12.2 5.5 copy-start.4
  12.2 5.5 copy-start.1
  12.2 5.5 copy-start.3
  12.3 187.3 %all-gather.9.cloned.1.call-start = ((), (), s32[]{:S(2)}) async-start(), calls=%async_computation.7 | async-start | bytes 23592960 | tf_op jit(solution)/shard_map/all_gather | solution.py:814
  17.7 276.8 %reduce-scatter.7.cloned.1.call-start = ((), (), s32[]{:S(2)}) async-start(), calls=%async_computation.8 | async-start | bytes 14155776 | tf_op jit(solution)/shard_map/reduce_scatter | solution.py:817
  51.0 34.5 %collective-permute-start = (bf16[1,2048,1408]{2,1,0:T(8,128)(2,1)}, bf16[1,2048,1408]{2,1,0:T(8,128)(2,1)}, u32[]{:S(2)}, u32[]{:S(2)}) collective-permute-start(bf16[1,2048,1408]{2,1,0:T(8,128)(2,1)} %constant_dynamic-slice_fusion.3), channel_id=1, source_target_pairs={{0,1},{1,0},{2,3},{3,2},{4,5},{5,4},{6,7},{7,6}} | collective-permute-start | bytes 17301512 | tf_op jit(solution)/shard_map/ppermute | solution.py:854
  56.6 7.7 copy-start.6
  56.6 28.9 %collective-permute-start.1 = (bf16[1,2048,1408]{2,1,0:T(8,128)(2,1)}, bf16[1,2048,1408]{2,1,0:T(8,128)(2,1)}, u32[]{:S(2)}, u32[]{:S(2)}) collective-permute-start(bf16[1,2048,1408]{2,1,0:T(8,128)(2,1)} %constant_dynamic-slice_fusion.2), channel_id=1, source_target_pairs={{0,1},{1,0},{2,3},{3,2},{4,5},{5,4},{6,7},{7,6}} | collective-permute-start | bytes 17301512 | tf_op jit(solution)/shard_map/ppermute | solution.py:854
  63.5 9.6 copy-start.5
  63.5 22.0 %collective-permute-start.2 = (bf16[1,1408,2048]{2,1,0:T(8,128)(2,1)}, bf16[1,1408,2048]{2,1,0:T(8,128)(2,1)}, u32[]{:S(2)}, u32[]{:S(2)}) collective-permute-start(bf16[1,1408,2048]{2,1,0:T(8,128)(2,1)} %constant_dynamic-slice_fusion.1), channel_id=1, source_target_pairs={{0,1},{1,0},{2,3},{3,2},{4,5},{5,4},{6,7},{7,6}} | collective-permute-start | bytes 17301512 | tf_op jit(solution)/shard_map/ppermute | solution.py:854
  199.6 221.6 %reduce-scatter.9.cloned.1.call-start = ((), (), s32[]{:S(2)}) async-start(), calls=%async_computation.9 | async-start | bytes 9437184 | tf_op jit(solution)/shard_map/reduce_scatter | solution.py:817
  305.6 1.4 copy-start
  305.6 132.8 %all-gather.11.cloned.1.call-start = ((), (), s32[]{:S(2)}) async-start(), calls=%async_computation.11 | async-start | bytes 14155776 | tf_op jit(solution)/shard_map/all_gather | solution.py:814
  310.2 232.5 %reduce-scatter.11.cloned.1.call-start = ((), (), s32[]{:S(2)}) async-start(), calls=%async_computation.10 | async-start | bytes 14155776 | tf_op jit(solution)/shard_map/reduce_scatter | solution.py:817
  421.2 1.2 copy-start.2
  421.3 155.5 %all-gather.13.cloned.1.call-start = ((), (), s32[]{:S(2)}) async-start(), calls=%async_computation.12 | async-start | bytes 9437184 | tf_op jit(solution)/shard_map/all_gather | solution.py:814
  425.1 244.6 %all-gather.15.cloned.1.call-start = ((), (), s32[]{:S(2)}) async-start(), calls=%async_computation.13 | async-start | bytes 14155776 | tf_op jit(solution)/shard_map/all_gather | solution.py:814
  546.5 439.7 %all-reduce.6.cloned.1.call-start = ((), (), s32[]{:S(2)}) async-start(), calls=%async_computation.14 | async-start | bytes 524288 | tf_op jit(solution)/shard_map/psum | solution.py:909
  781.2 207.5 %reduce-scatter.15.cloned.1.call-start = ((), (), s32[]{:S(2)}) async-start(), calls=%async_computation.16 | async-start | bytes 9437184 | tf_op jit(solution)/shard_map/reduce_scatter | solution.py:817
  781.8 213.3 %reduce-scatter.13.cloned.1.call-start = ((), (), s32[]{:S(2)}) async-start(), calls=%async_computation.15 | async-start | bytes 14155776 | tf_op jit(solution)/shard_map/reduce_scatter | solution.py:817
  782.5 303.4 %reduce-scatter.17.cloned.1.call-start = ((), (), s32[]{:S(2)}) async-start(), calls=%async_computation.17 | async-start | bytes 14155776 | tf_op jit(solution)/shard_map/reduce_scatter | solution.py:817
  783.1 377.3 %all-reduce.8.cloned.1.call-start = ((), (), s32[]{:S(2)}) async-start(), calls=%async_computation.18 | async-start | bytes 524288 | tf_op jit(solution)/shard_map/psum | solution.py:919
  946.6 153.1 %collective-permute-start.5 = (bf16[1,1408,2048]{2,1,0:T(8,128)(2,1)}, bf16[1,1408,2048]{2,1,0:T(8,128)(2,1)}, u32[]{:S(2)}, u32[]{:S(2)}) collective-permute-start(bf16[1,1408,2048]{2,1,0:T(8,128)(2,1)} %weight_grad.4), channel_id=1, source_target_pairs={{0,1},{1,0},{2,3},{3,2},{4,5},{5,4},{6,7},{7,6}} | collective-permute-start | bytes 17301512 | tf_op jit(solution)/shard_map/ppermute | solution.py:907
  985.7 114.1 %collective-permute-start.3 = (bf16[1,2048,1408]{2,1,0:T(8,128)(2,1)}, bf16[1,2048,1408]{2,1,0:T(8,128)(2,1)}, u32[]{:S(2)}, u32[]{:S(2)}) collective-permute-start(bf16[1,2048,1408]{2,1,0:T(8,128)(2,1)} %get-tuple-element.134), channel_id=1, source_target_pairs={{0,1},{1,0},{2,3},{3,2},{4,5},{5,4},{6,7},{7,6}} | collective-permute-start | bytes 17301512 | tf_op jit(solution)/shard_map/ppermute | solution.py:903
  985.7 114.1 %collective-permute-start.4 = (bf16[1,2048,1408]{2,1,0:T(8,128)(2,1)}, bf16[1,2048,1408]{2,1,0:T(8,128)(2,1)}, u32[]{:S(2)}, u32[]{:S(2)}) collective-permute-start(bf16[1,2048,1408]{2,1,0:T(8,128)(2,1)} %get-tuple-element.135), channel_id=1, source_target_pairs={{0,1},{1,0},{2,3},{3,2},{4,5},{5,4},{6,7},{7,6}} | collective-permute-start | bytes 17301512 | tf_op jit(solution)/shard_map/ppermute | solution.py:903
Sparse Core Ops, SparseCore 0:
  12.4 72.4 all-gather.6
  87.2 101.8 all-gather.8
  199.7 94.6 reduce-scatter.6
  305.8 64.4 reduce-scatter.8
  371.9 66.4 all-gather.10
  442.3 83.9 reduce-scatter.10
  528.1 48.6 all-gather.12
  578.6 66.4 all-gather.14
  781.3 60.5 all-reduce.5
  845.1 62.4 reduce-scatter.14
  911.0 83.9 reduce-scatter.12
  998.3 87.5 reduce-scatter.16
  1099.9 42.8 all-reduce.7

commit v5 on v3

--- a/solution.py
+++ b/solution.py
@@ -18,6 +18,8 @@
 PARTS = (384, 256, 384)
 CHUNKS = len(PARTS)
 WINDOWS = (1, 2, 3, 4)
+WIDE_WINDOWS = (6, 8)
+WHOLE_CHUNK = 99
 VMEM_LIMIT = 67_043_328
 
 
@@ -92,18 +94,36 @@
             if gate_ref is not None:
                 gate_ref[into, :] = jnp.broadcast_to(jnp.sum(gate, axis=1, keepdims=True), (LANES, LANES))
 
-        @pl.when(width > WINDOWS[-1])
-        def _():
-            self.await_tokens(self.spans)
-
-            @pl.loop(0, 2)
+        halves = 2 - self.table_ref[self.at["half"] + tile]
+
+        def start_of(half, count):
+            return jnp.minimum(self.table_ref[self.at["lo"] + 2 * tile + half], self.spans - count)
+
+        def one_by_one(count):
+            self.await_tokens(jnp.maximum(start_of(0, count), start_of(1, count)) + count)
+
+            @pl.loop(0, halves)
             def _(half):
-                window(half, self.spans, 0)
+                window(half, count, start_of(half, count))
+
+            @pl.when(halves == 1)
+            def _():
+                for ref in (x_ref,) if gate_ref is None else (x_ref, gate_ref):
+                    ref[LANES:, :] = jnp.zeros((TILE - LANES, ref.shape[1]), ref.dtype)
+
+        @pl.when(width == WHOLE_CHUNK)
+        def _():
+            one_by_one(self.spans)
+
+        for k in WIDE_WINDOWS:
+            @pl.when(width == k)
+            def _(k=k):
+                one_by_one(2 * k)
 
         for k in WINDOWS:
             @pl.when(width == k)
             def _(k=k):
-                starts = [jnp.minimum(self.table_ref[self.at["lo"] + 2 * tile + half], self.spans - 2 * k) for half in range(2)]
+                starts = [start_of(half, 2 * k) for half in range(2)]
                 self.await_tokens(jnp.maximum(starts[0], starts[1]) + 2 * k)
                 for half in range(2):
                     window(half, 2 * k, starts[half])
@@ -204,7 +224,7 @@
         into = pl.ds(q * LANES if isinstance(q, int) else pl.multiple_of(q * LANES, LANES), LANES)
         out_ref[into, :] = out.astype(out_ref.dtype)
         if with_gate:
-            gout_ref[into, :] = gate
+            gout_ref[:, into] = jnp.transpose(gate, (1, 0))[:8, :]
 
     @pl.when(over == 0)
     def _():
@@ -232,8 +252,8 @@
     if with_gate:
         operands.append(gate_rows)
         in_specs.append(ANY)
-        out_shape.append(jax.ShapeDtypeStruct((tokens, LANES), jnp.float32))
-        out_specs.append(pl.BlockSpec((block, LANES), lambda t, *_: (t, 0)))
+        out_shape.append(jax.ShapeDtypeStruct((8, tokens), jnp.float32))
+        out_specs.append(pl.BlockSpec((8, block), lambda t, *_: (0, t)))
         scratch.append(pltpu.VMEM((rows_max, LANES), jnp.float32))
     scratch += [pltpu.SMEM((groups,), jnp.int32), pltpu.SemaphoreType.DMA((2, rows_max // TILE))]
     kernel = functools.partial(combine_kernel, layout[chunk], spans, groups, with_gate)
@@ -409,9 +429,10 @@
 
 def weight_grad_kernel(at, tiles_max, outs, carried, table_ref, *rest):
     lhs_hbm, rhs_hbm, back, rest = rest[:CHUNKS], rest[CHUNKS:2 * CHUNKS], rest[2 * CHUNKS:2 * CHUNKS + carried], rest[2 * CHUNKS + 2 * carried:]
-    own_out, helped_out, filled, rest = rest[:outs], rest[outs:2 * outs], rest[2 * outs:2 * outs + carried], rest[2 * outs + carried:]
+    own_out, helped_out, rest = rest[:outs], rest[outs:2 * outs], rest[2 * outs:]
+    filled, rest = rest[:carried], rest[carried:]
     lhs, rhs, lhs_t, acc, staged, pending, sems, out_sems = rest[:8]
-    experts = own_out[0].shape[0]
+    experts = at["experts"]
     steps = table_ref[at["steps"]]
 
     def copies(chunk, row, s, half):
@@ -443,13 +464,14 @@
         pending[0] = 0
 
     pending[0] = 0
+
     start(0, 0)
 
     place = table_ref[at["insert"]]
     if carried:
-        bounce, fetch_sems, store_sems = rest[8:]
-        fetch = [pltpu.make_async_copy(back[i].at[0], bounce.at[i], fetch_sems.at[i]) for i in range(carried)]
-        store = [pltpu.make_async_copy(bounce.at[i], filled[i].at[jnp.maximum(place, 0)], store_sems.at[i]) for i in range(carried)]
+        *bounce, fetch_sems, store_sems = rest[8:]
+        fetch = [pltpu.make_async_copy(back[i].at[0], bounce[i], fetch_sems.at[i]) for i in range(carried)]
+        store = [pltpu.make_async_copy(bounce[i], filled[i].at[jnp.maximum(place, 0)], store_sems.at[i]) for i in range(carried)]
 
         @pl.when(place >= 0)
         def _():
@@ -525,7 +547,7 @@
 def weight_grad(layout, table, lhs, rhs, experts, outs, back=(), grads=()):
     left, right = lhs[0].shape[1], rhs[0].shape[1]
     width = right // outs
-    carried = len(grads)
+    carried = len(back)
     scratch = [
         pltpu.VMEM((2, 2 * TILE, left), jnp.bfloat16),
         pltpu.VMEM((2, 2 * TILE, right), jnp.bfloat16),
@@ -537,17 +559,20 @@
         pltpu.SemaphoreType.DMA((outs,)),
     ]
     if carried:
-        scratch += [pltpu.VMEM((carried, *grads[0].shape[1:]), jnp.bfloat16), pltpu.SemaphoreType.DMA((carried,)), pltpu.SemaphoreType.DMA((carried,))]
+        scratch += [pltpu.VMEM(b.shape[1:], b.dtype) for b in back]
+        scratch += [pltpu.SemaphoreType.DMA((carried,)), pltpu.SemaphoreType.DMA((carried,))]
     out_shape = [jax.ShapeDtypeStruct((n, left, width), jnp.bfloat16) for n in [experts] * outs + [1] * outs]
+    first = len(out_shape)
     out_shape += [jax.ShapeDtypeStruct(g.shape, g.dtype) for g in grads]
     operands = (*lhs, *rhs, *back, *grads)
+    at = layout["grad"] | {"experts": experts}
     return pl.pallas_call(
-        functools.partial(weight_grad_kernel, layout["grad"], layout["tiles_max"], outs, carried),
+        functools.partial(weight_grad_kernel, at, layout["tiles_max"], outs, carried),
         grid_spec=pltpu.PrefetchScalarGridSpec(
             num_scalar_prefetch=1, in_specs=[ANY] * len(operands), out_specs=[ANY] * len(out_shape), scratch_shapes=scratch
         ),
         out_shape=out_shape,
-        input_output_aliases={1 + 2 * CHUNKS + carried + i: 2 * outs + i for i in range(carried)},
+        input_output_aliases={1 + 2 * CHUNKS + carried + i: first + i for i in range(len(grads))},
         compiler_params=pltpu.CompilerParams(vmem_limit_bytes=VMEM_LIMIT),
         cost_estimate=pl.CostEstimate(flops=2 * 9000 * left * right, bytes_accessed=100 * 10**6, transcendentals=0),
         name="weight_grad",
@@ -626,23 +651,24 @@
     )(x, gain.reshape(1, dim))
 
 
-def finish_kernel(x_ref, y_grad_ref, logit_ref, gain_ref, router_ref, *rest):
+def finish_kernel(x_ref, y_grad_ref, prob_ref, gate_grad_ref, balance_ref, gain_ref, router_ref, *rest):
     in_refs, out_refs, (y_ref, x_grad_ref, stats_ref) = rest[:CHUNKS], rest[CHUNKS:2 * CHUNKS], rest[2 * CHUNKS:]
     height = x_ref.shape[0]
+    prob = prob_ref[...]
+    prob_grad = gate_grad_ref[...] + balance_ref[...]
+    logit_grad = (prob * (prob_grad - jnp.sum(prob * prob_grad, axis=0, keepdims=True))).astype(jnp.bfloat16)
     x = x_ref[...].astype(jnp.float32)
     inv_rms = lax.rsqrt(jnp.mean(x * x, axis=-1, keepdims=True) + NORM_EPS)
     unit = x * inv_rms
     gain = gain_ref[...]
     moe_out = of_this_chunk(height, out_refs).astype(jnp.float32)
     y_ref[...] = (x + moe_out).astype(y_ref.dtype)
-    logit_grad = logit_ref[...]
-    routed = lax.dot_general(logit_grad, router_ref[...], (((1,), (1,)), ((), ())), preferred_element_type=jnp.float32)
+    routed = lax.dot_general(logit_grad, router_ref[...], (((0,), (0,)), ((), ())), preferred_element_type=jnp.float32)
     x_norm_grad = of_this_chunk(height, in_refs).astype(jnp.float32) + routed
     unit_grad = x_norm_grad * gain
     x_grad = y_grad_ref[...].astype(jnp.float32) + inv_rms * (unit_grad - unit * jnp.mean(unit_grad * unit, axis=-1, keepdims=True))
     x_grad_ref[...] = x_grad.astype(x_grad_ref.dtype)
     x_norm = (unit * gain).astype(jnp.bfloat16)
-    by_expert = lax.dot_general(logit_grad, x_norm, (((0,), (0,)), ((), ())), preferred_element_type=jnp.float32)
 
     @pl.when(pl.program_id(0) == 0)
     def _():
@@ -651,23 +677,22 @@
     def folded(values):
         return jnp.sum(values.reshape(height // 8, 8, values.shape[1]), axis=0)
 
-    stats_ref[0:8, :] += by_expert[0:8, :]
+    stats_ref[0:8, :] += jnp.dot(logit_grad, x_norm, preferred_element_type=jnp.float32)
     stats_ref[8:16, :] += folded(x_norm_grad * unit)
     stats_ref[16:24, :] += folded(moe_out * moe_out)
 
 
-def finish(x, y_grad, logit_grad, gain, w_router, in_raw, out_raw):
+def finish(x, y_grad, prob, gate_grad, balance, gain, router, in_raw, out_raw):
     tokens, dim = x.shape
     height = LANES
     rows = pl.BlockSpec((height, dim), lambda t: (t, 0))
-    wide = jnp.pad(logit_grad, ((0, 0), (0, LANES - logit_grad.shape[1])))
-    router = jnp.pad(w_router, ((0, 0), (0, LANES - w_router.shape[1])))
+    of_tokens = pl.BlockSpec((8, height), lambda t: (0, t))
     return pl.pallas_call(
         finish_kernel,
         grid=(tokens // height,),
         in_specs=[
-            rows, rows, pl.BlockSpec((height, LANES), lambda t: (t, 0)), pl.BlockSpec((1, dim), lambda t: (0, 0)),
-            pl.BlockSpec((dim, LANES), lambda t: (0, 0)), *row_blocks(height, dim), *row_blocks(height, dim),
+            rows, rows, of_tokens, of_tokens, pl.BlockSpec((8, height), lambda t: (0, 0)), pl.BlockSpec((1, dim), lambda t: (0, 0)),
+            pl.BlockSpec((8, dim), lambda t: (0, 0)), *row_blocks(height, dim), *row_blocks(height, dim),
         ],
         out_specs=[rows, rows, pl.BlockSpec((32, dim), lambda t: (0, 0))],
         out_shape=[
@@ -677,7 +702,7 @@
         compiler_params=pltpu.CompilerParams(vmem_limit_bytes=VMEM_LIMIT),
         cost_estimate=pl.CostEstimate(flops=10**9, bytes_accessed=25 * 10**6, transcendentals=0),
         name="finish",
-    )(x, y_grad, wide, gain.reshape(1, dim), router, *in_raw, *out_raw)
+    )(x, y_grad, prob, gate_grad, balance, gain.reshape(1, dim), router, *in_raw, *out_raw)
 
 
 def below(size, strict):
@@ -757,6 +782,8 @@
     lo = count(jnp.logical_and(inside, stops <= row0), 2)
     hi = jnp.minimum(count(jnp.logical_and(inside, stops < row0 + LANES), 2), jnp.array(spans_of, jnp.int32)[:, None] - 1)
     width = jnp.maximum(jnp.max(((hi - lo + 2) // 2).reshape(CHUNKS, tiles_max, 2), axis=2), 1)
+    for narrower, wider in zip((WINDOWS[-1], *WIDE_WINDOWS), (*WIDE_WINDOWS, WHOLE_CHUNK)):
+        width = jnp.where(jnp.logical_and(width > narrower, width <= wider), wider, width)
     start = jnp.minimum(span_first // 16 * 16, to_spans(stop) * TILE - REACH)
     empty = to_spans(tiles) == 0
     leading = jnp.logical_and(jnp.logical_not(empty), to_spans(ordinal) == 0)
@@ -833,6 +860,9 @@
         def scatter(rows):
             return lax.psum_scatter(rows, rows_axes, scatter_dimension=0, tiled=True)
 
+        def of_chunk_span(values, c):
+            return values[:, firsts[c] * dev_count:(firsts[c] + PARTS[c]) * dev_count]
+
         def after(values, first):
             return lax.optimization_barrier((values, first))
 
@@ -869,6 +899,11 @@
         weights = (w_gate, w_up, w_down, *helped)
 
         grad_scale = 2.0 * ACT_COEF / (total_tokens * model_dim)
+        own_prob = route_prob.T
+        balance_row = jnp.broadcast_to(balance_scale * counts[:, None], (num_experts, LANES))
+        router = w_router.T
+        first_tok, (own_prob, balance_row, router, balance_loss) = after(tok[0][0], (own_prob, balance_row, router, balance_loss))
+        tok[0] = (first_tok, tok[0][1])
         x_rows, gate_rows, pre, hidden, d_rows, mg_rows = [], [], [], [], [], []
         out_raw, moe_out, m_own, m_tok, in_raw, gate_part = [], [], [], [], [], []
 
@@ -882,11 +917,13 @@
 
         for c in range(CHUNKS):
             rows, gates, ab, h, out_rows = forward(layout, c, table, pos, prob, tok[c], weights)
+            if c == 1:
+                out_rows = send_cotangent(0, out_rows)
             (partial,) = combine(layout, c, table, pos, out_rows)
             if c == 0:
                 partial, later = after(partial, gathered[1])
                 tok[1:] = [(later, place) for _, place in tok[1:]]
-            else:
+            if c > 1:
                 partial = send_cotangent(c - 1, partial)
             out_raw.append(scatter(partial))
             x_rows.append(rows)
@@ -897,24 +934,27 @@
             d, in_rows, mg, dgate = backward(layout, c, table, pos, m_tok[c], pre[c], hidden[c], gate_rows[c], weights)
             if c == 0:
                 in_rows = send_cotangent(CHUNKS - 1, in_rows)
-            partial, gate_tok = combine(layout, c, table, pos, in_rows, dgate)
+            partial, gate_terms = combine(layout, c, table, pos, in_rows, dgate)
             if c == 0:
                 m_tok[1], partial = after(m_tok[1], partial)
             in_raw.append(scatter(partial))
-            gate_part.append(gate_tok[:, :num_experts])
+            gate_part.append(gate_terms)
             d_rows.append(d)
             mg_rows.append(mg)
         *wide_grads, helped_gate, helped_up = weight_grad(layout, table, x_rows, d_rows, local_experts, 2)
-        back = [lax.ppermute(g, "ep", swap) for g in (helped_gate, helped_up)]
-
-        sums = jnp.concatenate([g.reshape(dev_count, -1) for g in gate_part], axis=1)
-        gate_weight_grad = lax.psum(sums, ("tp", "ep"))
-        gate_weight_grad = lax.dynamic_index_in_dim(gate_weight_grad, my_ep * tp_size + lax.axis_index("tp"), axis=0, keepdims=False)
+        back = []
+        for grad in (helped_gate, helped_up):
+            back.append(lax.ppermute(grad, "ep", swap))
+
+        gate_sums = lax.psum(jnp.concatenate(gate_part, axis=1), ("tp", "ep"))
+        device = my_ep * tp_size + lax.axis_index("tp")
+        gate_sums = [
+            lax.dynamic_slice_in_dim(of_chunk_span(gate_sums, c), device * PARTS[c], PARTS[c], axis=1) for c in range(CHUNKS)
+        ]
+        gate_weight_grad = jnp.concatenate(gate_sums, axis=1)
         gate_weight_grad, (wide_grads, in_raw) = after(gate_weight_grad, (wide_grads, in_raw))
-        prob_grad = gate_weight_grad.reshape(tokens, num_experts) + balance_scale * counts[None, :]
-        logit_grad = (route_prob * (prob_grad - jnp.sum(route_prob * prob_grad, axis=-1, keepdims=True))).astype(jnp.bfloat16)
-        y, x_grad, stats = finish(x, y_grad, logit_grad, gain, w_router, in_raw, moe_out)
-        stats, (mg_rows[0], x_grad, back) = after(stats, (mg_rows[0], x_grad, back))
+        y, x_grad, stats = finish(x, y_grad, own_prob, gate_weight_grad, balance_row, gain, router, in_raw, moe_out)
+        stats, (mg_rows[0], x_grad) = after(stats, (mg_rows[0], x_grad))
         down_grad, helped_down, gate_grad, up_grad = weight_grad(layout, table, hidden, mg_rows, local_experts, 1, back, wide_grads)
         (down_grad,) = insert(layout, table, [lax.ppermute(helped_down, "ep", swap)], [down_grad])
         stats = lax.psum(stats, ("tp", "ep"))

time: 1260 us -> 1250 us (level)
  transfers between devices with their start and end apart: 19 -> 19, of which waited for: 8 -> 7; matrix products, arithmetic and copies ran while one was open for 5% -> 4% of each run, Pallas kernels for 55% -> 55%
where the time goes in v5:
time: 1250 us; the launch traced here: 1240 us
  Pallas kernels  887 us (71%)
  waiting for transfers between devices  228 us (18%)
  local copies, waits for them, and re-layouts  29.8 us (2%)
  starting transfers between devices  27.6 us (2%)
  other arithmetic  24.2 us (2%)
  between operations  20.5 us (2%)
  blocking collectives  18.9 us (2%)
    pallas_call x12, Pallas kernels, call(): pl.pallas_call(kernel, grid_spec=pltpu.PrefetchScalarGridSpec(num_scalar_...  643 us
    pallas_call x2, Pallas kernels, weight_grad(): pl.pallas_call(functools.partial(weight_grad_kernel, at, layout['tiles_ma...  216 us
    reduce_scatter x6, waiting for transfers between devices, scatter(): return lax.psum_scatter(rows, rows_axes, scatter_dimension=0, tiled=True)  150 us
    psum x1, waiting for transfers between devices, body(): stats = lax.psum(stats, ('tp', 'ep'))  43 us
    all_gather x5, waiting for transfers between devices, gather(): return lax.all_gather(rows, rows_axes, axis=0, tiled=True)  33.4 us
  transfers between devices with their start and end apart: 19, of which 7 were waited for; matrix products, arithmetic and copies ran while one was open for 4% of the time, Pallas kernels for 55%

profile of v5, /device:TPU:0, one launch (start us, length us, event | category | flops | bytes accessed | tf_op | source)
XLA Modules:
  0.0 1240.8 jit_solution(574836184096019420)
XLA Ops:
  8.5 3.7 normalize.2
  12.3 5.4 normalize.3
  21.2 18.9 %all-gather = f32[128,1024]{1,0:T(8,128)S(1)} all-gather(f32[16,1024]{1,0:T(8,128)S(1)} %maximum_bitcast_fusion.1), channel_id=2, replica_groups=mesh['tp'=4,'ep'=2] {'ep','tp'}, dimensions={0}, use_global_device_ids=true | all-gather | bytes 589824 | tf_op jit(solution)/shard_map/all_gather | solution.py:879
  44.9 6.2 constant_dynamic-slice_fusion.3
  51.0 5.6 constant_dynamic-slice_fusion.2
  57.2 6.3 constant_dynamic-slice_fusion.1
  77.4 7.5 all-gather.7.cloned.1.call-done.tok_hbm
  85.5 108.5 %shard_map.160 = (bf16[7424,2048]{1,0:T(8,128)(2,1)}, f32[7424,128]{1,0:T(8,128)}, f32[7424,2816]{1,0:T(8,128)}, bf16[7424,1408]{1,0:T(8,128)(2,1)}, bf16[7424,2048]{1,0:T(8,128)(2,1)}) custom-call(s32[1204]{0:T(1024)} %concatenate.42.table_ref, s32[5,64,128]{2,1,0:T(8,128)} %fusion.6.pos_ref, f32[5,64,128]{2,1,0:T(8,128)} %get-tuple-element.182.prob_ref, ...), custom_call_target="tpu_custom_call" | custom-call | flops 74999996416 | bytes 150000000 | tf_op jit(solution)/shard_map/pallas_call | solution.py:27
  194.0 14.2 %shard_map.161 = bf16[3072,2048]{1,0:T(8,128)(2,1)} custom-call(s32[1204]{0:T(1024)} %concatenate.42.table_ref, s32[5,64,128]{2,1,0:T(8,128)} %fusion.6.pos_ref, bf16[7424,2048]{1,0:T(8,128)(2,1)} %get-tuple-element.79.rows_hbm), custom_call_target="tpu_custom_call" | custom-call | flops 8999999488 | bytes 35000000 | tf_op jit(solution)/shard_map/pallas_call | solution.py:27
  208.3 73.3 %shard_map.162 = (bf16[5376,2048]{1,0:T(8,128)(2,1)}, f32[5376,128]{1,0:T(8,128)}, f32[5376,2816]{1,0:T(8,128)}, bf16[5376,1408]{1,0:T(8,128)(2,1)}, bf16[5376,2048]{1,0:T(8,128)(2,1)}) custom-call(s32[1204]{0:T(1024)} %concatenate.42.table_ref, s32[5,64,128]{2,1,0:T(8,128)} %fusion.6.pos_ref, f32[5,64,128]{2,1,0:T(8,128)} %get-tuple-element.182.prob_ref, ...), custom_call_target="tpu_custom_call" | custom-call | flops 74999996416 | bytes 150000000 | tf_op jit(solution)/shard_map/pallas_call | solution.py:27
  281.6 19.9 %reduce-scatter.7.cloned.1.call-done.rest_3_ = bf16[384,2048]{1,0:T(8,128)(2,1)} async-done(((bf16[3072,2048]{1,0:T(8,128)(2,1)}), bf16[384,2048]{1,0:T(8,128)(2,1)}) %reduce-scatter.7.cloned.1.call-update) | async-done | bytes 1572880 | tf_op jit(solution)/shard_map/reduce_scatter | solution.py:861
  301.5 11.1 shard_map.163
  317.3 97.4 %shard_map.164 = (bf16[7424,2048]{1,0:T(8,128)(2,1)}, f32[7424,128]{1,0:T(8,128)}, f32[7424,2816]{1,0:T(8,128)}, bf16[7424,1408]{1,0:T(8,128)(2,1)}, bf16[7424,2048]{1,0:T(8,128)(2,1)}) custom-call(s32[1204]{0:T(1024)} %concatenate.42.table_ref, s32[5,64,128]{2,1,0:T(8,128)} %fusion.6.pos_ref, f32[5,64,128]{2,1,0:T(8,128)} %get-tuple-element.182.prob_ref, ...), custom_call_target="tpu_custom_call" | custom-call | flops 74999996416 | bytes 150000000 | tf_op jit(solution)/shard_map/pallas_call | solution.py:27
  414.8 14.2 %shard_map.165 = bf16[3072,2048]{1,0:T(8,128)(2,1)} custom-call(s32[1204]{0:T(1024)} %concatenate.42.table_ref, s32[5,64,128]{2,1,0:T(8,128)} %fusion.6.pos_ref, bf16[7424,2048]{1,0:T(8,128)(2,1)} %get-tuple-element.84.rows_hbm), custom_call_target="tpu_custom_call" | custom-call | flops 8999999488 | bytes 35000000 | tf_op jit(solution)/shard_map/pallas_call | solution.py:27
  432.9 12.4 %all-gather.11.cloned.1.call-done.tok_hbm = bf16[3072,2048]{1,0:T(8,128)(2,1)} async-done(((bf16[384,2048]{1,0:T(8,128)(2,1)}), bf16[3072,2048]{1,0:T(8,128)(2,1)}) %all-gather.11.cloned.1.call-update) | async-done | bytes 12582928 | tf_op jit(solution)/shard_map/all_gather | solution.py:858
  445.3 104.3 %shard_map.166 = (bf16[7424,2816]{1,0:T(8,128)(2,1)}, bf16[7424,2048]{1,0:T(8,128)(2,1)}, bf16[7424,2048]{1,0:T(8,128)(2,1)}, f32[7424,128]{1,0:T(8,128)}) custom-call(s32[1204]{0:T(1024)} %concatenate.42.table_ref, s32[5,64,128]{2,1,0:T(8,128)} %fusion.6.pos_ref, bf16[3072,2048]{1,0:T(8,128)(2,1)} %all-gather.11.cloned.1.call-done.tok_hbm, ...), custom_call_target="tpu_custom_call" | custom-call | flops 74999996416 | bytes 150000000 | tf_op jit(solution)/shard_map/pallas_call | solution.py:27
  549.6 3.7 add_convert_fusion
  553.4 16.8 %shard_map.167 = (bf16[3072,2048]{1,0:T(8,128)(2,1)}, f32[8,3072]{1,0:T(8,128)}) custom-call(s32[1204]{0:T(1024)} %concatenate.42.table_ref, s32[5,64,128]{2,1,0:T(8,128)} %fusion.6.pos_ref, bf16[7424,2048]{1,0:T(8,128)(2,1)} %get-tuple-element.92.rows_hbm, f32[7424,128]{1,0:T(8,128)} %get-tuple-element.93.rest_0_), custom_call_target="tpu_custom_call" | custom-call | flops 8999999488 | bytes 35000000 | tf_op jit(solution)/shard_map/pallas_call | solution.py:27
  570.2 13.5 %all-gather.13.cloned.1.call-done.tok_hbm = bf16[2048,2048]{1,0:T(8,128)(2,1)} async-done(((bf16[256,2048]{1,0:T(8,128)(2,1)}), bf16[2048,2048]{1,0:T(8,128)(2,1)}) %all-gather.13.cloned.1.call-update) | async-done | bytes 8388624 | tf_op jit(solution)/shard_map/all_gather | solution.py:858
  583.7 81.3 %shard_map.168 = (bf16[5376,2816]{1,0:T(8,128)(2,1)}, bf16[5376,2048]{1,0:T(8,128)(2,1)}, bf16[5376,2048]{1,0:T(8,128)(2,1)}, f32[5376,128]{1,0:T(8,128)}) custom-call(s32[1204]{0:T(1024)} %concatenate.42.table_ref, s32[5,64,128]{2,1,0:T(8,128)} %fusion.6.pos_ref, bf16[2048,2048]{1,0:T(8,128)(2,1)} %all-gather.13.cloned.1.call-done.tok_hbm, ...), custom_call_target="tpu_custom_call" | custom-call | flops 74999996416 | bytes 150000000 | tf_op jit(solution)/shard_map/pallas_call | solution.py:27
  665.1 11.9 shard_map.169
  677.0 94.5 %shard_map.170 = (bf16[7424,2816]{1,0:T(8,128)(2,1)}, bf16[7424,2048]{1,0:T(8,128)(2,1)}, bf16[7424,2048]{1,0:T(8,128)(2,1)}, f32[7424,128]{1,0:T(8,128)}) custom-call(s32[1204]{0:T(1024)} %concatenate.42.table_ref, s32[5,64,128]{2,1,0:T(8,128)} %fusion.6.pos_ref, bf16[3072,2048]{1,0:T(8,128)(2,1)} %all-gather.15.cloned.1.call-done.tok_hbm, ...), custom_call_target="tpu_custom_call" | custom-call | flops 74999996416 | bytes 150000000 | tf_op jit(solution)/shard_map/pallas_call | solution.py:27
  771.5 15.3 %shard_map.171 = (bf16[3072,2048]{1,0:T(8,128)(2,1)}, f32[8,3072]{1,0:T(8,128)}) custom-call(s32[1204]{0:T(1024)} %concatenate.42.table_ref, s32[5,64,128]{2,1,0:T(8,128)} %fusion.6.pos_ref, bf16[7424,2048]{1,0:T(8,128)(2,1)} %get-tuple-element.107.rows_hbm, f32[7424,128]{1,0:T(8,128)} %get-tuple-element.108.rest_0_), custom_call_target="tpu_custom_call" | custom-call | flops 8999999488 | bytes 35000000 | tf_op jit(solution)/shard_map/pallas_call | solution.py:27
  790.5 141.1 %weight_grad.2 = (bf16[4,2048,1408]{2,1,0:T(8,128)(2,1)}, bf16[4,2048,1408]{2,1,0:T(8,128)(2,1)}, bf16[1,2048,1408]{2,1,0:T(8,128)(2,1)}, bf16[1,2048,1408]{2,1,0:T(8,128)(2,1)}) custom-call(s32[1204]{0:T(1024)} %concatenate.42.table_ref, bf16[7424,2048]{1,0:T(8,128)(2,1)} %get-tuple-element.110.rest_0_, bf16[5376,2048]{1,0:T(8,128)(2,1)} %get-tuple-element.111.rest_1_, ...), custom_call_target="tpu_custom_call" | custom-call | flops 103809024000 | bytes 100000000 | tf_op jit(solution)/shard_map/weight_grad/pallas_call | solution.py:569
  931.6 22.1 %collective-permute-start.3 = (bf16[1,2048,1408]{2,1,0:T(8,128)(2,1)}, bf16[1,2048,1408]{2,1,0:T(8,128)(2,1)}, u32[]{:S(2)}, u32[]{:S(2)}) collective-permute-start(bf16[1,2048,1408]{2,1,0:T(8,128)(2,1)} %get-tuple-element.136), channel_id=1, source_target_pairs={{0,1},{1,0},{2,3},{3,2},{4,5},{5,4},{6,7},{7,6}} | collective-permute-start | bytes 17301512 | tf_op jit(solution)/shard_map/ppermute | solution.py:947
  956.3 42.6 %reduce-scatter.13.cloned.1.call-done.rest_0_ = bf16[384,2048]{1,0:T(8,128)(2,1)} async-done(((bf16[3072,2048]{1,0:T(8,128)(2,1)}), bf16[384,2048]{1,0:T(8,128)(2,1)}) %reduce-scatter.13.cloned.1.call-update) | async-done | bytes 1572880 | tf_op jit(solution)/shard_map/reduce_scatter | solution.py:861
  998.9 87.3 %reduce-scatter.17.cloned.1.call-done.rest_2_ = bf16[384,2048]{1,0:T(8,128)(2,1)} async-done(((bf16[3072,2048]{1,0:T(8,128)(2,1)}), bf16[384,2048]{1,0:T(8,128)(2,1)}) %reduce-scatter.17.cloned.1.call-update) | async-done | bytes 1572880 | tf_op jit(solution)/shard_map/reduce_scatter | solution.py:861
  1086.2 13.9 %finish.1 = (bf16[1024,2048]{1,0:T(8,128)(2,1)}, bf16[1024,2048]{1,0:T(8,128)(2,1)}, f32[32,2048]{1,0:T(8,128)}) custom-call(bf16[1024,2048]{1,0:T(8,128)(2,1)} %x_ref.5, bf16[1024,2048]{1,0:T(8,128)(2,1)} %y_grad_ref.1, f32[8,1024]{1,0:T(8,128)} %fusion.65.prob_ref, f32[8,1024]{1,0:T(8,128)} %pad_maximum_fusion.1.gate_grad_ref, ...), custom_call_target="tpu_custom_call" | custom-call | flops 1000000000 | bytes 25000000 | tf_op jit(solution)/shard_map/finish/pallas_call | solution.py:690
  1100.1 74.4 %weight_grad.3 = (bf16[4,1408,2048]{2,1,0:T(8,128)(2,1)}, bf16[1,1408,2048]{2,1,0:T(8,128)(2,1)}, bf16[4,2048,1408]{2,1,0:T(8,128)(2,1)}, bf16[4,2048,1408]{2,1,0:T(8,128)(2,1)}) custom-call(s32[1204]{0:T(1024)} %concatenate.42.table_ref, bf16[7424,1408]{1,0:T(8,128)(2,1)} %get-tuple-element.88.h_hbm.rest_0_, ...), custom_call_target="tpu_custom_call", output_to_operand_aliasing={{2}: (9, {}), {3}: (10, {})} | custom-call | flops 51904512000 | bytes 100000000 | tf_op jit(solution)/shard_map/weight_grad/pallas_call | solution.py:569
  1174.5 4.3 collective-permute-start.5
  1178.8 43.0 %all-reduce.8.cloned.1.call-done = f32[32,2048]{1,0:T(8,128)} async-done(((f32[32,2048]{1,0:T(8,128)}), f32[32,2048]{1,0:T(8,128)}) %all-reduce.8.cloned.1.call-update) | async-done | bytes 262160 | tf_op jit(solution)/shard_map/psum | solution.py:960
  1225.5 5.9 insert.1
  (182 shorter events, 39.6 us)
Async XLA Ops:
  7.2 77.7 %all-gather.7.cloned.1.call-start = ((), (), s32[]{:S(2)}) async-start(), calls=%async_computation.6 | async-start | bytes 14155776 | tf_op jit(solution)/shard_map/all_gather | solution.py:858
  12.2 5.5 copy-start.4
  12.2 5.5 copy-start.1
  12.2 5.5 copy-start.3
  12.3 196.0 %all-gather.9.cloned.1.call-start = ((), (), s32[]{:S(2)}) async-start(), calls=%async_computation.7 | async-start | bytes 23592960 | tf_op jit(solution)/shard_map/all_gather | solution.py:858
  17.7 283.8 %reduce-scatter.7.cloned.1.call-start = ((), (), s32[]{:S(2)}) async-start(), calls=%async_computation.8 | async-start | bytes 14155776 | tf_op jit(solution)/shard_map/reduce_scatter | solution.py:861
  51.0 34.5 %collective-permute-start = (bf16[1,2048,1408]{2,1,0:T(8,128)(2,1)}, bf16[1,2048,1408]{2,1,0:T(8,128)(2,1)}, u32[]{:S(2)}, u32[]{:S(2)}) collective-permute-start(bf16[1,2048,1408]{2,1,0:T(8,128)(2,1)} %constant_dynamic-slice_fusion.3), channel_id=1, source_target_pairs={{0,1},{1,0},{2,3},{3,2},{4,5},{5,4},{6,7},{7,6}} | collective-permute-start | bytes 17301512 | tf_op jit(solution)/shard_map/ppermute | solution.py:898
  56.6 7.7 copy-start.6
  56.6 28.9 %collective-permute-start.1 = (bf16[1,2048,1408]{2,1,0:T(8,128)(2,1)}, bf16[1,2048,1408]{2,1,0:T(8,128)(2,1)}, u32[]{:S(2)}, u32[]{:S(2)}) collective-permute-start(bf16[1,2048,1408]{2,1,0:T(8,128)(2,1)} %constant_dynamic-slice_fusion.2), channel_id=1, source_target_pairs={{0,1},{1,0},{2,3},{3,2},{4,5},{5,4},{6,7},{7,6}} | collective-permute-start | bytes 17301512 | tf_op jit(solution)/shard_map/ppermute | solution.py:898
  63.5 9.0 copy-start.5
  63.5 22.0 %collective-permute-start.2 = (bf16[1,1408,2048]{2,1,0:T(8,128)(2,1)}, bf16[1,1408,2048]{2,1,0:T(8,128)(2,1)}, u32[]{:S(2)}, u32[]{:S(2)}) collective-permute-start(bf16[1,1408,2048]{2,1,0:T(8,128)(2,1)} %constant_dynamic-slice_fusion.1), channel_id=1, source_target_pairs={{0,1},{1,0},{2,3},{3,2},{4,5},{5,4},{6,7},{7,6}} | collective-permute-start | bytes 17301512 | tf_op jit(solution)/shard_map/ppermute | solution.py:898
  208.2 220.7 %reduce-scatter.9.cloned.1.call-start = ((), (), s32[]{:S(2)}) async-start(), calls=%async_computation.9 | async-start | bytes 9437184 | tf_op jit(solution)/shard_map/reduce_scatter | solution.py:861
  312.7 1.4 copy-start
  312.7 132.6 %all-gather.11.cloned.1.call-start = ((), (), s32[]{:S(2)}) async-start(), calls=%async_computation.11 | async-start | bytes 14155776 | tf_op jit(solution)/shard_map/all_gather | solution.py:858
  317.3 232.3 %reduce-scatter.11.cloned.1.call-start = ((), (), s32[]{:S(2)}) async-start(), calls=%async_computation.10 | async-start | bytes 14155776 | tf_op jit(solution)/shard_map/reduce_scatter | solution.py:861
  429.0 1.2 copy-start.2
  429.0 154.7 %all-gather.13.cloned.1.call-start = ((), (), s32[]{:S(2)}) async-start(), calls=%async_computation.12 | async-start | bytes 9437184 | tf_op jit(solution)/shard_map/all_gather | solution.py:858
  432.8 244.2 %all-gather.15.cloned.1.call-start = ((), (), s32[]{:S(2)}) async-start(), calls=%async_computation.13 | async-start | bytes 14155776 | tf_op jit(solution)/shard_map/all_gather | solution.py:858
  553.3 400.4 %all-reduce.6.cloned.1.call-start = ((), (), s32[]{:S(2)}) async-start(), calls=%async_computation.14 | async-start | bytes 524288 | tf_op jit(solution)/shard_map/psum | solution.py:949
  788.5 167.8 %reduce-scatter.15.cloned.1.call-start = ((), (), s32[]{:S(2)}) async-start(), calls=%async_computation.16 | async-start | bytes 9437184 | tf_op jit(solution)/shard_map/reduce_scatter | solution.py:861
  789.1 209.8 %reduce-scatter.13.cloned.1.call-start = ((), (), s32[]{:S(2)}) async-start(), calls=%async_computation.15 | async-start | bytes 14155776 | tf_op jit(solution)/shard_map/reduce_scatter | solution.py:861
  789.8 296.3 %reduce-scatter.17.cloned.1.call-start = ((), (), s32[]{:S(2)}) async-start(), calls=%async_computation.17 | async-start | bytes 14155776 | tf_op jit(solution)/shard_map/reduce_scatter | solution.py:861
  790.4 431.4 %all-reduce.8.cloned.1.call-start = ((), (), s32[]{:S(2)}) async-start(), calls=%async_computation.18 | async-start | bytes 524288 | tf_op jit(solution)/shard_map/psum | solution.py:960
  931.6 168.4 %collective-permute-start.3 = (bf16[1,2048,1408]{2,1,0:T(8,128)(2,1)}, bf16[1,2048,1408]{2,1,0:T(8,128)(2,1)}, u32[]{:S(2)}, u32[]{:S(2)}) collective-permute-start(bf16[1,2048,1408]{2,1,0:T(8,128)(2,1)} %get-tuple-element.136), channel_id=1, source_target_pairs={{0,1},{1,0},{2,3},{3,2},{4,5},{5,4},{6,7},{7,6}} | collective-permute-start | bytes 17301512 | tf_op jit(solution)/shard_map/ppermute | solution.py:947
  953.8 146.3 %collective-permute-start.4 = (bf16[1,2048,1408]{2,1,0:T(8,128)(2,1)}, bf16[1,2048,1408]{2,1,0:T(8,128)(2,1)}, u32[]{:S(2)}, u32[]{:S(2)}) collective-permute-start(bf16[1,2048,1408]{2,1,0:T(8,128)(2,1)} %get-tuple-element.137), channel_id=1, source_target_pairs={{0,1},{1,0},{2,3},{3,2},{4,5},{5,4},{6,7},{7,6}} | collective-permute-start | bytes 17301512 | tf_op jit(solution)/shard_map/ppermute | solution.py:947
  1174.5 51.1 %collective-permute-start.5 = (bf16[1,1408,2048]{2,1,0:T(8,128)(2,1)}, bf16[1,1408,2048]{2,1,0:T(8,128)(2,1)}, u32[]{:S(2)}, u32[]{:S(2)}) collective-permute-start(bf16[1,1408,2048]{2,1,0:T(8,128)(2,1)} %get-tuple-element.142), channel_id=1, source_target_pairs={{0,1},{1,0},{2,3},{3,2},{4,5},{5,4},{6,7},{7,6}} | collective-permute-start | bytes 17301512 | tf_op jit(solution)/shard_map/ppermute | solution.py:959
Sparse Core Ops, SparseCore 0:
  12.4 72.4 all-gather.6
  87.2 101.8 all-gather.8
  208.4 93.0 reduce-scatter.6
  312.8 64.3 reduce-scatter.8
  378.9 66.4 all-gather.10
  449.2 83.9 reduce-scatter.10
  535.0 48.6 all-gather.12
  585.5 66.4 all-gather.14
  788.6 57.0 all-reduce.5
  848.9 62.4 reduce-scatter.14
  914.9 83.9 reduce-scatter.12
  1002.2 83.9 reduce-scatter.16
  1178.9 42.8 all-reduce.7

commit v6 on v5

--- a/solution.py
+++ b/solution.py
@@ -20,6 +20,7 @@
 WINDOWS = (1, 2, 3, 4)
 WIDE_WINDOWS = (6, 8)
 WHOLE_CHUNK = 99
+UNITS = 4
 VMEM_LIMIT = 67_043_328
 
 
@@ -436,20 +437,22 @@
     steps = table_ref[at["steps"]]
 
     def copies(chunk, row, s, half):
-        source = pl.ds(pl.multiple_of(row, TILE), TILE)
-        into = pl.ds(half * TILE, TILE)
+        source = pl.ds(pl.multiple_of(row, LANES), LANES)
+        into = pl.ds(half * LANES, LANES)
         return (
             pltpu.make_async_copy(lhs_hbm[chunk].at[source, :], lhs.at[s, into, :], sems.at[s, half, 0]),
             pltpu.make_async_copy(rhs_hbm[chunk].at[source, :], rhs.at[s, into, :], sems.at[s, half, 1]),
         )
 
     def start(index, s):
-        for half in range(2):
-            src = table_ref[at["src"] + 2 * index + half]
+        for unit in range(UNITS):
+            src = table_ref[at["src"] + UNITS * index + unit]
             for chunk in range(CHUNKS):
-                @pl.when(jnp.logical_and(src >= chunk * tiles_max, src < (chunk + 1) * tiles_max))
-                def _(chunk=chunk, src=src, half=half):
-                    for copy in copies(chunk, (src - chunk * tiles_max) * TILE, s, half):
+                first = 2 * chunk * tiles_max
+
+                @pl.when(jnp.logical_and(src >= first, src < first + 2 * tiles_max))
+                def _(first=first, chunk=chunk, src=src, unit=unit):
+                    for copy in copies(chunk, (src - first) * LANES, s, unit):
                         copy.start()
 
     def out_copies(targets):
@@ -503,17 +506,24 @@
 
         fresh = jnp.logical_or(step == 0, group != table_ref[at["owner"] + jnp.maximum(step - 1, 0)])
         last = jnp.logical_or(step == steps - 1, group != table_ref[at["owner"] + step + 1])
-        pair = table_ref[at["src"] + 2 * step + 1] >= 0
-        for copy in copies(0, 0, slot, 0):
-            copy.wait()
-
-        @pl.when(pair)
-        def _():
-            for copy in copies(0, 0, slot, 1):
-                copy.wait()
+        there = [table_ref[at["src"] + UNITS * step + unit] >= 0 for unit in range(UNITS)]
+        for unit in range(UNITS):
+            @pl.when(there[unit])
+            def _(unit=unit):
+                for copy in copies(0, 0, slot, unit):
+                    copy.wait()
+
+        for unit in range(1, UNITS, 2):
+            @pl.when(jnp.logical_and(there[unit - 1], jnp.logical_not(there[unit])))
+            def _(unit=unit):
+                for ref in (lhs, rhs):
+                    ref[slot, unit * LANES:(unit + 1) * LANES, :] = jnp.zeros((LANES, ref.shape[2]), ref.dtype)
+
+        @pl.when(there[2])
+        def _():
             accumulate(slot, fresh, 2 * TILE)
 
-        @pl.when(jnp.logical_not(pair))
+        @pl.when(jnp.logical_not(there[2]))
         def _():
             accumulate(slot, fresh, TILE)
 
@@ -555,7 +565,7 @@
         pltpu.VMEM((left, right), jnp.float32),
         pltpu.VMEM((outs, left, width), jnp.bfloat16),
         pltpu.SMEM((1,), jnp.int32),
-        pltpu.SemaphoreType.DMA((2, 2, 2)),
+        pltpu.SemaphoreType.DMA((2, UNITS, 2)),
         pltpu.SemaphoreType.DMA((outs,)),
     ]
     if carried:
@@ -791,10 +801,11 @@
     over = jnp.any(jnp.logical_and(jnp.logical_not(empty), span_stop - start > REACH), axis=0)
     over = jnp.any(over.reshape(-1, GROUP), axis=1)
 
-    in_chunks = running(tiles.T)
+    units = (total + LANES - 1) // LANES
+    in_chunks = running(units.T)
     both = in_chunks[:, -1]
-    step_stop = running((both + 1) // 2)
-    step_first = step_stop - (both + 1) // 2
+    step_stop = running((both + UNITS - 1) // UNITS)
+    step_first = step_stop - (both + UNITS - 1) // UNITS
     steps = CHUNKS * tiles_max // 2 + groups
     step = jnp.arange(steps, dtype=jnp.int32)
     owner = jnp.minimum(count(step[:, None] >= step_stop[None, :], 1), groups - 1)
@@ -803,12 +814,12 @@
     def of_step(values):
         return jnp.sum(jnp.where(step_mine[:, :, None], values[None], 0), axis=1)[:, None, :]
 
-    local = 2 * (step - of_step(step_first[:, None])[:, 0, 0])[:, None, None] + jnp.arange(2, dtype=jnp.int32)[None, :, None]
-    ends, sizes = of_step(in_chunks), of_step(tiles.T)
+    local = UNITS * (step - of_step(step_first[:, None])[:, 0, 0])[:, None, None] + jnp.arange(UNITS, dtype=jnp.int32)[None, :, None]
+    ends, sizes = of_step(in_chunks), of_step(units.T)
     offset = local - (ends - sizes)
     found = jnp.logical_and(offset >= 0, local < ends)
-    chunk_at = jnp.arange(CHUNKS, dtype=jnp.int32) * tiles_max
-    src = jnp.sum(jnp.where(found, of_step(begin.T) + offset + chunk_at + 1, 0), axis=2) - 1
+    chunk_at = jnp.arange(CHUNKS, dtype=jnp.int32) * 2 * tiles_max
+    src = jnp.sum(jnp.where(found, 2 * of_step(begin.T) + offset + chunk_at + 1, 0), axis=2) - 1
 
     sections = (
         ("expert", experts_of), ("insert", place.reshape(1)), ("steps", step_stop[-1:]), ("owner", owner), ("src", src),

time: 1250 us -> 1240 us (level)
  no operation moved by 1% of the time
where the time goes in v6:
time: 1240 us
  Pallas kernels  882 us (71%)
  waiting for transfers between devices  237 us (19%)
  local copies, waits for them, and re-layouts  29.8 us (2%)
  other arithmetic  24.2 us (2%)
  between operations  20.5 us (2%)
  starting transfers between devices  19.2 us (2%)
  blocking collectives  18.9 us (2%)
    pallas_call x12, Pallas kernels, call(): pl.pallas_call(kernel, grid_spec=pltpu.PrefetchScalarGridSpec(num_scalar_...  643 us
    pallas_call x2, Pallas kernels, weight_grad(): pl.pallas_call(functools.partial(weight_grad_kernel, at, layout['tiles_ma...  210 us
    reduce_scatter x6, waiting for transfers between devices, scatter(): return lax.psum_scatter(rows, rows_axes, scatter_dimension=0, tiled=True)  158 us
    psum x1, waiting for transfers between devices, body(): stats = lax.psum(stats, ('tp', 'ep'))  43 us
    all_gather x5, waiting for transfers between devices, gather(): return lax.all_gather(rows, rows_axes, axis=0, tiled=True)  33.5 us
  transfers between devices with their start and end apart: 19, of which 7 were waited for; matrix products, arithmetic and copies ran while one was open for 4% of the time, Pallas kernels for 55%

profile of v6, /device:TPU:0, one launch (start us, length us, event | category | flops | bytes accessed | tf_op | source)
XLA Modules:
  0.0 1235.6 jit_solution(1538474621738952221)
XLA Ops:
  8.5 3.7 normalize.2
  12.3 5.4 normalize.3
  17.8 3.3 fusion.66
  21.2 18.9 %all-gather = f32[128,1024]{1,0:T(8,128)S(1)} all-gather(f32[16,1024]{1,0:T(8,128)S(1)} %maximum_bitcast_fusion.1), channel_id=2, replica_groups=mesh['tp'=4,'ep'=2] {'ep','tp'}, dimensions={0}, use_global_device_ids=true | all-gather | bytes 589824 | tf_op jit(solution)/shard_map/all_gather | solution.py:890
  44.9 6.2 constant_dynamic-slice_fusion.2
  51.0 5.6 constant_dynamic-slice_fusion.1
  57.2 6.3 constant_dynamic-slice_fusion
  77.4 7.5 all-gather.7.cloned.1.call-done.tok_hbm
  85.5 108.5 %shard_map.160 = (bf16[7424,2048]{1,0:T(8,128)(2,1)}, f32[7424,128]{1,0:T(8,128)}, f32[7424,2816]{1,0:T(8,128)}, bf16[7424,1408]{1,0:T(8,128)(2,1)}, bf16[7424,2048]{1,0:T(8,128)(2,1)}) custom-call(s32[1300]{0:T(1024)} %concatenate.42.table_ref, s32[5,64,128]{2,1,0:T(8,128)} %fusion.6.pos_ref, f32[5,64,128]{2,1,0:T(8,128)} %get-tuple-element.182.prob_ref, ...), custom_call_target="tpu_custom_call" | custom-call | flops 74999996416 | bytes 150000000 | tf_op jit(solution)/shard_map/pallas_call | solution.py:28
  194.0 14.2 %shard_map.161 = bf16[3072,2048]{1,0:T(8,128)(2,1)} custom-call(s32[1300]{0:T(1024)} %concatenate.42.table_ref, s32[5,64,128]{2,1,0:T(8,128)} %fusion.6.pos_ref, bf16[7424,2048]{1,0:T(8,128)(2,1)} %get-tuple-element.79.rows_hbm), custom_call_target="tpu_custom_call" | custom-call | flops 8999999488 | bytes 35000000 | tf_op jit(solution)/shard_map/pallas_call | solution.py:28
  208.3 73.4 %shard_map.162 = (bf16[5376,2048]{1,0:T(8,128)(2,1)}, f32[5376,128]{1,0:T(8,128)}, f32[5376,2816]{1,0:T(8,128)}, bf16[5376,1408]{1,0:T(8,128)(2,1)}, bf16[5376,2048]{1,0:T(8,128)(2,1)}) custom-call(s32[1300]{0:T(1024)} %concatenate.42.table_ref, s32[5,64,128]{2,1,0:T(8,128)} %fusion.6.pos_ref, f32[5,64,128]{2,1,0:T(8,128)} %get-tuple-element.182.prob_ref, ...), custom_call_target="tpu_custom_call" | custom-call | flops 74999996416 | bytes 150000000 | tf_op jit(solution)/shard_map/pallas_call | solution.py:28
  281.7 19.8 %reduce-scatter.7.cloned.1.call-done.rest_3_ = bf16[384,2048]{1,0:T(8,128)(2,1)} async-done(((bf16[3072,2048]{1,0:T(8,128)(2,1)}), bf16[384,2048]{1,0:T(8,128)(2,1)}) %reduce-scatter.7.cloned.1.call-update) | async-done | bytes 1572880 | tf_op jit(solution)/shard_map/reduce_scatter | solution.py:872
  301.5 11.2 shard_map.163
  317.3 97.4 %shard_map.164 = (bf16[7424,2048]{1,0:T(8,128)(2,1)}, f32[7424,128]{1,0:T(8,128)}, f32[7424,2816]{1,0:T(8,128)}, bf16[7424,1408]{1,0:T(8,128)(2,1)}, bf16[7424,2048]{1,0:T(8,128)(2,1)}) custom-call(s32[1300]{0:T(1024)} %concatenate.42.table_ref, s32[5,64,128]{2,1,0:T(8,128)} %fusion.6.pos_ref, f32[5,64,128]{2,1,0:T(8,128)} %get-tuple-element.182.prob_ref, ...), custom_call_target="tpu_custom_call" | custom-call | flops 74999996416 | bytes 150000000 | tf_op jit(solution)/shard_map/pallas_call | solution.py:28
  414.8 14.2 %shard_map.165 = bf16[3072,2048]{1,0:T(8,128)(2,1)} custom-call(s32[1300]{0:T(1024)} %concatenate.42.table_ref, s32[5,64,128]{2,1,0:T(8,128)} %fusion.6.pos_ref, bf16[7424,2048]{1,0:T(8,128)(2,1)} %get-tuple-element.84.rows_hbm), custom_call_target="tpu_custom_call" | custom-call | flops 8999999488 | bytes 35000000 | tf_op jit(solution)/shard_map/pallas_call | solution.py:28
  432.9 12.5 %all-gather.11.cloned.1.call-done.tok_hbm = bf16[3072,2048]{1,0:T(8,128)(2,1)} async-done(((bf16[384,2048]{1,0:T(8,128)(2,1)}), bf16[3072,2048]{1,0:T(8,128)(2,1)}) %all-gather.11.cloned.1.call-update) | async-done | bytes 12582928 | tf_op jit(solution)/shard_map/all_gather | solution.py:869
  445.3 104.3 %shard_map.166 = (bf16[7424,2816]{1,0:T(8,128)(2,1)}, bf16[7424,2048]{1,0:T(8,128)(2,1)}, bf16[7424,2048]{1,0:T(8,128)(2,1)}, f32[7424,128]{1,0:T(8,128)}) custom-call(s32[1300]{0:T(1024)} %concatenate.42.table_ref, s32[5,64,128]{2,1,0:T(8,128)} %fusion.6.pos_ref, bf16[3072,2048]{1,0:T(8,128)(2,1)} %all-gather.11.cloned.1.call-done.tok_hbm, ...), custom_call_target="tpu_custom_call" | custom-call | flops 74999996416 | bytes 150000000 | tf_op jit(solution)/shard_map/pallas_call | solution.py:28
  549.6 3.7 add_convert_fusion
  553.4 16.8 %shard_map.167 = (bf16[3072,2048]{1,0:T(8,128)(2,1)}, f32[8,3072]{1,0:T(8,128)}) custom-call(s32[1300]{0:T(1024)} %concatenate.42.table_ref, s32[5,64,128]{2,1,0:T(8,128)} %fusion.6.pos_ref, bf16[7424,2048]{1,0:T(8,128)(2,1)} %get-tuple-element.92.rows_hbm, f32[7424,128]{1,0:T(8,128)} %get-tuple-element.93.rest_0_), custom_call_target="tpu_custom_call" | custom-call | flops 8999999488 | bytes 35000000 | tf_op jit(solution)/shard_map/pallas_call | solution.py:28
  570.2 13.5 %all-gather.13.cloned.1.call-done.tok_hbm = bf16[2048,2048]{1,0:T(8,128)(2,1)} async-done(((bf16[256,2048]{1,0:T(8,128)(2,1)}), bf16[2048,2048]{1,0:T(8,128)(2,1)}) %all-gather.13.cloned.1.call-update) | async-done | bytes 8388624 | tf_op jit(solution)/shard_map/all_gather | solution.py:869
  583.7 81.3 %shard_map.168 = (bf16[5376,2816]{1,0:T(8,128)(2,1)}, bf16[5376,2048]{1,0:T(8,128)(2,1)}, bf16[5376,2048]{1,0:T(8,128)(2,1)}, f32[5376,128]{1,0:T(8,128)}) custom-call(s32[1300]{0:T(1024)} %concatenate.42.table_ref, s32[5,64,128]{2,1,0:T(8,128)} %fusion.6.pos_ref, bf16[2048,2048]{1,0:T(8,128)(2,1)} %all-gather.13.cloned.1.call-done.tok_hbm, ...), custom_call_target="tpu_custom_call" | custom-call | flops 74999996416 | bytes 150000000 | tf_op jit(solution)/shard_map/pallas_call | solution.py:28
  665.1 11.9 shard_map.169
  677.0 94.5 %shard_map.170 = (bf16[7424,2816]{1,0:T(8,128)(2,1)}, bf16[7424,2048]{1,0:T(8,128)(2,1)}, bf16[7424,2048]{1,0:T(8,128)(2,1)}, f32[7424,128]{1,0:T(8,128)}) custom-call(s32[1300]{0:T(1024)} %concatenate.42.table_ref, s32[5,64,128]{2,1,0:T(8,128)} %fusion.6.pos_ref, bf16[3072,2048]{1,0:T(8,128)(2,1)} %all-gather.15.cloned.1.call-done.tok_hbm, ...), custom_call_target="tpu_custom_call" | custom-call | flops 74999996416 | bytes 150000000 | tf_op jit(solution)/shard_map/pallas_call | solution.py:28
  771.6 15.3 %shard_map.171 = (bf16[3072,2048]{1,0:T(8,128)(2,1)}, f32[8,3072]{1,0:T(8,128)}) custom-call(s32[1300]{0:T(1024)} %concatenate.42.table_ref, s32[5,64,128]{2,1,0:T(8,128)} %fusion.6.pos_ref, bf16[7424,2048]{1,0:T(8,128)(2,1)} %get-tuple-element.107.rows_hbm, f32[7424,128]{1,0:T(8,128)} %get-tuple-element.108.rest_0_), custom_call_target="tpu_custom_call" | custom-call | flops 8999999488 | bytes 35000000 | tf_op jit(solution)/shard_map/pallas_call | solution.py:28
  790.5 137.6 %weight_grad.2 = (bf16[4,2048,1408]{2,1,0:T(8,128)(2,1)}, bf16[4,2048,1408]{2,1,0:T(8,128)(2,1)}, bf16[1,2048,1408]{2,1,0:T(8,128)(2,1)}, bf16[1,2048,1408]{2,1,0:T(8,128)(2,1)}) custom-call(s32[1300]{0:T(1024)} %concatenate.42.table_ref, bf16[7424,2048]{1,0:T(8,128)(2,1)} %get-tuple-element.110.rest_0_, bf16[5376,2048]{1,0:T(8,128)(2,1)} %get-tuple-element.111.rest_1_, ...), custom_call_target="tpu_custom_call" | custom-call | flops 103809024000 | bytes 100000000 | tf_op jit(solution)/shard_map/weight_grad/pallas_call | solution.py:579
  928.1 17.0 %collective-permute-start.3 = (bf16[1,2048,1408]{2,1,0:T(8,128)(2,1)}, bf16[1,2048,1408]{2,1,0:T(8,128)(2,1)}, u32[]{:S(2)}, u32[]{:S(2)}) collective-permute-start(bf16[1,2048,1408]{2,1,0:T(8,128)(2,1)} %get-tuple-element.136), channel_id=1, source_target_pairs={{0,1},{1,0},{2,3},{3,2},{4,5},{5,4},{6,7},{7,6}} | collective-permute-start | bytes 17301512 | tf_op jit(solution)/shard_map/ppermute | solution.py:958
  947.7 51.3 %reduce-scatter.13.cloned.1.call-done.rest_0_ = bf16[384,2048]{1,0:T(8,128)(2,1)} async-done(((bf16[3072,2048]{1,0:T(8,128)(2,1)}), bf16[384,2048]{1,0:T(8,128)(2,1)}) %reduce-scatter.13.cloned.1.call-update) | async-done | bytes 1572880 | tf_op jit(solution)/shard_map/reduce_scatter | solution.py:872
  999.0 87.3 %reduce-scatter.17.cloned.1.call-done.rest_2_ = bf16[384,2048]{1,0:T(8,128)(2,1)} async-done(((bf16[3072,2048]{1,0:T(8,128)(2,1)}), bf16[384,2048]{1,0:T(8,128)(2,1)}) %reduce-scatter.17.cloned.1.call-update) | async-done | bytes 1572880 | tf_op jit(solution)/shard_map/reduce_scatter | solution.py:872
  1086.3 13.9 %finish.1 = (bf16[1024,2048]{1,0:T(8,128)(2,1)}, bf16[1024,2048]{1,0:T(8,128)(2,1)}, f32[32,2048]{1,0:T(8,128)}) custom-call(bf16[1024,2048]{1,0:T(8,128)(2,1)} %x_ref.5, bf16[1024,2048]{1,0:T(8,128)(2,1)} %y_grad_ref.1, f32[8,1024]{1,0:T(8,128)} %fusion.69.prob_ref, f32[8,1024]{1,0:T(8,128)} %pad_maximum_fusion.1.gate_grad_ref, ...), custom_call_target="tpu_custom_call" | custom-call | flops 1000000000 | bytes 25000000 | tf_op jit(solution)/shard_map/finish/pallas_call | solution.py:700
  1100.2 72.5 %weight_grad.3 = (bf16[4,1408,2048]{2,1,0:T(8,128)(2,1)}, bf16[1,1408,2048]{2,1,0:T(8,128)(2,1)}, bf16[4,2048,1408]{2,1,0:T(8,128)(2,1)}, bf16[4,2048,1408]{2,1,0:T(8,128)(2,1)}) custom-call(s32[1300]{0:T(1024)} %concatenate.42.table_ref, bf16[7424,1408]{1,0:T(8,128)(2,1)} %get-tuple-element.88.h_hbm.rest_0_, ...), custom_call_target="tpu_custom_call", output_to_operand_aliasing={{2}: (9, {}), {3}: (10, {})} | custom-call | flops 51904512000 | bytes 100000000 | tf_op jit(solution)/shard_map/weight_grad/pallas_call | solution.py:579
  1173.7 43.0 %all-reduce.8.cloned.1.call-done = f32[32,2048]{1,0:T(8,128)} async-done(((f32[32,2048]{1,0:T(8,128)}), f32[32,2048]{1,0:T(8,128)}) %all-reduce.8.cloned.1.call-update) | async-done | bytes 262160 | tf_op jit(solution)/shard_map/psum | solution.py:971
  1220.4 5.9 insert.1
  (183 shorter events, 37.3 us)
Async XLA Ops:
  7.2 77.7 %all-gather.7.cloned.1.call-start = ((), (), s32[]{:S(2)}) async-start(), calls=%async_computation.6 | async-start | bytes 14155776 | tf_op jit(solution)/shard_map/all_gather | solution.py:869
  12.2 5.5 copy-start.4
  12.2 5.5 copy-start.1
  12.2 5.5 copy-start.3
  12.3 196.0 %all-gather.9.cloned.1.call-start = ((), (), s32[]{:S(2)}) async-start(), calls=%async_computation.7 | async-start | bytes 23592960 | tf_op jit(solution)/shard_map/all_gather | solution.py:869
  17.7 283.8 %reduce-scatter.7.cloned.1.call-start = ((), (), s32[]{:S(2)}) async-start(), calls=%async_computation.8 | async-start | bytes 14155776 | tf_op jit(solution)/shard_map/reduce_scatter | solution.py:872
  51.0 34.5 %collective-permute-start = (bf16[1,2048,1408]{2,1,0:T(8,128)(2,1)}, bf16[1,2048,1408]{2,1,0:T(8,128)(2,1)}, u32[]{:S(2)}, u32[]{:S(2)}) collective-permute-start(bf16[1,2048,1408]{2,1,0:T(8,128)(2,1)} %constant_dynamic-slice_fusion.2), channel_id=1, source_target_pairs={{0,1},{1,0},{2,3},{3,2},{4,5},{5,4},{6,7},{7,6}} | collective-permute-start | bytes 17301512 | tf_op jit(solution)/shard_map/ppermute | solution.py:909
  56.6 7.7 copy-start.6
  56.6 28.9 %collective-permute-start.1 = (bf16[1,2048,1408]{2,1,0:T(8,128)(2,1)}, bf16[1,2048,1408]{2,1,0:T(8,128)(2,1)}, u32[]{:S(2)}, u32[]{:S(2)}) collective-permute-start(bf16[1,2048,1408]{2,1,0:T(8,128)(2,1)} %constant_dynamic-slice_fusion.1), channel_id=1, source_target_pairs={{0,1},{1,0},{2,3},{3,2},{4,5},{5,4},{6,7},{7,6}} | collective-permute-start | bytes 17301512 | tf_op jit(solution)/shard_map/ppermute | solution.py:909
  63.5 9.0 copy-start.5
  63.5 22.0 %collective-permute-start.2 = (bf16[1,1408,2048]{2,1,0:T(8,128)(2,1)}, bf16[1,1408,2048]{2,1,0:T(8,128)(2,1)}, u32[]{:S(2)}, u32[]{:S(2)}) collective-permute-start(bf16[1,1408,2048]{2,1,0:T(8,128)(2,1)} %constant_dynamic-slice_fusion), channel_id=1, source_target_pairs={{0,1},{1,0},{2,3},{3,2},{4,5},{5,4},{6,7},{7,6}} | collective-permute-start | bytes 17301512 | tf_op jit(solution)/shard_map/ppermute | solution.py:909
  208.3 220.7 %reduce-scatter.9.cloned.1.call-start = ((), (), s32[]{:S(2)}) async-start(), calls=%async_computation.9 | async-start | bytes 9437184 | tf_op jit(solution)/shard_map/reduce_scatter | solution.py:872
  312.7 1.4 copy-start
  312.7 132.6 %all-gather.11.cloned.1.call-start = ((), (), s32[]{:S(2)}) async-start(), calls=%async_computation.11 | async-start | bytes 14155776 | tf_op jit(solution)/shard_map/all_gather | solution.py:869
  317.3 232.3 %reduce-scatter.11.cloned.1.call-start = ((), (), s32[]{:S(2)}) async-start(), calls=%async_computation.10 | async-start | bytes 14155776 | tf_op jit(solution)/shard_map/reduce_scatter | solution.py:872
  429.0 1.2 copy-start.2
  429.0 154.7 %all-gather.13.cloned.1.call-start = ((), (), s32[]{:S(2)}) async-start(), calls=%async_computation.12 | async-start | bytes 9437184 | tf_op jit(solution)/shard_map/all_gather | solution.py:869
  432.8 244.2 %all-gather.15.cloned.1.call-start = ((), (), s32[]{:S(2)}) async-start(), calls=%async_computation.13 | async-start | bytes 14155776 | tf_op jit(solution)/shard_map/all_gather | solution.py:869
  553.4 391.8 %all-reduce.6.cloned.1.call-start = ((), (), s32[]{:S(2)}) async-start(), calls=%async_computation.14 | async-start | bytes 524288 | tf_op jit(solution)/shard_map/psum | solution.py:960
  788.6 159.1 %reduce-scatter.15.cloned.1.call-start = ((), (), s32[]{:S(2)}) async-start(), calls=%async_computation.16 | async-start | bytes 9437184 | tf_op jit(solution)/shard_map/reduce_scatter | solution.py:872
  789.2 209.8 %reduce-scatter.13.cloned.1.call-start = ((), (), s32[]{:S(2)}) async-start(), calls=%async_computation.15 | async-start | bytes 14155776 | tf_op jit(solution)/shard_map/reduce_scatter | solution.py:872
  789.9 296.4 %reduce-scatter.17.cloned.1.call-start = ((), (), s32[]{:S(2)}) async-start(), calls=%async_computation.17 | async-start | bytes 14155776 | tf_op jit(solution)/shard_map/reduce_scatter | solution.py:872
  790.5 426.2 %all-reduce.8.cloned.1.call-start = ((), (), s32[]{:S(2)}) async-start(), calls=%async_computation.18 | async-start | bytes 524288 | tf_op jit(solution)/shard_map/psum | solution.py:971
  928.1 172.1 %collective-permute-start.3 = (bf16[1,2048,1408]{2,1,0:T(8,128)(2,1)}, bf16[1,2048,1408]{2,1,0:T(8,128)(2,1)}, u32[]{:S(2)}, u32[]{:S(2)}) collective-permute-start(bf16[1,2048,1408]{2,1,0:T(8,128)(2,1)} %get-tuple-element.136), channel_id=1, source_target_pairs={{0,1},{1,0},{2,3},{3,2},{4,5},{5,4},{6,7},{7,6}} | collective-permute-start | bytes 17301512 | tf_op jit(solution)/shard_map/ppermute | solution.py:958
  945.1 155.1 %collective-permute-start.4 = (bf16[1,2048,1408]{2,1,0:T(8,128)(2,1)}, bf16[1,2048,1408]{2,1,0:T(8,128)(2,1)}, u32[]{:S(2)}, u32[]{:S(2)}) collective-permute-start(bf16[1,2048,1408]{2,1,0:T(8,128)(2,1)} %get-tuple-element.137), channel_id=1, source_target_pairs={{0,1},{1,0},{2,3},{3,2},{4,5},{5,4},{6,7},{7,6}} | collective-permute-start | bytes 17301512 | tf_op jit(solution)/shard_map/ppermute | solution.py:958
  1172.6 47.8 %collective-permute-start.5 = (bf16[1,1408,2048]{2,1,0:T(8,128)(2,1)}, bf16[1,1408,2048]{2,1,0:T(8,128)(2,1)}, u32[]{:S(2)}, u32[]{:S(2)}) collective-permute-start(bf16[1,1408,2048]{2,1,0:T(8,128)(2,1)} %get-tuple-element.142), channel_id=1, source_target_pairs={{0,1},{1,0},{2,3},{3,2},{4,5},{5,4},{6,7},{7,6}} | collective-permute-start | bytes 17301512 | tf_op jit(solution)/shard_map/ppermute | solution.py:970
Sparse Core Ops, SparseCore 0:
  12.4 72.4 all-gather.6
  87.2 101.8 all-gather.8
  208.4 93.0 reduce-scatter.6
  312.8 64.3 reduce-scatter.8
  378.9 66.4 all-gather.10
  449.2 83.9 reduce-scatter.10
  535.0 48.6 all-gather.12
  585.5 66.5 all-gather.14
  788.7 57.0 all-reduce.5
  849.0 62.4 reduce-scatter.14
  915.0 83.9 reduce-scatter.12
  1002.3 83.9 reduce-scatter.16
  1173.8 42.8 all-reduce.7
